TPU v7x, 256 devices: a whole 4x4x8 slice. The times are simulated.
256 devices in a mesh: dp: 8 (over y_hi, x), ctx: 32 (over z, y_lo, core).
Axes of the slice: x: 4, y: 4 (y_hi: 2, y_lo: 2; y = y_hi * 2 + y_lo), z: 8, core: 2. Of those that a mesh axis runs over, the one named last changes fastest.
Arguments:
- layer_input: bfloat16 [8, 4096, 7168], P(None, 'ctx', 'dp'), may hold values from -6 to 6
- kv_latent: bfloat16 [8, 4096, 512], P('dp', 'ctx'), may hold values from -8 to 8
- key_rope: bfloat16 [8, 4096, 64], P('dp', 'ctx'), may hold values from -6 to 6
- q_latent: bfloat16 [8, 4096, 8, 512], P('dp', 'ctx'), may hold values from -60 to 60
- q_rope: bfloat16 [8, 4096, 8, 64], P('dp', 'ctx'), may hold values from -3 to 3
- saved_output: bfloat16 [8, 4096, 8, 512], P('dp', 'ctx'), may hold values from -4 to 4
- w_uv: bfloat16 [512, 1024], replicated, may hold values from -0.25 to 0.25
- d_out: bfloat16 [8, 4096, 1024], P('dp', 'ctx'), may hold values from -6 to 6
- blocks: int32 [64], replicated, may hold values from 0 to 63, each once
Outputs:
- d_q_latent: bfloat16 [8, 4096, 8, 512], P('dp', 'ctx')
- d_q_rope: bfloat16 [8, 4096, 8, 64], P('dp', 'ctx')
- d_kv_latent: bfloat16 [8, 4096, 512], P('dp', 'ctx')
- d_key_rope: bfloat16 [8, 4096, 64], P('dp', 'ctx')
- grad_w_down: float32 [7168, 576], P(('dp', 'ctx'))
- grad_w_uv: float32 [512, 1024], P(('dp', 'ctx'))
Inputs may be any that keep to these rules, and one draw needn't show every extreme that they name: A permutation: blocks[k] is the position block of rows k * 64 to (k + 1) * 64 - 1 of every sequence.
All inputs are finite; a program needn't handle non-finite values.
Results may differ from a plain program's by a relative error of at most 0.028.
Values may be sent and summed in bfloat16 or wider, within the bound.
No kernel may reach another device: no remote copies, remote signals or barrier semaphores. Data moves between devices by JAX's collectives and lax.ppermute only.
A program may use at most 128 MiB of HBM per device.

v0:
```python
import math

import jax
import jax.numpy as jnp
from jax import lax
from jax.experimental import pallas as pl
from jax.experimental.pallas import tpu as pltpu
from jax.sharding import Mesh, PartitionSpec as P


softmax_scale = 1.0 / math.sqrt(192.0)
log2e = 1.0 / math.log(2.0)
TILE = 256
N_DP = 8
N_CTX = 32


def nt(a, b):
    return lax.dot_general(a, b, (((1,), (1,)), ((), ())), preferred_element_type=jnp.float32)


def nn(a, b):
    return lax.dot_general(a, b, (((1,), (0,)), ((), ())), preferred_element_type=jnp.float32)


def tn(a, b):
    return lax.dot_general(a, b, (((0,), (0,)), ((), ())), preferred_element_type=jnp.float32)


def swapped(x, axis):
    return lax.ppermute(x, axis, [(0, 1), (1, 0)])


def shifted(x, axis, by):
    n = lax.axis_size(axis)
    return lax.ppermute(x, axis, [(i, (i + by) % n) for i in range(n)])


def around(x, axis):
    n = lax.axis_size(axis)
    got = [x] * n
    ahead = behind = x
    for k in range(1, n // 2 + 1):
        behind = shifted(behind, axis, 1)
        got[n - k] = behind
        if k < n - n // 2:
            ahead = shifted(ahead, axis, -1)
            got[k] = ahead
    return got


def added(a, b):
    return (a.astype(jnp.float32) + b.astype(jnp.float32)).astype(a.dtype)


def ring_sum(parts, axis):
    n = lax.axis_size(axis)
    up = parts[n // 2]
    for k in range(n // 2 - 1, 0, -1):
        up = added(parts[k], shifted(up, axis, 1))
    up = shifted(up, axis, 1)
    down = parts[n // 2 + 1]
    for k in range(n // 2 + 2, n):
        down = added(parts[k], shifted(down, axis, -1))
    down = shifted(down, axis, -1)
    f32 = jnp.float32
    return parts[0].astype(f32) + up.astype(f32) + down.astype(f32)


def owner_at(me, core, ahead, y):
    n_z, my_z, my_y, my_core = me[0], me[1], me[2], me[3]
    return (lax.rem(my_z + ahead, n_z) * 2 + (my_y ^ y)) * 2 + (my_core ^ core)


def place_keys(me, blocks_ref, aheads, table, order):
    places = []
    for core in range(2):
        for ahead in aheads:
            for y in range(2):
                owner = owner_at(me, core, ahead, y)
                places += [blocks_ref[2 * owner + side] for side in range(2)]
    for i, q in enumerate(places):
        table[i] = q

    def rank_step(i, carry):
        q = table[i]
        rank = sum((p < q).astype(jnp.int32) for p in places)
        table[i] = rank
        order[rank] = q
        return carry

    lax.fori_loop(0, len(places), rank_step, 0)
    return places


def seen_blocks(places, block):
    return sum((p <= block).astype(jnp.int32) for p in places)


def each_block(piece_refs, items, table, half, do):
    n = len(piece_refs) // 2

    def item_step(j, carry):
        for i, ref in enumerate(piece_refs):
            for side in range(2):
                rank = table[(i * items + j) * 2 + side]
                do(i // n, i % n, j, side, pl.ds(pl.multiple_of(rank * half, half), half))
        return carry

    lax.fori_loop(0, items, item_step, 0)


def sort_keys(piece_refs, first, items, table, keys_ref, latent, rope):
    n = len(piece_refs) // 2
    half, wide = piece_refs[0].shape[1], keys_ref.shape[1]
    zero_pad = jnp.zeros((half, wide - latent - rope), keys_ref.dtype)

    def copy(core, i, j, side, at):
        ref = piece_refs[core * n + i]
        j = first + j
        keys_ref[at, :latent] = ref[j, :, side * latent : (side + 1) * latent]
        start = 2 * latent + side * rope
        keys_ref[at, latent:] = jnp.concatenate([ref[j, :, start : start + rope], zero_pad], axis=1)

    each_block(piece_refs, items, table, half, copy)


def tile_scores(t, keys, queries, order, block, heads, half):
    per = keys.shape[0] // half
    group = queries.shape[0]
    ahead = block * half + lax.broadcasted_iota(jnp.int32, (1, group), 1) // heads
    row = lax.broadcasted_iota(jnp.int32, (half, group), 0)
    s = nt(keys, queries) * (softmax_scale * log2e)
    return jnp.concatenate(
        [
            jnp.where(
                row <= ahead - order[t * per + k] * half, s[k * half : (k + 1) * half], -jnp.inf
            )
            for k in range(per)
        ],
        axis=0,
    )


vmem = pl.BlockSpec(memory_space=pltpu.VMEM)
smem = pl.BlockSpec(memory_space=pltpu.SMEM)


def call(kernel, out_shape, n_smem, operands, scratch, flops, limit=60):
    return pl.pallas_call(
        kernel,
        out_shape=tuple(jax.ShapeDtypeStruct(*o) for o in out_shape),
        in_specs=[smem] * n_smem + [vmem] * (len(operands) - n_smem),
        out_specs=(vmem,) * len(out_shape),
        scratch_shapes=scratch,
        compiler_params=pltpu.CompilerParams(vmem_limit_bytes=limit * 1024 * 1024),
        cost_estimate=pl.CostEstimate(flops=flops, bytes_accessed=4 << 20, transcendentals=0),
    )(*operands)


def pack_keys(lat, rope):
    tokens, latent = lat.shape
    half, width = tokens // 2, rope.shape[1]

    def kernel(lat_ref, rope_ref, out_ref):
        out_ref[:, :latent] = lat_ref[:half]
        out_ref[:, latent : 2 * latent] = lat_ref[half:]
        out_ref[:, 2 * latent :] = jnp.concatenate([rope_ref[:half], rope_ref[half:]], axis=1)

    shape = ((half, 2 * (latent + width)), lat.dtype)
    return call(kernel, [shape], 0, (lat, rope), [], 1000, 8)[0]


def prepare(me, queries, query_rope, outputs, grad_out, weight):
    rows, latent = queries.shape
    rope = query_rope.shape[1]
    tokens = grad_out.shape[0]
    heads = rows // tokens
    value = grad_out.shape[1] // heads
    wide = latent + 128
    f32, bf16 = jnp.float32, jnp.bfloat16
    n_dp, n_z = N_DP, N_CTX // 4
    each = latent // (n_dp * N_CTX)

    def kernel(me_ref, q_ref, qr_ref, out_ref, d_ref, w_ref, wide_ref, g_ref, delta_ref, v_ref,
               out_wide, g_wide, v_wide):
        wide_ref[:, :latent] = q_ref[...]
        wide_ref[:, latent:] = jnp.concatenate(
            [qr_ref[...], jnp.zeros((rows, wide - latent - rope), bf16)], axis=1
        )
        lanes = [slice(k, k + 128) for k in range(0, latent, 128)]
        for k, lane in enumerate(lanes):
            out_wide[k] = out_ref[:, lane].astype(f32)

        def head_step(h, carry):
            at = pl.ds(h, tokens, stride=heads)
            column = pl.ds(pl.multiple_of(h * value, value), value)
            d = d_ref[:, column]
            g = nt(d, w_ref[:, column])
            for k, lane in enumerate(lanes):
                g_wide[k, at, :] = g[:, lane]
                v_wide[pl.ds(h + k * 128 * heads, 128, stride=heads), :] = tn(
                    out_wide[k, at, :].astype(bf16), d
                )
            return carry

        lax.fori_loop(0, heads, head_step, 0)
        delta = jnp.zeros((rows, 128), f32)
        for k, lane in enumerate(lanes):
            g = g_wide[k].astype(bf16)
            g_ref[:, lane] = g
            delta += g.astype(f32) * out_wide[k]
        delta = jnp.sum(delta, axis=1, keepdims=True)
        delta = jnp.broadcast_to(delta, (rows, 128)).T[:1]
        delta_ref[0] = delta[:, : rows // 2]
        delta_ref[1] = delta[:, rows // 2 :]
        me = [me_ref[i] for i in range(4)]

        def slot_step(slot, carry):
            owner = owner_at(me, slot // (2 * n_z), slot // 2 % n_z, slot % 2)
            for r in range(each):
                parts = []
                for dp in range(n_dp):
                    row = ((dp * N_CTX + owner) * each + r) * heads
                    parts.append(v_wide[pl.ds(pl.multiple_of(row, heads), heads), :])
                v_ref[slot, :, r * value : (r + 1) * value] = jnp.concatenate(
                    parts, axis=0
                ).astype(bf16)
            return carry

        lax.fori_loop(0, N_CTX, slot_step, 0)

    return call(
        kernel,
        [
            ((rows, wide), bf16),
            ((rows, latent), bf16),
            ((2, 1, rows // 2), f32),
            ((N_CTX, n_dp * heads, each * value), bf16),
        ],
        1,
        (me, queries, query_rope, outputs, grad_out, weight),
        [
            pltpu.VMEM((latent // 128, rows, 128), f32),
            pltpu.VMEM((latent // 128, rows, 128), f32),
            pltpu.VMEM((latent * heads, value), f32),
        ],
        1000,
    )


def score_step(me, blocks, aheads, pieces, queries, latent, rope, before):
    half = pieces[0].shape[1]
    rows, wide = queries.shape
    keys = 8 * len(aheads) * half
    per, group = TILE // half, rows // 2
    heads = group // half
    f32, bf16 = jnp.float32, jnp.bfloat16
    n = len(pieces)

    def kernel(me_ref, blocks_ref, *refs):
        piece_refs, q_ref, refs = refs[:n], refs[n], refs[n + 1 :]
        if before:
            peak_in, total_in, *refs = refs
        peak_ref, total_ref, keys_ref, table, order = refs
        me = [me_ref[i] for i in range(4)]
        places = place_keys(me, blocks_ref, aheads, table, order)
        sort_keys(piece_refs, 0, pieces[0].shape[0], table, keys_ref, latent, rope)

        def block_step(which, carry):
            block = blocks_ref[2 * owner_at(me, 0, 0, 0) + which]
            base = pl.multiple_of(which * group, group)

            def tile_step(t, carry):
                m, l = carry
                at = pl.ds(pl.multiple_of(t * TILE, TILE), TILE)
                s = tile_scores(
                    t, keys_ref[at, :], q_ref[pl.ds(base, group), :], order, block, heads, half
                )
                new = jnp.maximum(m, jnp.max(s, axis=0, keepdims=True))
                l = l * jnp.exp2(m - new) + jnp.sum(jnp.exp2(s - new), axis=0, keepdims=True)
                return new, l

            if before:
                begin = (peak_in[which], total_in[which])
            else:
                begin = (jnp.full((1, group), -jnp.inf, f32), jnp.zeros((1, group), f32))
            tiles = (seen_blocks(places, block) + per - 1) // per
            peak_ref[which], total_ref[which] = lax.fori_loop(0, tiles, tile_step, begin)
            return carry

        lax.fori_loop(0, 2, block_step, 0)

    stat = ((2, 1, group), f32)
    return call(
        kernel,
        [stat, stat],
        2,
        (me, blocks, *pieces, queries, *before),
        [pltpu.VMEM((keys, wide), bf16)] + [pltpu.SMEM((keys // half,), jnp.int32)] * 2,
        rows * keys * wide,
    )


def grad_step(me, blocks, aheads, pieces, queries, grads, delta, stats, values, dq, start, last):
    half, packed = pieces[0].shape[1:]
    rows, latent = grads.shape
    wide = queries.shape[1]
    cols = packed // 2
    rope = cols - latent
    keys = 8 * len(aheads) * half
    per, group = TILE // half, rows // 2
    heads = group // half
    f32, bf16 = jnp.float32, jnp.bfloat16
    n = len(pieces)
    first = dq is None
    extra = values.shape[2]
    n_z = values.shape[0] // 4

    def kernel(me_ref, blocks_ref, *refs):
        piece_refs, refs = refs[:n], refs[n:]
        q_ref, g_ref, delta_ref, peak_ref, total_ref, v_ref, *refs = refs
        if not first:
            dq_in, *refs = refs
        near_ref, far_ref, *refs = refs
        if last:
            dq_ref, dqr_ref, keys_ref, table, order, dk_acc, dq_acc = refs
        else:
            dq_acc, keys_ref, table, order, dk_acc = refs
        me = [me_ref[i] for i in range(4)]
        places = place_keys(me, blocks_ref, aheads, table, order)
        items = 2 * len(aheads)
        sort_keys(piece_refs, start, items, table, keys_ref, latent, rope)

        def clear_step(k, carry):
            at = pl.ds(pl.multiple_of(k * half, half), half)
            dk_acc[at, :] = jnp.zeros((half, wide), f32)
            return carry

        lax.fori_loop(0, keys // half, clear_step, 0)

        def block_step(which, carry):
            block = blocks_ref[2 * owner_at(me, 0, 0, 0) + which]
            base = pl.multiple_of(which * group, group)
            log_total = peak_ref[which] + jnp.log2(total_ref[which])
            row_delta = delta_ref[which]

            def start_step(k, carry):
                at = pl.ds(pl.multiple_of(k * 64, 64), 64)
                dq_acc[which, at] = jnp.zeros((64, group), f32) if first else dq_in[which, at]
                return carry

            lax.fori_loop(0, wide // 64, start_step, 0)

            def tile_step(t, carry):
                at = pl.ds(pl.multiple_of(t * TILE, TILE), TILE)
                q = q_ref[pl.ds(base, group), :]
                g = g_ref[pl.ds(base, group), :]
                s = tile_scores(t, keys_ref[at, :], q, order, block, heads, half)
                p = jnp.exp2(s - log_total)
                dp = nt(keys_ref[at, :latent], g)
                ds = (p * (softmax_scale * (dp - row_delta))).astype(bf16)
                dk = nn(ds, q)
                dk_acc[at, :latent] += dk[:, :latent] + nn(p.astype(bf16), g)
                dk_acc[at, latent:] += dk[:, latent:]
                dq_acc[which] += tn(keys_ref[at, :], ds)
                return carry

            tiles = (seen_blocks(places, block) + per - 1) // per
            lax.fori_loop(0, tiles, tile_step, 0)
            if last:
                done = dq_acc[which].T.astype(bf16)
                dq_ref[pl.ds(base, group), :] = done[:, :latent]
                dqr_ref[pl.ds(base, group), :] = done[:, latent:cols]
            return carry

        lax.fori_loop(0, 2, block_step, 0)

        def unsort(core, i, j, side, at):
            part = dk_acc[at, :].astype(bf16)
            out = far_ref if core else near_ref
            out[j, :, side * latent : (side + 1) * latent] = part[:, :latent]
            at_rope = 2 * latent + side * rope
            out[j, :, at_rope : at_rope + rope] = part[:, latent:cols]

        each_block(piece_refs, items, table, half, unsort)
        for core, out in enumerate((near_ref, far_ref)):
            for k, ahead in enumerate(aheads):
                slot = (core * n_z + ahead) * 2
                out[2 * k : 2 * k + 2, :, packed:] = v_ref[slot : slot + 2]

    dk_shape = ((2 * len(aheads), half, packed + extra), bf16)
    dq_shape = (2, wide, group)
    scratch = [
        pltpu.VMEM((keys, wide), bf16),
        pltpu.SMEM((keys // half,), jnp.int32),
        pltpu.SMEM((keys // half,), jnp.int32),
        pltpu.VMEM((keys, wide), f32),
    ]
    if last:
        outs = [((rows, latent), bf16), ((rows, rope), bf16)]
        scratch += [pltpu.VMEM(dq_shape, f32)]
    else:
        outs = [(dq_shape, f32)]
    before = () if first else (dq,)
    return call(
        kernel,
        [dk_shape, dk_shape] + outs,
        2,
        (me, blocks, *pieces, queries, grads, delta, *stats, values, *before),
        scratch,
        4 * rows * keys * wide,
    )


def down_part(me, pieces, layer_input, latent, rope, heads):
    count, tokens, width = layer_input.shape
    half, packed = pieces[0].shape[1:]
    cols = latent + rope
    wide = latent + 128
    n = len(pieces)
    each = width // N_CTX
    room = -(-each // 16) * 16
    f32, bf16 = jnp.float32, jnp.bfloat16
    lanes = packed - 2 * cols

    def kernel(me_ref, *refs):
        piece_refs, refs = refs[:n], refs[n:]
        x_ref, near_ref, far_ref, lat_ref, rope_ref, v_ref, joined, total, placed, v_total = refs
        me = [me_ref[i] for i in range(4)]
        my_x, my_hi = me_ref[4], me_ref[5]
        zero_pad = jnp.zeros((half, wide - cols), bf16)
        values = jnp.zeros((half, lanes), f32)
        for i in range(n):
            for j in range(2):
                dp = (my_hi ^ j) * n + lax.rem(my_x + i, n)
                values += piece_refs[i][j, :, 2 * cols :].astype(f32)
                for side in range(2):
                    at = pl.ds(pl.multiple_of(dp * tokens + side * half, half), half)
                    lat = piece_refs[i][j, :, side * latent : (side + 1) * latent]
                    start = 2 * latent + side * rope
                    rot = piece_refs[i][j, :, start : start + rope]
                    joined[at, :latent] = lat
                    joined[at, latent:] = jnp.concatenate([rot, zero_pad], axis=1)
                    if i == 0 and j == 0:
                        lat_ref[side * half : (side + 1) * half] = lat
                        rope_ref[side * half : (side + 1) * half] = rot
        v_total[...] = values
        mine = v_total[pl.ds(pl.multiple_of((my_hi * n + my_x) * heads, heads), heads), :]
        value = lanes // v_ref.shape[0]
        for r in range(v_ref.shape[0]):
            v_ref[r] = mine[:, r * value : (r + 1) * value]
        total[...] = tn(x_ref[...].reshape(count * tokens, width), joined[...])
        for c in range(N_CTX):
            placed[c, :each] = total[c * each : (c + 1) * each]
            if room > each:
                placed[c, each:] = jnp.zeros((room - each, wide), f32)

        def slot_step(slot, carry):
            for core, ref in enumerate((near_ref, far_ref)):
                owner = owner_at(me, core, slot // 2, slot % 2)
                ref[slot] = placed[owner, :, :cols].astype(bf16)
            return carry

        lax.fori_loop(0, N_CTX // 2, slot_step, 0)

    shape = ((N_CTX // 2, room, cols), bf16)
    return call(
        kernel,
        [
            shape,
            shape,
            ((tokens, latent), bf16),
            ((tokens, rope), bf16),
            ((lanes * half // (N_DP * heads * 128), heads, 128), f32),
        ],
        1,
        (me, *pieces, layer_input),
        [
            pltpu.VMEM((count * tokens, wide), bf16),
            pltpu.VMEM((width, wide), f32),
            pltpu.VMEM((N_CTX, room, wide), f32),
            pltpu.VMEM((half, lanes), f32),
        ],
        1000,
    )


def body(layer_input, kv_latent, key_rope, q_latent, q_rope, saved_output, w_uv, d_out, blocks):
    wide, bf16 = jnp.float32, jnp.bfloat16
    latent, rope = kv_latent.shape[2], key_rope.shape[2]
    heads = q_latent.shape[2]
    n_z = lax.axis_size("z")
    me = jnp.stack(
        [jnp.int32(n_z)] + [lax.axis_index(a) for a in ("z", "ylo", "core", "x", "yhi")]
    )

    mine = pack_keys(kv_latent[0], key_rope[0])
    near = around(jnp.stack([mine, swapped(mine, "ylo")]), "z")
    pairs = [(n_z // 2 - c, (n_z // 2 + 1 + c) % n_z) for c in range(n_z // 2)]
    last = len(pairs) // 2
    spans = [[k] for k in range(last)] + [range(last, len(pairs))]
    near = [jnp.concatenate([near[a] for k in span for a in pairs[k]], axis=0) for span in spans]
    far = [swapped(x, "core") for x in near]

    queries, grads, delta, values = prepare(
        me,
        q_latent.reshape(-1, latent),
        q_rope.reshape(-1, rope),
        saved_output.reshape(-1, latent),
        d_out[0],
        w_uv,
    )
    stats = ()
    for k in (slice(last, None), slice(0, last)):
        aheads = [a for pair in pairs[k] for a in pair]
        stats = score_step(me, blocks, aheads, near[k] + far[k], queries, latent, rope, stats)
    d_q = up = down = None
    for c, pair in enumerate(pairs):
        k, start = min(c, last), 4 * max(c - last, 0)
        piece = [x[k] for x in (near, far)]
        near_dk, far_dk, *d_q = grad_step(
            me, blocks, pair, piece, queries, grads, delta, stats, values,
            d_q[0] if d_q else None, start, c == len(pairs) - 1,
        )
        there = swapped(far_dk, "core")
        both = near_dk.astype(wide) + there.astype(wide)
        at_a, at_b = both[:2], both[2:]
        if c:
            up = shifted(up, "z", 1)
            at_a = at_a + up.astype(wide)
            at_b = at_b + shifted(down, "z", -1).astype(wide)
        up = at_a.astype(bf16)
        down = at_b if pair[1] == 0 else at_b.astype(bf16)
    d_q, d_qr = d_q
    summed = down + shifted(up, "z", 1).astype(wide)
    summed = (summed[0] + swapped(summed[1].astype(bf16), "ylo").astype(wide)).astype(bf16)

    dp_pieces = around(jnp.stack([summed, swapped(summed, "yhi")]), "x")
    near_part, far_part, d_lat, d_rope, grad_uv = down_part(
        me, dp_pieces, layer_input, latent, rope, heads
    )
    parts = (near_part.astype(wide) + swapped(far_part, "core").astype(wide)).astype(bf16)
    parts = parts.reshape(n_z, 2, *parts.shape[1:])
    part = ring_sum([parts[k] for k in range(n_z)], "z")
    grad_down = part[0] + swapped(part[1].astype(bf16), "ylo").astype(wide)
    return (
        d_q.reshape(q_latent.shape),
        d_qr.reshape(q_rope.shape),
        d_lat[None],
        d_rope[None],
        grad_down[: layer_input.shape[2] // N_CTX],
        grad_uv.reshape(-1, w_uv.shape[1]),
    )


DP = ("yhi", "x")
CTX = ("z", "ylo", "core")


def solution(mesh):
    n_dp, n_ctx = mesh.shape["dp"], mesh.shape["ctx"]
    fine = Mesh(mesh.devices.reshape(2, n_dp // 2, n_ctx // 4, 2, 2), DP + CTX)
    in_specs = (
        P(None, CTX, DP),
        P(DP, CTX, None),
        P(DP, CTX, None),
        P(DP, CTX, None, None),
        P(DP, CTX, None, None),
        P(DP, CTX, None, None),
        P(),
        P(DP, CTX, None),
        P(),
    )
    out_specs = (
        P(DP, CTX, None, None),
        P(DP, CTX, None, None),
        P(DP, CTX, None),
        P(DP, CTX, None),
        P(DP + CTX, None),
        P(DP + CTX, None),
    )

    return jax.shard_map(body, mesh=fine, in_specs=in_specs, out_specs=out_specs, check_vma=False)
```

profile of v0, /device:TPU:16, one launch (start us, length us, event | category | flops | bytes accessed | tf_op | source)
XLA Modules:
  0.0 262.5 jit_solution(9676552626467142163)
XLA Ops:
  0.6 0.8 copy.15
  1.5 0.9 copy-done
  2.4 1.3 collective-permute-start
  3.8 4.3 %collective-permute-done = bf16[64,1152]{1,0:T(8,128)(2,1)S(1)} collective-permute-done((bf16[64,1152]{1,0:T(8,128)(2,1)S(1)}, bf16[64,1152]{1,0:T(8,128)(2,1)S(1)}, u32[]{:S(2)}, u32[]{:S(2)}) %collective-permute-start) | collective-permute-done | bytes 147488 | tf_op jit(solution)/shard_map/ppermute | solution.py:31
  8.1 5.9 %collective-permute-start.1 = (bf16[2,64,1152]{2,1,0:T(8,128)(2,1)S(1)}, bf16[2,64,1152]{2,1,0:T(8,128)(2,1)S(1)}, u32[]{:S(2)}, u32[]{:S(2)}) collective-permute-start(bf16[2,64,1152]{2,1,0:T(8,128)(2,1)S(1)} %pad_maximum_fusion.1), channel_id=1, source_target_pairs={{0,28},{4,0},{8,4},{12,8},{16,12},{20,16},{24,20},{28,24},{1,29},{... | collective-permute-start | bytes 884744 | tf_op jit(solution)/shard_map/ppermute | solution.py:36
  14.0 5.4 %collective-permute-done.1 = bf16[2,64,1152]{2,1,0:T(8,128)(2,1)S(1)} collective-permute-done((bf16[2,64,1152]{2,1,0:T(8,128)(2,1)S(1)}, bf16[2,64,1152]{2,1,0:T(8,128)(2,1)S(1)}, u32[]{:S(2)}, u32[]{:S(2)}) %collective-permute-start.1) | collective-permute-done | bytes 294944 | tf_op jit(solution)/shard_map/ppermute | solution.py:36
  19.4 3.7 %collective-permute-start.2 = (bf16[2,64,1152]{2,1,0:T(8,128)(2,1)S(1)}, bf16[2,64,1152]{2,1,0:T(8,128)(2,1)S(1)}, u32[]{:S(2)}, u32[]{:S(2)}) collective-permute-start(bf16[2,64,1152]{2,1,0:T(8,128)(2,1)S(1)} %collective-permute-done.1), channel_id=1, source_target_pairs={{0,28},{4,0},{8,4},{12,8},{16,12},{20,16},{24,20},{28,24},{1,29},{... | collective-permute-start | bytes 884744 | tf_op jit(solution)/shard_map/ppermute | solution.py:36
  23.1 4.5 %collective-permute-done.2 = bf16[2,64,1152]{2,1,0:T(8,128)(2,1)S(1)} collective-permute-done((bf16[2,64,1152]{2,1,0:T(8,128)(2,1)S(1)}, bf16[2,64,1152]{2,1,0:T(8,128)(2,1)S(1)}, u32[]{:S(2)}, u32[]{:S(2)}) %collective-permute-start.2) | collective-permute-done | bytes 294944 | tf_op jit(solution)/shard_map/ppermute | solution.py:36
  27.7 3.8 %collective-permute-start.8 = (bf16[2,64,1152]{2,1,0:T(8,128)(2,1)S(1)}, bf16[2,64,1152]{2,1,0:T(8,128)(2,1)S(1)}, u32[]{:S(2)}, u32[]{:S(2)}) collective-permute-start(bf16[2,64,1152]{2,1,0:T(8,128)(2,1)S(1)} %collective-permute-done.2), channel_id=1, source_target_pairs={{0,28},{4,0},{8,4},{12,8},{16,12},{20,16},{24,20},{28,24},{1,29},{... | collective-permute-start | bytes 884744 | tf_op jit(solution)/shard_map/ppermute | solution.py:36
  31.8 8.1 %collective-permute-done.6 = bf16[2,64,1152]{2,1,0:T(8,128)(2,1)S(1)} collective-permute-done((bf16[2,64,1152]{2,1,0:T(8,128)(2,1)S(1)}, bf16[2,64,1152]{2,1,0:T(8,128)(2,1)S(1)}, u32[]{:S(2)}, u32[]{:S(2)}) %collective-permute-start.6) | collective-permute-done | bytes 294944 | tf_op jit(solution)/shard_map/ppermute | solution.py:36
  40.2 7.8 %collective-permute-done.7 = bf16[2,64,1152]{2,1,0:T(8,128)(2,1)S(1)} collective-permute-done((bf16[2,64,1152]{2,1,0:T(8,128)(2,1)S(1)}, bf16[2,64,1152]{2,1,0:T(8,128)(2,1)S(1)}, u32[]{:S(2)}, u32[]{:S(2)}) %collective-permute-start.7) | collective-permute-done | bytes 294944 | tf_op jit(solution)/shard_map/ppermute | solution.py:36
  48.1 0.9 copy.16
  49.0 0.6 stack.41.me_ref
  49.6 8.1 %shard_map.137 = (bf16[1024,640]{1,0:T(8,128)(2,1)}, bf16[1024,512]{1,0:T(8,128)(2,1)}, f32[2,1,512]{2,1,0:T(1,128)}, bf16[32,64,256]{2,1,0:T(8,128)(2,1)}) custom-call(s32[6]{0:T(128)} %stack.41.me_ref, bf16[1024,512]{1,0:T(8,128)(2,1)} %bitcast.40, bf16[1024,64]{1,0:T(8,128)(2,1)} %bitcast.42, bf16[1024,512]{1,0:T(8,128)(2,1)} %bitcast.41, ...), custom_call_target="tpu_custom_call" | custom-call | flops 1000 | bytes 4194304 | tf_op jit(solution)/shard_map/pallas_call | solution.py:150
  57.8 7.1 %shard_map.138 = (f32[2,1,512]{2,1,0:T(1,128)}, f32[2,1,512]{2,1,0:T(1,128)}) custom-call(s32[6]{0:T(128)} %stack.41.me_ref, s32[64]{0:T(128)} %blocks_ref.11, bf16[8,64,1152]{2,1,0:T(8,128)(2,1)} %copy-done.13, bf16[8,64,1152]{2,1,0:T(8,128)(2,1)} %collective-permute-done.4.refs_1_, bf16[1024,640]{1,0:T(8,128)(2,1)} %get-tuple-element.32.refs_2_.refs_4_), custom_call_target="tpu_custom_call" | custom-call | flops 1342177280 | bytes 4194304 | tf_op jit(solution)/shard_map/pallas_call | solution.py:150
  64.9 0.8 copy-done.16
  65.7 7.4 %shard_map.139 = (f32[2,1,512]{2,1,0:T(1,128)}, f32[2,1,512]{2,1,0:T(1,128)}) custom-call(s32[6]{0:T(128)} %stack.41.me_ref, s32[64]{0:T(128)} %blocks_ref.11, bf16[4,64,1152]{2,1,0:T(8,128)(2,1)} %copy-done.11, bf16[4,64,1152]{2,1,0:T(8,128)(2,1)} %copy-done.10, bf16[4,64,1152]{2,1,0:T(8,128)(2,1)} %collective-permute-done.9.refs_2_.refs_1_, ...), custom_call_target="tpu_custom_call" | custom-call | flops 1342177280 | bytes 4194304 | tf_op jit(solution)/shard_map/pallas_call | solution.py:150
  73.1 9.5 %shard_map.140 = (bf16[4,64,1408]{2,1,0:T(8,128)(2,1)}, bf16[4,64,1408]{2,1,0:T(8,128)(2,1)}, f32[2,640,512]{2,1,0:T(8,128)}) custom-call(s32[6]{0:T(128)} %stack.41.me_ref, s32[64]{0:T(128)} %blocks_ref.11, bf16[4,64,1152]{2,1,0:T(8,128)(2,1)} %copy-done.11, bf16[4,64,1152]{2,1,0:T(8,128)(2,1)} %collective-permute-done.9.refs_2_.refs_1_, ...), custom_call_target="tpu_custom_call" | custom-call | flops 2684354560 | bytes 4194304 | tf_op jit(solution)/shard_map/pallas_call | solution.py:150
  82.6 6.9 %collective-permute-start.14 = (bf16[4,64,1408]{2,1,0:T(8,128)(2,1)}, bf16[4,64,1408]{2,1,0:T(8,128)(2,1)S(1)}, u32[]{:S(2)}, u32[]{:S(2)}) collective-permute-start(bf16[4,64,1408]{2,1,0:T(8,128)(2,1)} %get-tuple-element.52), channel_id=1, source_target_pairs={{0,1},{1,0},{2,3},{3,2},{4,5},{5,4},{6,7},{7,6},{8,9},{9,8},{10,11... | collective-permute-start | bytes 2162696 | tf_op jit(solution)/shard_map/ppermute | solution.py:31
  89.5 9.2 %shard_map.141 = (bf16[4,64,1408]{2,1,0:T(8,128)(2,1)}, bf16[4,64,1408]{2,1,0:T(8,128)(2,1)}, f32[2,640,512]{2,1,0:T(8,128)}) custom-call(s32[6]{0:T(128)} %stack.41.me_ref, s32[64]{0:T(128)} %blocks_ref.11, bf16[4,64,1152]{2,1,0:T(8,128)(2,1)} %copy-done.10, bf16[4,64,1152]{2,1,0:T(8,128)(2,1)} %copy-done.16, ...), custom_call_target="tpu_custom_call" | custom-call | flops 2684354560 | bytes 4194304 | tf_op jit(solution)/shard_map/pallas_call | solution.py:150
  98.6 3.4 %collective-permute-start.13 = (bf16[4,64,1408]{2,1,0:T(8,128)(2,1)}, bf16[4,64,1408]{2,1,0:T(8,128)(2,1)S(1)}, u32[]{:S(2)}, u32[]{:S(2)}) collective-permute-start(bf16[4,64,1408]{2,1,0:T(8,128)(2,1)} %get-tuple-element.50), channel_id=1, source_target_pairs={{0,1},{1,0},{2,3},{3,2},{4,5},{5,4},{6,7},{7,6},{8,9},{9,8},{10,11... | collective-permute-start | bytes 2162696 | tf_op jit(solution)/shard_map/ppermute | solution.py:31
  102.0 9.5 %shard_map.142 = (bf16[4,64,1408]{2,1,0:T(8,128)(2,1)}, bf16[4,64,1408]{2,1,0:T(8,128)(2,1)}, f32[2,640,512]{2,1,0:T(8,128)}) custom-call(s32[6]{0:T(128)} %stack.41.me_ref, s32[64]{0:T(128)} %blocks_ref.11, bf16[8,64,1152]{2,1,0:T(8,128)(2,1)} %copy-done.13, bf16[8,64,1152]{2,1,0:T(8,128)(2,1)} %collective-permute-done.4.refs_1_, ...), custom_call_target="tpu_custom_call" | custom-call | flops 2684354560 | bytes 4194304 | tf_op jit(solution)/shard_map/pallas_call | solution.py:150
  111.5 3.4 %collective-permute-start.12 = (bf16[4,64,1408]{2,1,0:T(8,128)(2,1)}, bf16[4,64,1408]{2,1,0:T(8,128)(2,1)S(1)}, u32[]{:S(2)}, u32[]{:S(2)}) collective-permute-start(bf16[4,64,1408]{2,1,0:T(8,128)(2,1)} %get-tuple-element.48), channel_id=1, source_target_pairs={{0,1},{1,0},{2,3},{3,2},{4,5},{5,4},{6,7},{7,6},{8,9},{9,8},{10,11... | collective-permute-start | bytes 2162696 | tf_op jit(solution)/shard_map/ppermute | solution.py:31
  115.0 10.6 %shard_map.143 = (bf16[4,64,1408]{2,1,0:T(8,128)(2,1)}, bf16[4,64,1408]{2,1,0:T(8,128)(2,1)}, bf16[1024,512]{1,0:T(8,128)(2,1)}, bf16[1024,64]{1,0:T(8,128)(2,1)}) custom-call(s32[6]{0:T(128)} %stack.41.me_ref, s32[64]{0:T(128)} %blocks_ref.11, bf16[8,64,1152]{2,1,0:T(8,128)(2,1)} %copy-done.13, bf16[8,64,1152]{2,1,0:T(8,128)(2,1)} %collective-permute-done.4.refs_1_, ...), custom_call_target="tpu_custom_call" | custom-call | flops 2684354560 | bytes 4194304 | tf_op jit(solution)/shard_map/pallas_call | solution.py:150
  125.6 2.3 collective-permute-start.11
  128.1 1.8 collective-permute-start.15
  130.0 0.3 collective-permute-start.18
  130.4 8.1 %collective-permute-done.15 = bf16[2,64,1408]{2,1,0:T(8,128)(2,1)S(1)} collective-permute-done((bf16[2,64,1408]{2,1,0:T(8,128)(2,1)S(1)}, bf16[2,64,1408]{2,1,0:T(8,128)(2,1)S(1)}, u32[]{:S(2)}, u32[]{:S(2)}) %collective-permute-start.15) | collective-permute-done | bytes 360480 | tf_op jit(solution)/shard_map/ppermute | solution.py:36
  138.6 3.5 %collective-permute-done.18 = bf16[2,64,1408]{2,1,0:T(8,128)(2,1)S(1)} collective-permute-done((bf16[2,64,1408]{2,1,0:T(8,128)(2,1)S(1)}, bf16[2,64,1408]{2,1,0:T(8,128)(2,1)S(1)}, u32[]{:S(2)}, u32[]{:S(2)}) %collective-permute-start.18) | collective-permute-done | bytes 360480 | tf_op jit(solution)/shard_map/ppermute | solution.py:36
  142.2 1.8 collective-permute-start.16
  144.0 0.8 collective-permute-start.19
  145.1 7.8 %collective-permute-done.16 = bf16[2,64,1408]{2,1,0:T(8,128)(2,1)S(1)} collective-permute-done((bf16[2,64,1408]{2,1,0:T(8,128)(2,1)S(1)}, bf16[2,64,1408]{2,1,0:T(8,128)(2,1)S(1)}, u32[]{:S(2)}, u32[]{:S(2)}) %collective-permute-start.16) | collective-permute-done | bytes 360480 | tf_op jit(solution)/shard_map/ppermute | solution.py:36
  152.8 1.4 collective-permute-done.19
  154.3 7.0 %collective-permute-start.20 = (bf16[2,64,1408]{2,1,0:T(8,128)(2,1)S(1)}, bf16[2,64,1408]{2,1,0:T(8,128)(2,1)S(1)}, u32[]{:S(2)}, u32[]{:S(2)}) collective-permute-start(bf16[2,64,1408]{2,1,0:T(8,128)(2,1)S(1)} %get-tuple-element.65), channel_id=1, source_target_pairs={{0,4},{4,8},{8,12},{12,16},{16,20},{20,24},{24,28},{28,0},{1,5},{5... | collective-permute-start | bytes 1081352 | tf_op jit(solution)/shard_map/ppermute | solution.py:36
  161.4 2.5 collective-permute-start.17
  163.9 7.1 %collective-permute-done.20 = bf16[2,64,1408]{2,1,0:T(8,128)(2,1)S(1)} collective-permute-done((bf16[2,64,1408]{2,1,0:T(8,128)(2,1)S(1)}, bf16[2,64,1408]{2,1,0:T(8,128)(2,1)S(1)}, u32[]{:S(2)}, u32[]{:S(2)}) %collective-permute-start.20) | collective-permute-done | bytes 360480 | tf_op jit(solution)/shard_map/ppermute | solution.py:36
  171.2 0.4 collective-permute-done.17
  171.5 9.3 %collective-permute-done.21 = bf16[2,64,1408]{2,1,0:T(8,128)(2,1)S(1)} collective-permute-done((bf16[2,64,1408]{2,1,0:T(8,128)(2,1)S(1)}, bf16[2,64,1408]{2,1,0:T(8,128)(2,1)S(1)}, u32[]{:S(2)}, u32[]{:S(2)}) %collective-permute-start.21) | collective-permute-done | bytes 360480 | tf_op jit(solution)/shard_map/ppermute | solution.py:36
  181.0 7.1 %collective-permute-start.22 = (bf16[64,1408]{1,0:T(8,128)(2,1)S(1)}, bf16[64,1408]{1,0:T(8,128)(2,1)S(1)}, u32[]{:S(2)}, u32[]{:S(2)}) collective-permute-start(bf16[64,1408]{1,0:T(8,128)(2,1)S(1)} %fusion.8), channel_id=1, source_target_pairs={{0,2},{2,0},{1,3},{3,1},{4,6},{6,4},{5,7},{7,5},{8,10},{10,8},{9,1... | collective-permute-start | bytes 540680 | tf_op jit(solution)/shard_map/ppermute | solution.py:31
  188.2 4.4 %collective-permute-done.22 = bf16[64,1408]{1,0:T(8,128)(2,1)S(1)} collective-permute-done((bf16[64,1408]{1,0:T(8,128)(2,1)S(1)}, bf16[64,1408]{1,0:T(8,128)(2,1)S(1)}, u32[]{:S(2)}, u32[]{:S(2)}) %collective-permute-start.22) | collective-permute-done | bytes 180256 | tf_op jit(solution)/shard_map/ppermute | solution.py:31
  192.7 7.0 %collective-permute-done.23 = bf16[64,1408]{1,0:T(8,128)(2,1)S(1)} collective-permute-done((bf16[64,1408]{1,0:T(8,128)(2,1)S(1)}, bf16[64,1408]{1,0:T(8,128)(2,1)S(1)}, u32[]{:S(2)}, u32[]{:S(2)}) %collective-permute-start.23) | collective-permute-done | bytes 180256 | tf_op jit(solution)/shard_map/ppermute | solution.py:31
  199.7 1.6 collective-permute-start.25
  201.3 1.7 collective-permute-start.24
  203.1 8.4 %collective-permute-done.25.refs_3_ = bf16[2,64,1408]{2,1,0:T(8,128)(2,1)S(1)} collective-permute-done((bf16[2,64,1408]{2,1,0:T(8,128)(2,1)S(1)}, bf16[2,64,1408]{2,1,0:T(8,128)(2,1)S(1)}, u32[]{:S(2)}, u32[]{:S(2)}) %collective-permute-start.25) | collective-permute-done | bytes 360480 | tf_op jit(solution)/shard_map/ppermute | solution.py:36
  211.5 0.8 collective-permute-start.26
  212.2 7.9 %collective-permute-done.26.refs_2_ = bf16[2,64,1408]{2,1,0:T(8,128)(2,1)S(1)} collective-permute-done((bf16[2,64,1408]{2,1,0:T(8,128)(2,1)S(1)}, bf16[2,64,1408]{2,1,0:T(8,128)(2,1)S(1)}, u32[]{:S(2)}, u32[]{:S(2)}) %collective-permute-start.26) | collective-permute-done | bytes 360480 | tf_op jit(solution)/shard_map/ppermute | solution.py:36
  220.1 0.7 copy-done.8
  220.9 5.3 %shard_map.144 = (bf16[16,32,576]{2,1,0:T(8,128)(2,1)}, bf16[16,32,576]{2,1,0:T(8,128)(2,1)}, bf16[128,512]{1,0:T(8,128)(2,1)}, bf16[128,64]{1,0:T(8,128)(2,1)}, f32[2,8,128]{2,1,0:T(8,128)}) custom-call(s32[6]{0:T(128)} %stack.41.me_ref, bf16[2,64,1408]{2,1,0:T(8,128)(2,1)} %copy-done.1, bf16[2,64,1408]{2,1,0:T(8,128)(2,1)} %copy-done.7, ...), custom_call_target="tpu_custom_call" | custom-call | flops 1000 | bytes 4194304 | tf_op jit(solution)/shard_map/pallas_call | solution.py:150
  226.2 2.3 collective-permute-done.27
  228.5 1.3 add_convert_fusion.1
  229.9 5.7 %collective-permute-done.28 = bf16[2,32,576]{2,1,0:T(8,128)(2,1)S(1)} collective-permute-done((bf16[2,32,576]{2,1,0:T(8,128)(2,1)S(1)}, bf16[2,32,576]{2,1,0:T(8,128)(2,1)S(1)}, u32[]{:S(2)}, u32[]{:S(2)}) %collective-permute-start.28) | collective-permute-done | bytes 73760 | tf_op jit(solution)/shard_map/ppermute | solution.py:36
  235.7 3.2 %collective-permute-start.32 = (bf16[2,32,576]{2,1,0:T(8,128)(2,1)S(1)}, bf16[2,32,576]{2,1,0:T(8,128)(2,1)S(1)}, u32[]{:S(2)}, u32[]{:S(2)}) collective-permute-start(bf16[2,32,576]{2,1,0:T(8,128)(2,1)S(1)} %get-tuple-element.73), channel_id=1, source_target_pairs={{0,28},{4,0},{8,4},{12,8},{16,12},{20,16},{24,20},{28,24},{1,29},{... | collective-permute-start | bytes 221192 | tf_op jit(solution)/shard_map/ppermute | solution.py:36
  239.0 2.4 collective-permute-done.29
  241.5 5.6 %collective-permute-done.30 = bf16[2,32,576]{2,1,0:T(8,128)(2,1)S(1)} collective-permute-done((bf16[2,32,576]{2,1,0:T(8,128)(2,1)S(1)}, bf16[2,32,576]{2,1,0:T(8,128)(2,1)S(1)}, u32[]{:S(2)}, u32[]{:S(2)}) %collective-permute-start.30) | collective-permute-done | bytes 73760 | tf_op jit(solution)/shard_map/ppermute | solution.py:36
  247.3 2.0 collective-permute-start.31
  249.3 2.7 %collective-permute-done.33 = bf16[2,32,576]{2,1,0:T(8,128)(2,1)S(1)} collective-permute-done((bf16[2,32,576]{2,1,0:T(8,128)(2,1)S(1)}, bf16[2,32,576]{2,1,0:T(8,128)(2,1)S(1)}, u32[]{:S(2)}, u32[]{:S(2)}) %collective-permute-start.33) | collective-permute-done | bytes 73760 | tf_op jit(solution)/shard_map/ppermute | solution.py:36
  252.0 1.0 collective-permute-start.34
  253.0 0.8 copy.17
  253.9 0.7 copy.18
  254.6 0.6 copy.21
  255.2 1.4 collective-permute-done.34
  256.6 3.3 %collective-permute-start.35 = (bf16[32,576]{1,0:T(8,128)(2,1)S(1)}, bf16[32,576]{1,0:T(8,128)(2,1)S(1)}, u32[]{:S(2)}, u32[]{:S(2)}) collective-permute-start(bf16[32,576]{1,0:T(8,128)(2,1)S(1)} %fusion.9), channel_id=1, source_target_pairs={{0,2},{2,0},{1,3},{3,1},{4,6},{6,4},{5,7},{7,5},{8,10},{10,8},{9,1... | collective-permute-start | bytes 110600 | tf_op jit(solution)/shard_map/ppermute | solution.py:31
  259.9 2.0 collective-permute-done.35
  261.9 0.6 slice_add_fusion.6
  (89 shorter events, 2.7 us)
Async XLA Ops:
  1.5 0.9 copy-start
  2.4 5.6 %collective-permute-start = (bf16[64,1152]{1,0:T(8,128)(2,1)S(1)}, bf16[64,1152]{1,0:T(8,128)(2,1)S(1)}, u32[]{:S(2)}, u32[]{:S(2)}) collective-permute-start(bf16[64,1152]{1,0:T(8,128)(2,1)S(1)} %shard_map.136), channel_id=1, source_target_pairs={{0,2},{2,0},{1,3},{3,1},{4,6},{6,4},{5,7},{7,5},{8,10},{10,8},{9,1... | collective-permute-start | bytes 442376 | tf_op jit(solution)/shard_map/ppermute | solution.py:31
  8.1 11.3 %collective-permute-start.1 = (bf16[2,64,1152]{2,1,0:T(8,128)(2,1)S(1)}, bf16[2,64,1152]{2,1,0:T(8,128)(2,1)S(1)}, u32[]{:S(2)}, u32[]{:S(2)}) collective-permute-start(bf16[2,64,1152]{2,1,0:T(8,128)(2,1)S(1)} %pad_maximum_fusion.1), channel_id=1, source_target_pairs={{0,28},{4,0},{8,4},{12,8},{16,12},{20,16},{24,20},{28,24},{1,29},{... | collective-permute-start | bytes 884744 | tf_op jit(solution)/shard_map/ppermute | solution.py:36
  14.0 9.1 %collective-permute-start.3 = (bf16[2,64,1152]{2,1,0:T(8,128)(2,1)S(1)}, bf16[2,64,1152]{2,1,0:T(8,128)(2,1)S(1)}, u32[]{:S(2)}, u32[]{:S(2)}) collective-permute-start(bf16[2,64,1152]{2,1,0:T(8,128)(2,1)S(1)} %pad_maximum_fusion.1), channel_id=1, source_target_pairs={{0,4},{4,8},{8,12},{12,16},{16,20},{20,24},{24,28},{28,0},{1,5},{5... | collective-permute-start | bytes 884744 | tf_op jit(solution)/shard_map/ppermute | solution.py:36
  19.4 8.2 %collective-permute-start.2 = (bf16[2,64,1152]{2,1,0:T(8,128)(2,1)S(1)}, bf16[2,64,1152]{2,1,0:T(8,128)(2,1)S(1)}, u32[]{:S(2)}, u32[]{:S(2)}) collective-permute-start(bf16[2,64,1152]{2,1,0:T(8,128)(2,1)S(1)} %collective-permute-done.1), channel_id=1, source_target_pairs={{0,28},{4,0},{8,4},{12,8},{16,12},{20,16},{24,20},{28,24},{1,29},{... | collective-permute-start | bytes 884744 | tf_op jit(solution)/shard_map/ppermute | solution.py:36
  23.1 8.5 %collective-permute-start.5 = (bf16[2,64,1152]{2,1,0:T(8,128)(2,1)S(1)}, bf16[2,64,1152]{2,1,0:T(8,128)(2,1)S(1)}, u32[]{:S(2)}, u32[]{:S(2)}) collective-permute-start(bf16[2,64,1152]{2,1,0:T(8,128)(2,1)S(1)} %collective-permute-done.3), channel_id=1, source_target_pairs={{0,4},{4,8},{8,12},{12,16},{16,20},{20,24},{24,28},{28,0},{1,5},{5... | collective-permute-start | bytes 884744 | tf_op jit(solution)/shard_map/ppermute | solution.py:36
  27.7 12.3 %collective-permute-start.8 = (bf16[2,64,1152]{2,1,0:T(8,128)(2,1)S(1)}, bf16[2,64,1152]{2,1,0:T(8,128)(2,1)S(1)}, u32[]{:S(2)}, u32[]{:S(2)}) collective-permute-start(bf16[2,64,1152]{2,1,0:T(8,128)(2,1)S(1)} %collective-permute-done.2), channel_id=1, source_target_pairs={{0,28},{4,0},{8,4},{12,8},{16,12},{20,16},{24,20},{28,24},{1,29},{... | collective-permute-start | bytes 884744 | tf_op jit(solution)/shard_map/ppermute | solution.py:36
  31.6 16.5 %copy-start.12 = (bf16[1,128,8,64]{1,3,2,0:T(8,128)(2,1)S(1)}, bf16[1,128,8,64]{1,3,2,0:T(8,128)(2,1)}, u32[]{:S(2)}) copy-start(bf16[1,128,8,64]{1,3,2,0:T(8,128)(2,1)} %param.13) | copy-start | bytes 393220
  31.6 8.4 %collective-permute-start.6 = (bf16[2,64,1152]{2,1,0:T(8,128)(2,1)S(1)}, bf16[2,64,1152]{2,1,0:T(8,128)(2,1)S(1)}, u32[]{:S(2)}, u32[]{:S(2)}) collective-permute-start(bf16[2,64,1152]{2,1,0:T(8,128)(2,1)S(1)} %collective-permute-done.5), channel_id=1, source_target_pairs={{0,4},{4,8},{8,12},{12,16},{16,20},{20,24},{24,28},{28,0},{1,5},{5... | collective-permute-start | bytes 884744 | tf_op jit(solution)/shard_map/ppermute | solution.py:36
  31.7 26.0 %copy-start.13 = (bf16[8,64,1152]{2,1,0:T(8,128)(2,1)}, bf16[8,64,1152]{2,1,0:T(8,128)(2,1)S(1)}, u32[]{:S(2)}) copy-start(bf16[8,64,1152]{2,1,0:T(8,128)(2,1)S(1)} %constant_dynamic-update-slice_fusion.refs_0_) | copy-start | bytes 3538948
  31.7 26.0 %collective-permute-start.4 = (bf16[8,64,1152]{2,1,0:T(8,128)(2,1)S(1)}, bf16[8,64,1152]{2,1,0:T(8,128)(2,1)}, u32[]{:S(2)}, u32[]{:S(2)}) collective-permute-start(bf16[8,64,1152]{2,1,0:T(8,128)(2,1)S(1)} %constant_dynamic-update-slice_fusion.refs_0_), channel_id=1, source_target_pairs={{0,1},{1,0},{2,3},{3,2},{4,5},{5,4},{6,7},{7,6},{8,9},{9,8},{10,11... | collective-permute-start | bytes 3538952 | tf_op jit(solution)/shard_map/ppermute | solution.py:31
  40.0 7.9 %collective-permute-start.7 = (bf16[2,64,1152]{2,1,0:T(8,128)(2,1)S(1)}, bf16[2,64,1152]{2,1,0:T(8,128)(2,1)S(1)}, u32[]{:S(2)}, u32[]{:S(2)}) collective-permute-start(bf16[2,64,1152]{2,1,0:T(8,128)(2,1)S(1)} %collective-permute-done.6), channel_id=1, source_target_pairs={{0,4},{4,8},{8,12},{12,16},{16,20},{20,24},{24,28},{28,0},{1,5},{5... | collective-permute-start | bytes 884744 | tf_op jit(solution)/shard_map/ppermute | solution.py:36
  40.1 17.7 %copy-start.10 = (bf16[4,64,1152]{2,1,0:T(8,128)(2,1)}, bf16[4,64,1152]{2,1,0:T(8,128)(2,1)S(1)}, u32[]{:S(2)}) copy-start(bf16[4,64,1152]{2,1,0:T(8,128)(2,1)S(1)} %constant_dynamic-update-slice_fusion.7.refs_1_.refs_0_) | copy-start | bytes 1769476
  40.1 24.8 %collective-permute-start.10 = (bf16[4,64,1152]{2,1,0:T(8,128)(2,1)S(1)}, bf16[4,64,1152]{2,1,0:T(8,128)(2,1)S(1)}, u32[]{:S(2)}, u32[]{:S(2)}) collective-permute-start(bf16[4,64,1152]{2,1,0:T(8,128)(2,1)S(1)} %constant_dynamic-update-slice_fusion.7.refs_1_.refs_0_), channel_id=1, source_target_pairs={{0,1},{1,0},{2,3},{3,2},{4,5},{5,4},{6,7},{7,6},{8,9},{9,8},{10,11... | collective-permute-start | bytes 1769480 | tf_op jit(solution)/shard_map/ppermute | solution.py:31
  48.0 9.8 %copy-start.11 = (bf16[4,64,1152]{2,1,0:T(8,128)(2,1)}, bf16[4,64,1152]{2,1,0:T(8,128)(2,1)S(1)}, u32[]{:S(2)}) copy-start(bf16[4,64,1152]{2,1,0:T(8,128)(2,1)S(1)} %constant_dynamic-update-slice_fusion.5.refs_0_) | copy-start | bytes 1769476
  48.0 16.9 %collective-permute-start.9 = (bf16[4,64,1152]{2,1,0:T(8,128)(2,1)S(1)}, bf16[4,64,1152]{2,1,0:T(8,128)(2,1)}, u32[]{:S(2)}, u32[]{:S(2)}) collective-permute-start(bf16[4,64,1152]{2,1,0:T(8,128)(2,1)S(1)} %constant_dynamic-update-slice_fusion.5.refs_0_), channel_id=1, source_target_pairs={{0,1},{1,0},{2,3},{3,2},{4,5},{5,4},{6,7},{7,6},{8,9},{9,8},{10,11... | collective-permute-start | bytes 1769480 | tf_op jit(solution)/shard_map/ppermute | solution.py:31
  64.9 0.8 copy-start.16
  82.6 45.3 %collective-permute-start.14 = (bf16[4,64,1408]{2,1,0:T(8,128)(2,1)}, bf16[4,64,1408]{2,1,0:T(8,128)(2,1)S(1)}, u32[]{:S(2)}, u32[]{:S(2)}) collective-permute-start(bf16[4,64,1408]{2,1,0:T(8,128)(2,1)} %get-tuple-element.52), channel_id=1, source_target_pairs={{0,1},{1,0},{2,3},{3,2},{4,5},{5,4},{6,7},{7,6},{8,9},{9,8},{10,11... | collective-permute-start | bytes 2162696 | tf_op jit(solution)/shard_map/ppermute | solution.py:31
  98.6 31.6 %collective-permute-start.13 = (bf16[4,64,1408]{2,1,0:T(8,128)(2,1)}, bf16[4,64,1408]{2,1,0:T(8,128)(2,1)S(1)}, u32[]{:S(2)}, u32[]{:S(2)}) collective-permute-start(bf16[4,64,1408]{2,1,0:T(8,128)(2,1)} %get-tuple-element.50), channel_id=1, source_target_pairs={{0,1},{1,0},{2,3},{3,2},{4,5},{5,4},{6,7},{7,6},{8,9},{9,8},{10,11... | collective-permute-start | bytes 2162696 | tf_op jit(solution)/shard_map/ppermute | solution.py:31
  111.5 33.4 %collective-permute-start.12 = (bf16[4,64,1408]{2,1,0:T(8,128)(2,1)}, bf16[4,64,1408]{2,1,0:T(8,128)(2,1)S(1)}, u32[]{:S(2)}, u32[]{:S(2)}) collective-permute-start(bf16[4,64,1408]{2,1,0:T(8,128)(2,1)} %get-tuple-element.48), channel_id=1, source_target_pairs={{0,1},{1,0},{2,3},{3,2},{4,5},{5,4},{6,7},{7,6},{8,9},{9,8},{10,11... | collective-permute-start | bytes 2162696 | tf_op jit(solution)/shard_map/ppermute | solution.py:31
  115.0 12.9 %copy-start.2 = (bf16[4,64,1408]{2,1,0:T(8,128)(2,1)S(1)}, bf16[4,64,1408]{2,1,0:T(8,128)(2,1)}, u32[]{:S(2)}) copy-start(bf16[4,64,1408]{2,1,0:T(8,128)(2,1)} %get-tuple-element.51) | copy-start | bytes 2162692
  125.6 35.7 %collective-permute-start.11 = (bf16[4,64,1408]{2,1,0:T(8,128)(2,1)}, bf16[4,64,1408]{2,1,0:T(8,128)(2,1)S(1)}, u32[]{:S(2)}, u32[]{:S(2)}) collective-permute-start(bf16[4,64,1408]{2,1,0:T(8,128)(2,1)} %get-tuple-element.46), channel_id=1, source_target_pairs={{0,1},{1,0},{2,3},{3,2},{4,5},{5,4},{6,7},{7,6},{8,9},{9,8},{10,11... | collective-permute-start | bytes 2162696 | tf_op jit(solution)/shard_map/ppermute | solution.py:31
  127.9 2.3 copy-start.5
  128.1 10.4 %collective-permute-start.15 = (bf16[2,64,1408]{2,1,0:T(8,128)(2,1)S(1)}, bf16[2,64,1408]{2,1,0:T(8,128)(2,1)S(1)}, u32[]{:S(2)}, u32[]{:S(2)}) collective-permute-start(bf16[2,64,1408]{2,1,0:T(8,128)(2,1)S(1)} %get-tuple-element.68), channel_id=1, source_target_pairs={{0,28},{4,0},{8,4},{12,8},{16,12},{20,16},{24,20},{28,24},{1,29},{... | collective-permute-start | bytes 1081352 | tf_op jit(solution)/shard_map/ppermute | solution.py:36
  130.0 12.1 %collective-permute-start.18 = (bf16[2,64,1408]{2,1,0:T(8,128)(2,1)S(1)}, bf16[2,64,1408]{2,1,0:T(8,128)(2,1)S(1)}, u32[]{:S(2)}, u32[]{:S(2)}) collective-permute-start(bf16[2,64,1408]{2,1,0:T(8,128)(2,1)S(1)} %get-tuple-element.69), channel_id=1, source_target_pairs={{0,4},{4,8},{8,12},{12,16},{16,20},{20,24},{24,28},{28,0},{1,5},{5... | collective-permute-start | bytes 1081352 | tf_op jit(solution)/shard_map/ppermute | solution.py:36
  130.4 14.5 %copy-start.4 = (bf16[4,64,1408]{2,1,0:T(8,128)(2,1)S(1)}, bf16[4,64,1408]{2,1,0:T(8,128)(2,1)}, u32[]{:S(2)}) copy-start(bf16[4,64,1408]{2,1,0:T(8,128)(2,1)} %get-tuple-element.47) | copy-start | bytes 2162692
  142.2 10.6 %collective-permute-start.16 = (bf16[2,64,1408]{2,1,0:T(8,128)(2,1)S(1)}, bf16[2,64,1408]{2,1,0:T(8,128)(2,1)S(1)}, u32[]{:S(2)}, u32[]{:S(2)}) collective-permute-start(bf16[2,64,1408]{2,1,0:T(8,128)(2,1)S(1)} %get-tuple-element.66), channel_id=1, source_target_pairs={{0,28},{4,0},{8,4},{12,8},{16,12},{20,16},{24,20},{28,24},{1,29},{... | collective-permute-start | bytes 1081352 | tf_op jit(solution)/shard_map/ppermute | solution.py:36
  144.0 10.1 %collective-permute-start.19 = (bf16[2,64,1408]{2,1,0:T(8,128)(2,1)S(1)}, bf16[2,64,1408]{2,1,0:T(8,128)(2,1)S(1)}, u32[]{:S(2)}, u32[]{:S(2)}) collective-permute-start(bf16[2,64,1408]{2,1,0:T(8,128)(2,1)S(1)} %get-tuple-element.67), channel_id=1, source_target_pairs={{0,4},{4,8},{8,12},{12,16},{16,20},{20,24},{24,28},{28,0},{1,5},{5... | collective-permute-start | bytes 1081352 | tf_op jit(solution)/shard_map/ppermute | solution.py:36
  145.1 16.2 %copy-start.3 = (bf16[4,64,1408]{2,1,0:T(8,128)(2,1)S(1)}, bf16[4,64,1408]{2,1,0:T(8,128)(2,1)}, u32[]{:S(2)}) copy-start(bf16[4,64,1408]{2,1,0:T(8,128)(2,1)} %get-tuple-element.45) | copy-start | bytes 2162692
  154.3 16.7 %collective-permute-start.20 = (bf16[2,64,1408]{2,1,0:T(8,128)(2,1)S(1)}, bf16[2,64,1408]{2,1,0:T(8,128)(2,1)S(1)}, u32[]{:S(2)}, u32[]{:S(2)}) collective-permute-start(bf16[2,64,1408]{2,1,0:T(8,128)(2,1)S(1)} %get-tuple-element.65), channel_id=1, source_target_pairs={{0,4},{4,8},{8,12},{12,16},{16,20},{20,24},{24,28},{28,0},{1,5},{5... | collective-permute-start | bytes 1081352 | tf_op jit(solution)/shard_map/ppermute | solution.py:36
  161.4 10.1 %collective-permute-start.17 = (bf16[2,64,1408]{2,1,0:T(8,128)(2,1)S(1)}, bf16[2,64,1408]{2,1,0:T(8,128)(2,1)S(1)}, u32[]{:S(2)}, u32[]{:S(2)}) collective-permute-start(bf16[2,64,1408]{2,1,0:T(8,128)(2,1)S(1)} %get-tuple-element.64), channel_id=1, source_target_pairs={{0,28},{4,0},{8,4},{12,8},{16,12},{20,16},{24,20},{28,24},{1,29},{... | collective-permute-start | bytes 1081352 | tf_op jit(solution)/shard_map/ppermute | solution.py:36
  171.1 9.8 %collective-permute-start.21 = (bf16[2,64,1408]{2,1,0:T(8,128)(2,1)S(1)}, bf16[2,64,1408]{2,1,0:T(8,128)(2,1)S(1)}, u32[]{:S(2)}, u32[]{:S(2)}) collective-permute-start(bf16[2,64,1408]{2,1,0:T(8,128)(2,1)S(1)} %fusion.2), channel_id=1, source_target_pairs={{0,4},{4,8},{8,12},{12,16},{16,20},{20,24},{24,28},{28,0},{1,5},{5... | collective-permute-start | bytes 1081352 | tf_op jit(solution)/shard_map/ppermute | solution.py:36
  181.0 11.6 %collective-permute-start.22 = (bf16[64,1408]{1,0:T(8,128)(2,1)S(1)}, bf16[64,1408]{1,0:T(8,128)(2,1)S(1)}, u32[]{:S(2)}, u32[]{:S(2)}) collective-permute-start(bf16[64,1408]{1,0:T(8,128)(2,1)S(1)} %fusion.8), channel_id=1, source_target_pairs={{0,2},{2,0},{1,3},{3,1},{4,6},{6,4},{5,7},{7,5},{8,10},{10,8},{9,1... | collective-permute-start | bytes 540680 | tf_op jit(solution)/shard_map/ppermute | solution.py:31
  192.6 7.1 %collective-permute-start.23 = (bf16[64,1408]{1,0:T(8,128)(2,1)S(1)}, bf16[64,1408]{1,0:T(8,128)(2,1)S(1)}, u32[]{:S(2)}, u32[]{:S(2)}) collective-permute-start(bf16[64,1408]{1,0:T(8,128)(2,1)S(1)} %fusion.7), channel_id=1, source_target_pairs={{0,128},{128,0},{1,129},{129,1},{2,130},{130,2},{3,131},{131,3},{4... | collective-permute-start | bytes 540680 | tf_op jit(solution)/shard_map/ppermute | solution.py:31
  199.7 20.4 %copy-start.1 = (bf16[2,64,1408]{2,1,0:T(8,128)(2,1)}, bf16[2,64,1408]{2,1,0:T(8,128)(2,1)S(1)}, u32[]{:S(2)}) copy-start(bf16[2,64,1408]{2,1,0:T(8,128)(2,1)S(1)} %pad_maximum_fusion.refs_0_) | copy-start | bytes 1081348
  199.7 11.7 %collective-permute-start.25 = (bf16[2,64,1408]{2,1,0:T(8,128)(2,1)S(1)}, bf16[2,64,1408]{2,1,0:T(8,128)(2,1)S(1)}, u32[]{:S(2)}, u32[]{:S(2)}) collective-permute-start(bf16[2,64,1408]{2,1,0:T(8,128)(2,1)S(1)} %pad_maximum_fusion.refs_0_), channel_id=1, source_target_pairs={{0,32},{32,64},{64,96},{96,0},{1,33},{33,65},{65,97},{97,1},{2,34}... | collective-permute-start | bytes 1081352 | tf_op jit(solution)/shard_map/ppermute | solution.py:36
  201.3 10.9 %collective-permute-start.24 = (bf16[2,64,1408]{2,1,0:T(8,128)(2,1)S(1)}, bf16[2,64,1408]{2,1,0:T(8,128)(2,1)S(1)}, u32[]{:S(2)}, u32[]{:S(2)}) collective-permute-start(bf16[2,64,1408]{2,1,0:T(8,128)(2,1)S(1)} %pad_maximum_fusion.refs_0_), channel_id=1, source_target_pairs={{0,96},{32,0},{64,32},{96,64},{1,97},{33,1},{65,33},{97,65},{2,98}... | collective-permute-start | bytes 1081352 | tf_op jit(solution)/shard_map/ppermute | solution.py:36
  211.5 8.6 %copy-start.6 = (bf16[2,64,1408]{2,1,0:T(8,128)(2,1)}, bf16[2,64,1408]{2,1,0:T(8,128)(2,1)S(1)}, u32[]{:S(2)}) copy-start(bf16[2,64,1408]{2,1,0:T(8,128)(2,1)S(1)} %collective-permute-done.25.refs_3_) | copy-start | bytes 1081348
  211.5 8.6 %collective-permute-start.26 = (bf16[2,64,1408]{2,1,0:T(8,128)(2,1)S(1)}, bf16[2,64,1408]{2,1,0:T(8,128)(2,1)S(1)}, u32[]{:S(2)}, u32[]{:S(2)}) collective-permute-start(bf16[2,64,1408]{2,1,0:T(8,128)(2,1)S(1)} %collective-permute-done.25.refs_3_), channel_id=1, source_target_pairs={{0,32},{32,64},{64,96},{96,0},{1,33},{33,65},{65,97},{97,1},{2,34}... | collective-permute-start | bytes 1081352 | tf_op jit(solution)/shard_map/ppermute | solution.py:36
  212.2 7.9 %copy-start.7 = (bf16[2,64,1408]{2,1,0:T(8,128)(2,1)}, bf16[2,64,1408]{2,1,0:T(8,128)(2,1)S(1)}, u32[]{:S(2)}) copy-start(bf16[2,64,1408]{2,1,0:T(8,128)(2,1)S(1)} %collective-permute-done.24.refs_1_) | copy-start | bytes 1081348
  220.1 0.7 copy-start.8
  226.2 2.3 collective-permute-start.27
  228.5 24.5 %copy-start.9 = (bf16[1024,64]{1,0:T(8,128)(2,1)S(1)}, bf16[1024,64]{1,0:T(8,128)(2,1)}, u32[]{:S(2)}) copy-start(bf16[1024,64]{1,0:T(8,128)(2,1)} %get-tuple-element.44) | copy-start | bytes 393220
  229.8 24.1 %copy-start.14 = (bf16[128,64]{1,0:T(8,128)(2,1)S(1)}, bf16[128,64]{1,0:T(8,128)(2,1)}, u32[]{:S(2)}) copy-start(bf16[128,64]{1,0:T(8,128)(2,1)} %get-tuple-element.54) | copy-start | bytes 49156
  229.8 24.8 %copy-start.15 = (f32[2,8,128]{2,1,0:T(8,128)S(1)}, f32[2,8,128]{2,1,0:T(8,128)}, u32[]{:S(2)}) copy-start(f32[2,8,128]{2,1,0:T(8,128)} %get-tuple-element.57) | copy-start | bytes 24580
  229.8 5.8 %collective-permute-start.28 = (bf16[2,32,576]{2,1,0:T(8,128)(2,1)S(1)}, bf16[2,32,576]{2,1,0:T(8,128)(2,1)S(1)}, u32[]{:S(2)}, u32[]{:S(2)}) collective-permute-start(bf16[2,32,576]{2,1,0:T(8,128)(2,1)S(1)} %get-tuple-element.72), channel_id=1, source_target_pairs={{0,4},{4,8},{8,12},{12,16},{16,20},{20,24},{24,28},{28,0},{1,5},{5... | collective-permute-start | bytes 221192 | tf_op jit(solution)/shard_map/ppermute | solution.py:36
  235.6 5.7 %collective-permute-start.29 = (bf16[2,32,576]{2,1,0:T(8,128)(2,1)S(1)}, bf16[2,32,576]{2,1,0:T(8,128)(2,1)S(1)}, u32[]{:S(2)}, u32[]{:S(2)}) collective-permute-start(bf16[2,32,576]{2,1,0:T(8,128)(2,1)S(1)} %add_convert_fusion.6), channel_id=1, source_target_pairs={{0,4},{4,8},{8,12},{12,16},{16,20},{20,24},{24,28},{28,0},{1,5},{5... | collective-permute-start | bytes 221192 | tf_op jit(solution)/shard_map/ppermute | solution.py:36
  235.7 5.8 %collective-permute-start.32 = (bf16[2,32,576]{2,1,0:T(8,128)(2,1)S(1)}, bf16[2,32,576]{2,1,0:T(8,128)(2,1)S(1)}, u32[]{:S(2)}, u32[]{:S(2)}) collective-permute-start(bf16[2,32,576]{2,1,0:T(8,128)(2,1)S(1)} %get-tuple-element.73), channel_id=1, source_target_pairs={{0,28},{4,0},{8,4},{12,8},{16,12},{20,16},{24,20},{28,24},{1,29},{... | collective-permute-start | bytes 221192 | tf_op jit(solution)/shard_map/ppermute | solution.py:36
  241.4 5.7 %collective-permute-start.30 = (bf16[2,32,576]{2,1,0:T(8,128)(2,1)S(1)}, bf16[2,32,576]{2,1,0:T(8,128)(2,1)S(1)}, u32[]{:S(2)}, u32[]{:S(2)}) collective-permute-start(bf16[2,32,576]{2,1,0:T(8,128)(2,1)S(1)} %add_convert_fusion.5), channel_id=1, source_target_pairs={{0,4},{4,8},{8,12},{12,16},{16,20},{20,24},{24,28},{28,0},{1,5},{5... | collective-permute-start | bytes 221192 | tf_op jit(solution)/shard_map/ppermute | solution.py:36
  247.2 4.8 %collective-permute-start.33 = (bf16[2,32,576]{2,1,0:T(8,128)(2,1)S(1)}, bf16[2,32,576]{2,1,0:T(8,128)(2,1)S(1)}, u32[]{:S(2)}, u32[]{:S(2)}) collective-permute-start(bf16[2,32,576]{2,1,0:T(8,128)(2,1)S(1)} %get-tuple-element.71), channel_id=1, source_target_pairs={{0,28},{4,0},{8,4},{12,8},{16,12},{20,16},{24,20},{28,24},{1,29},{... | collective-permute-start | bytes 221192 | tf_op jit(solution)/shard_map/ppermute | solution.py:36
  247.3 7.9 %collective-permute-start.31 = (bf16[2,32,576]{2,1,0:T(8,128)(2,1)S(1)}, bf16[2,32,576]{2,1,0:T(8,128)(2,1)S(1)}, u32[]{:S(2)}, u32[]{:S(2)}) collective-permute-start(bf16[2,32,576]{2,1,0:T(8,128)(2,1)S(1)} %get-tuple-element.70), channel_id=1, source_target_pairs={{0,4},{4,8},{8,12},{12,16},{16,20},{20,24},{24,28},{28,0},{1,5},{5... | collective-permute-start | bytes 221192 | tf_op jit(solution)/shard_map/ppermute | solution.py:36
  252.0 4.5 %collective-permute-start.34 = (bf16[2,32,576]{2,1,0:T(8,128)(2,1)S(1)}, bf16[2,32,576]{2,1,0:T(8,128)(2,1)S(1)}, u32[]{:S(2)}, u32[]{:S(2)}) collective-permute-start(bf16[2,32,576]{2,1,0:T(8,128)(2,1)S(1)} %add_convert_fusion.2), channel_id=1, source_target_pairs={{0,28},{4,0},{8,4},{12,8},{16,12},{20,16},{24,20},{28,24},{1,29},{... | collective-permute-start | bytes 221192 | tf_op jit(solution)/shard_map/ppermute | solution.py:36
  256.6 5.3 %collective-permute-start.35 = (bf16[32,576]{1,0:T(8,128)(2,1)S(1)}, bf16[32,576]{1,0:T(8,128)(2,1)S(1)}, u32[]{:S(2)}, u32[]{:S(2)}) collective-permute-start(bf16[32,576]{1,0:T(8,128)(2,1)S(1)} %fusion.9), channel_id=1, source_target_pairs={{0,2},{2,0},{1,3},{3,1},{4,6},{6,4},{5,7},{7,5},{8,10},{10,8},{9,1... | collective-permute-start | bytes 110600 | tf_op jit(solution)/shard_map/ppermute | solution.py:31
where the time goes:
time: 263 us
  waiting for transfers between devices  117 us (44%)
  Pallas kernels  66.8 us (25%)
  starting transfers between devices  66.6 us (25%)
  local copies, waits for them, and re-layouts  7.32 us (3%)
  other arithmetic  3.26 us (1%)
    ppermute x24, waiting for transfers between devices, shifted(): return lax.ppermute(x, axis, [(i, (i + by) % n) for i in range(n)])  97.5 us
    pallas_call x9, Pallas kernels, call(): pl.pallas_call(kernel, out_shape=tuple((jax.ShapeDtypeStruct(*o) for o in...  66.8 us
    ppermute x24, starting transfers between devices, shifted(): return lax.ppermute(x, axis, [(i, (i + by) % n) for i in range(n)])  38.4 us
    ppermute x12, starting transfers between devices, swapped(): return lax.ppermute(x, axis, [(0, 1), (1, 0)])  28.2 us
    ppermute x12, waiting for transfers between devices, swapped(): return lax.ppermute(x, axis, [(0, 1), (1, 0)])  20 us
    unnamed x45, local copies, waits for them, and re-layouts  6.53 us
  transfers between devices with their start and end apart: 36, of which 23 were waited for; matrix products, arithmetic and copies ran while one was open for 2% of the time, Pallas kernels for 17%

commit v1 on v0

v1 whole, which is shorter than its diff:
```python
import math

import jax
import jax.numpy as jnp
from jax import lax
from jax.experimental import pallas as pl
from jax.experimental.pallas import tpu as pltpu
from jax.sharding import Mesh, PartitionSpec as P


softmax_scale = 1.0 / math.sqrt(192.0)
log2e = 1.0 / math.log(2.0)
TILE = 256
N_DP = 8
N_CTX = 32


def nt(a, b):
    return lax.dot_general(a, b, (((1,), (1,)), ((), ())), preferred_element_type=jnp.float32)


def nn(a, b):
    return lax.dot_general(a, b, (((1,), (0,)), ((), ())), preferred_element_type=jnp.float32)


def tn(a, b):
    return lax.dot_general(a, b, (((0,), (0,)), ((), ())), preferred_element_type=jnp.float32)


def swapped(x, axis):
    return lax.ppermute(x, axis, [(0, 1), (1, 0)])


def shifted(x, axis, by):
    n = lax.axis_size(axis)
    return lax.ppermute(x, axis, [(i, (i + by) % n) for i in range(n)])


def added(a, b):
    return (a.astype(jnp.float32) + b.astype(jnp.float32)).astype(a.dtype)


def ring_sum(parts, axis):
    n = lax.axis_size(axis)
    up = parts[n // 2]
    for k in range(n // 2 - 1, 0, -1):
        up = added(parts[k], shifted(up, axis, 1))
    up = shifted(up, axis, 1)
    down = parts[n // 2 + 1]
    for k in range(n // 2 + 2, n):
        down = added(parts[k], shifted(down, axis, -1))
    down = shifted(down, axis, -1)
    f32 = jnp.float32
    return parts[0].astype(f32) + up.astype(f32) + down.astype(f32)


def owner_at(me, core, ahead, y):
    n_z, my_z, my_y, my_core = me[0], me[1], me[2], me[3]
    return (lax.rem(my_z + ahead, n_z) * 2 + (my_y ^ y)) * 2 + (my_core ^ core)


vmem = pl.BlockSpec(memory_space=pltpu.VMEM)
smem = pl.BlockSpec(memory_space=pltpu.SMEM)


def call(kernel, out_shape, n_smem, operands, scratch, flops, limit=60):
    return pl.pallas_call(
        kernel,
        out_shape=tuple(jax.ShapeDtypeStruct(*o) for o in out_shape),
        in_specs=[smem] * n_smem + [vmem] * (len(operands) - n_smem),
        out_specs=(vmem,) * len(out_shape),
        scratch_shapes=scratch,
        compiler_params=pltpu.CompilerParams(vmem_limit_bytes=limit * 1024 * 1024),
        cost_estimate=pl.CostEstimate(flops=flops, bytes_accessed=4 << 20, transcendentals=0),
    )(*operands)


def pack_keys(lat, rope):
    tokens, latent = lat.shape
    half, width = tokens // 2, rope.shape[1]

    def kernel(lat_ref, rope_ref, out_ref):
        out_ref[:, :latent] = lat_ref[:half]
        out_ref[:, latent : 2 * latent] = lat_ref[half:]
        out_ref[:, 2 * latent :] = jnp.concatenate([rope_ref[:half], rope_ref[half:]], axis=1)

    shape = ((half, 2 * (latent + width)), lat.dtype)
    return call(kernel, [shape], 0, (lat, rope), [], 1000, 8)[0]


def prepare(me, queries, query_rope, outputs, grad_out, weight):
    rows, latent = queries.shape
    rope = query_rope.shape[1]
    tokens = grad_out.shape[0]
    heads = rows // tokens
    value = grad_out.shape[1] // heads
    wide = latent + 128
    f32, bf16 = jnp.float32, jnp.bfloat16
    n_dp, n_z = N_DP, N_CTX // 4
    each = latent // (n_dp * N_CTX)

    def kernel(me_ref, q_ref, qr_ref, out_ref, d_ref, w_ref, wide_ref, g_ref, delta_ref, v_ref,
               out_wide, g_wide, v_wide):
        wide_ref[:, :latent] = q_ref[...]
        wide_ref[:, latent:] = jnp.concatenate(
            [qr_ref[...], jnp.zeros((rows, wide - latent - rope), bf16)], axis=1
        )
        lanes = [slice(k, k + 128) for k in range(0, latent, 128)]
        for k, lane in enumerate(lanes):
            out_wide[k] = out_ref[:, lane].astype(f32)

        def head_step(h, carry):
            at = pl.ds(h, tokens, stride=heads)
            column = pl.ds(pl.multiple_of(h * value, value), value)
            d = d_ref[:, column]
            g = nt(d, w_ref[:, column])
            for k, lane in enumerate(lanes):
                g_wide[k, at, :] = g[:, lane]
                v_wide[pl.ds(h + k * 128 * heads, 128, stride=heads), :] = tn(
                    out_wide[k, at, :].astype(bf16), d
                )
            return carry

        lax.fori_loop(0, heads, head_step, 0)
        delta = jnp.zeros((rows, 128), f32)
        for k, lane in enumerate(lanes):
            g = g_wide[k].astype(bf16)
            g_ref[:, lane] = g
            delta += g.astype(f32) * out_wide[k]
        delta = jnp.sum(delta, axis=1, keepdims=True)
        delta = jnp.broadcast_to(delta, (rows, 128)).T[:1]
        delta_ref[0] = delta[:, : rows // 2]
        delta_ref[1] = delta[:, rows // 2 :]
        me = [me_ref[i] for i in range(4)]

        def slot_step(slot, carry):
            owner = owner_at(me, slot // (2 * n_z), slot // 2 % n_z, slot % 2)
            for r in range(each):
                parts = []
                for dp in range(n_dp):
                    row = ((dp * N_CTX + owner) * each + r) * heads
                    parts.append(v_wide[pl.ds(pl.multiple_of(row, heads), heads), :])
                v_ref[slot, :, r * value : (r + 1) * value] = jnp.concatenate(
                    parts, axis=0
                ).astype(bf16)
            return carry

        lax.fori_loop(0, N_CTX, slot_step, 0)

    return call(
        kernel,
        [
            ((rows, wide), bf16),
            ((rows, latent), bf16),
            ((2, 1, rows // 2), f32),
            ((N_CTX, n_dp * heads, each * value), bf16),
        ],
        1,
        (me, queries, query_rope, outputs, grad_out, weight),
        [
            pltpu.VMEM((latent // 128, rows, 128), f32),
            pltpu.VMEM((latent // 128, rows, 128), f32),
            pltpu.VMEM((latent * heads, value), f32),
        ],
        1000,
    )


def attention(me, blocks, pieces, items, queries, grads, delta, values):
    half, packed = pieces[0].shape[1:]
    rows, latent = grads.shape
    wide = queries.shape[1]
    cols = packed // 2
    rope = cols - latent
    count = 2 * N_CTX
    seq = count * half
    per, group = TILE // half, rows // 2
    heads = group // half
    f32, bf16 = jnp.float32, jnp.bfloat16
    n = len(pieces)
    extra = values.shape[2]
    n_z = N_CTX // 4

    def kernel(me_ref, blocks_ref, *refs):
        piece_refs, refs = refs[:n], refs[n:]
        q_ref, g_ref, delta_ref, v_ref, dq_ref, dqr_ref, near_ref, far_ref, *refs = refs
        keys_ref, table, scores, dk_acc, dq_acc = refs
        me = [me_ref[i] for i in range(4)]
        zero_pad = jnp.zeros((half, wide - cols), bf16)
        first = 0
        for ref, places in zip(piece_refs, items):
            for j, place in enumerate(places):
                table[first + j] = owner_at(me, *place)

            def sort_step(j, carry, ref=ref, first=first):
                owner = table[first + j]
                for side in range(2):
                    row = blocks_ref[2 * owner + side] * half
                    at = pl.ds(pl.multiple_of(row, half), half)
                    keys_ref[at, :latent] = ref[j, :, side * latent : (side + 1) * latent]
                    start = 2 * latent + side * rope
                    keys_ref[at, latent:] = jnp.concatenate(
                        [ref[j, :, start : start + rope], zero_pad], axis=1
                    )
                return carry

            lax.fori_loop(0, len(places), sort_step, 0)
            first += len(places)

        device = owner_at(me, 0, 0, 0)
        swap = (blocks_ref[2 * device + 1] > blocks_ref[2 * device]).astype(jnp.int32)
        top = jnp.maximum(blocks_ref[2 * device + 1], blocks_ref[2 * device]) // per

        def block_step(turn, carry):
            which = turn ^ swap
            block = blocks_ref[2 * device + which]
            base = pl.multiple_of(which * group, group)
            final = block // per

            def score_tile(t):
                at = pl.ds(pl.multiple_of(t * TILE, TILE), TILE)
                s = nt(keys_ref[at, :], q_ref[pl.ds(base, group), :])
                return s * (softmax_scale * log2e)

            def fold(t, s, m, l):
                scores[pl.ds(pl.multiple_of(t * TILE, TILE), TILE), :] = s
                new = jnp.maximum(m, jnp.max(s, axis=0, keepdims=True))
                l = l * jnp.exp2(m - new) + jnp.sum(jnp.exp2(s - new), axis=0, keepdims=True)
                return new, l

            begin = (jnp.full((1, group), -jnp.inf, f32), jnp.zeros((1, group), f32))
            m, l = lax.fori_loop(0, final, lambda t, c: fold(t, score_tile(t), *c), begin)
            ahead = block * half + lax.broadcasted_iota(jnp.int32, (1, group), 1) // heads
            row = lax.broadcasted_iota(jnp.int32, (TILE, group), 0)
            s = jnp.where(row <= ahead - final * TILE, score_tile(final), -jnp.inf)
            m, l = fold(final, s, m, l)
            log_total = m + jnp.log2(l)
            row_delta = delta_ref[which]
            dq_acc[...] = jnp.zeros((wide, group), f32)

            def tile_step(t, carry):
                at = pl.ds(pl.multiple_of(t * TILE, TILE), TILE)
                g = g_ref[pl.ds(base, group), :]
                p = jnp.exp2(scores[at, :] - log_total)
                dp = nt(keys_ref[at, :latent], g)
                ds = (p * (softmax_scale * (dp - row_delta))).astype(bf16)
                dk = nn(ds, q_ref[pl.ds(base, group), :])
                before = jnp.where(turn == 0, 0.0, dk_acc[at, :])
                dk_acc[at, :latent] = (
                    before[:, :latent] + dk[:, :latent] + nn(p.astype(bf16), g)
                )
                dk_acc[at, latent:] = before[:, latent:] + dk[:, latent:]
                dq_acc[...] += tn(keys_ref[at, :], ds)
                return carry

            lax.fori_loop(0, final + 1, tile_step, 0)
            done = dq_acc[...].T.astype(bf16)
            dq_ref[pl.ds(base, group), :] = done[:, :latent]
            dqr_ref[pl.ds(base, group), :] = done[:, latent:cols]
            return carry

        lax.fori_loop(0, 2, block_step, 0)

        def unsort_step(j, carry):
            for core, out in enumerate((near_ref, far_ref)):
                owner = owner_at(me, core, j // 2, j % 2)
                for side in range(2):
                    place = blocks_ref[2 * owner + side]
                    at = pl.ds(pl.multiple_of(place * half, half), half)
                    part = jnp.where(place // per <= top, dk_acc[at, :], 0.0).astype(bf16)
                    out[j, :, side * latent : (side + 1) * latent] = part[:, :latent]
                    start = 2 * latent + side * rope
                    out[j, :, start : start + rope] = part[:, latent:cols]
                out[j, :, packed:] = v_ref[core * 2 * n_z + j]
            return carry

        lax.fori_loop(0, 2 * n_z, unsort_step, 0)

    dk_shape = ((2 * n_z, half, packed + extra), bf16)
    return call(
        kernel,
        [((rows, latent), bf16), ((rows, rope), bf16), dk_shape, dk_shape],
        2,
        (me, blocks, *pieces, queries, grads, delta, values),
        [
            pltpu.VMEM((seq, wide), bf16),
            pltpu.SMEM((N_CTX,), jnp.int32),
            pltpu.VMEM((seq, group), f32),
            pltpu.VMEM((seq, wide), f32),
            pltpu.VMEM((wide, group), f32),
        ],
        5 * rows * seq * wide,
    )


def down_part(me, pieces, items, layer_input, latent, rope, heads):
    count, tokens, width = layer_input.shape
    half, packed = pieces[0].shape[1:]
    cols = latent + rope
    wide = latent + 128
    n = len(pieces)
    each = width // N_CTX
    room = -(-each // 16) * 16
    f32, bf16 = jnp.float32, jnp.bfloat16
    lanes = packed - 2 * cols
    n_x = N_DP // 2

    def kernel(me_ref, *refs):
        piece_refs, refs = refs[:n], refs[n:]
        x_ref, near_ref, far_ref, lat_ref, rope_ref, v_ref, joined, total, placed, v_total = refs
        me = [me_ref[i] for i in range(4)]
        my_x, my_hi = me_ref[4], me_ref[5]
        zero_pad = jnp.zeros((half, wide - cols), bf16)
        values = jnp.zeros((half, lanes), f32)
        for i, places in enumerate(items):
            for j, (ahead, hi) in enumerate(places):
                dp = (my_hi ^ hi) * n_x + lax.rem(my_x + ahead, n_x)
                values += piece_refs[i][j, :, 2 * cols :].astype(f32)
                for side in range(2):
                    at = pl.ds(pl.multiple_of(dp * tokens + side * half, half), half)
                    lat = piece_refs[i][j, :, side * latent : (side + 1) * latent]
                    start = 2 * latent + side * rope
                    rot = piece_refs[i][j, :, start : start + rope]
                    joined[at, :latent] = lat
                    joined[at, latent:] = jnp.concatenate([rot, zero_pad], axis=1)
                    if i == 0 and j == 0:
                        lat_ref[side * half : (side + 1) * half] = lat
                        rope_ref[side * half : (side + 1) * half] = rot
        v_total[...] = values
        mine = v_total[pl.ds(pl.multiple_of((my_hi * n_x + my_x) * heads, heads), heads), :]
        value = lanes // v_ref.shape[0]
        for r in range(v_ref.shape[0]):
            v_ref[r] = mine[:, r * value : (r + 1) * value]
        total[...] = tn(x_ref[...].reshape(count * tokens, width), joined[...])
        for c in range(N_CTX):
            placed[c, :each] = total[c * each : (c + 1) * each]
            if room > each:
                placed[c, each:] = jnp.zeros((room - each, wide), f32)

        def slot_step(slot, carry):
            for core, ref in enumerate((near_ref, far_ref)):
                owner = owner_at(me, core, slot // 2, slot % 2)
                ref[slot] = placed[owner, :, :cols].astype(bf16)
            return carry

        lax.fori_loop(0, N_CTX // 2, slot_step, 0)

    shape = ((N_CTX // 2, room, cols), bf16)
    return call(
        kernel,
        [
            shape,
            shape,
            ((tokens, latent), bf16),
            ((tokens, rope), bf16),
            ((lanes * half // (N_DP * heads * 128), heads, 128), f32),
        ],
        1,
        (me, *pieces, layer_input),
        [
            pltpu.VMEM((count * tokens, wide), bf16),
            pltpu.VMEM((width, wide), f32),
            pltpu.VMEM((N_CTX, room, wide), f32),
            pltpu.VMEM((half, lanes), f32),
        ],
        1000,
    )


def body(layer_input, kv_latent, key_rope, q_latent, q_rope, saved_output, w_uv, d_out, blocks):
    wide, bf16 = jnp.float32, jnp.bfloat16
    latent, rope = kv_latent.shape[2], key_rope.shape[2]
    heads = q_latent.shape[2]
    n_z = lax.axis_size("z")
    me = jnp.stack(
        [jnp.int32(n_z)] + [lax.axis_index(a) for a in ("z", "ylo", "core", "x", "yhi")]
    )

    mine = pack_keys(kv_latent[0], key_rope[0])
    ahead, behind = mine, mine
    groups, items, group, places = [], [], [], []
    for k in range(n_z // 2 + 1):
        if k:
            behind = shifted(behind, "z", 1)
            if k < n_z // 2:
                ahead = shifted(ahead, "z", -1)
        at_z = sorted({k, (n_z - k) % n_z})
        here = jnp.stack([ahead, behind][: len(at_z)] if k < n_z // 2 else [behind])
        there = swapped(here, "ylo")
        group += [here, there]
        places += [(z, y) for y in range(2) for z in at_z]
        if k in (n_z // 4, n_z // 2):
            groups.append(jnp.concatenate(group, axis=0))
            items.append(places)
            group, places = [], []
    pieces = groups + [swapped(x, "core") for x in groups]
    items = [[(core, *place) for place in p] for core in range(2) for p in items]

    queries, grads, delta, values = prepare(
        me,
        q_latent.reshape(-1, latent),
        q_rope.reshape(-1, rope),
        saved_output.reshape(-1, latent),
        d_out[0],
        w_uv,
    )
    d_q, d_qr, near_dk, far_dk = attention(
        me, blocks, pieces, items, queries, grads, delta, values
    )
    near_dk = near_dk.reshape(n_z, 2, *near_dk.shape[1:]).astype(wide)
    far_dk = swapped(far_dk, "core").reshape(near_dk.shape).astype(wide)
    summed = ring_sum([(near_dk[k] + far_dk[k]).astype(bf16) for k in range(n_z)], "z")
    summed = summed.astype(bf16)

    flipped = [(i, 3 - i) for i in range(4)]
    summed = jnp.stack(
        [
            added(summed[0], swapped(summed[1], "ylo")),
            added(swapped(summed[0], "yhi"), lax.ppermute(summed[1], ("yhi", "ylo"), flipped)),
        ]
    )

    n_x = lax.axis_size("x")
    after, before = shifted(summed, "x", -1), shifted(summed, "x", 1)
    opposite = [shifted(before[:1], "x", 1), shifted(after[1:], "x", -1)]
    dp_pieces = [summed, after, before] + opposite
    dp_items = [[(k, hi) for hi in range(2)] for k in (0, 1, n_x - 1)] + [[(2, 0)], [(2, 1)]]
    near_part, far_part, d_lat, d_rope, grad_uv = down_part(
        me, dp_pieces, dp_items, layer_input, latent, rope, heads
    )
    parts = (near_part.astype(wide) + swapped(far_part, "core").astype(wide)).astype(bf16)
    parts = parts.reshape(n_z, 2, *parts.shape[1:])
    part = ring_sum([parts[k] for k in range(n_z)], "z")
    grad_down = part[0] + swapped(part[1].astype(bf16), "ylo").astype(wide)
    return (
        d_q.reshape(q_latent.shape),
        d_qr.reshape(q_rope.shape),
        d_lat[None],
        d_rope[None],
        grad_down[: layer_input.shape[2] // N_CTX],
        grad_uv.reshape(-1, w_uv.shape[1]),
    )


DP = ("yhi", "x")
CTX = ("z", "ylo", "core")


def solution(mesh):
    n_dp, n_ctx = mesh.shape["dp"], mesh.shape["ctx"]
    fine = Mesh(mesh.devices.reshape(2, n_dp // 2, n_ctx // 4, 2, 2), DP + CTX)
    in_specs = (
        P(None, CTX, DP),
        P(DP, CTX, None),
        P(DP, CTX, None),
        P(DP, CTX, None, None),
        P(DP, CTX, None, None),
        P(DP, CTX, None, None),
        P(),
        P(DP, CTX, None),
        P(),
    )
    out_specs = (
        P(DP, CTX, None, None),
        P(DP, CTX, None, None),
        P(DP, CTX, None),
        P(DP, CTX, None),
        P(DP + CTX, None),
        P(DP + CTX, None),
    )

    return jax.shard_map(body, mesh=fine, in_specs=in_specs, out_specs=out_specs, check_vma=False)
```

time: 263 us -> 236 us (0.90)
  Pallas kernels: 66.8 us -> 36.4 us
  waiting for transfers between devices: 117 us -> 104 us
  starting transfers between devices: 66.6 us -> 78.3 us
  other arithmetic: 3.26 us -> 6.1 us
    pallas_call x9 -> x4, Pallas kernels: 66.8 us -> 36.4 us  [call(): pl.pallas_call(kernel, out_shape=tuple((jax.ShapeDtypeStruct(*o) for o in...]
    ppermute x24 -> x25, starting transfers between devices: 38.4 us -> 49.4 us  [shifted(): return lax.ppermute(x, axis, [(i, (i + by) % n) for i in range(n)])]
    ppermute x24 -> x25, waiting for transfers between devices: 97.5 us -> 87 us  [shifted(): return lax.ppermute(x, axis, [(i, (i + by) % n) for i in range(n)])]
    ppermute x12, waiting for transfers between devices: 20 us -> 16.5 us  [swapped(): return lax.ppermute(x, axis, [(0, 1), (1, 0)])]
    convert_element_type x4, other arithmetic: 0.37 us -> 3.23 us  [the longest x1 2.42 us: body(): near_dk = near_dk.reshape(n_z, 2, *near_dk.shape[1:]).astype(wide)]
    unnamed x45 -> x42, local copies, waits for them, and re-layouts: 6.53 us -> 7.24 us
  transfers between devices with their start and end apart: 36 -> 38, of which waited for: 23 -> 25; matrix products, arithmetic and copies ran while one was open for 2% -> 3% of each run, Pallas kernels for 17% -> 3%
where the time goes in v1:
time: 236 us; the launch traced here: 234 us
  waiting for transfers between devices  104 us (44%)
  starting transfers between devices  78.3 us (33%)
  Pallas kernels  36.4 us (15%)
  local copies, waits for them, and re-layouts  7.97 us (3%)
  other arithmetic  6.1 us (3%)
    ppermute x25, waiting for transfers between devices, shifted(): return lax.ppermute(x, axis, [(i, (i + by) % n) for i in range(n)])  87 us
    ppermute x25, starting transfers between devices, shifted(): return lax.ppermute(x, axis, [(i, (i + by) % n) for i in range(n)])  49.4 us
    pallas_call x4, Pallas kernels, call(): pl.pallas_call(kernel, out_shape=tuple((jax.ShapeDtypeStruct(*o) for o in...  36.4 us
    ppermute x12, starting transfers between devices, swapped(): return lax.ppermute(x, axis, [(0, 1), (1, 0)])  28.9 us
    ppermute x12, waiting for transfers between devices, swapped(): return lax.ppermute(x, axis, [(0, 1), (1, 0)])  16.5 us
    unnamed x42, local copies, waits for them, and re-layouts  7.24 us
  transfers between devices with their start and end apart: 38, of which 25 were waited for; matrix products, arithmetic and copies ran while one was open for 3% of the time, Pallas kernels for 3%

profile of v1, /device:TPU:16, one launch (start us, length us, event | category | flops | bytes accessed | tf_op | source)
XLA Modules:
  0.0 233.7 jit_solution(3304272298304775914)
XLA Ops:
  0.6 0.8 copy.15
  1.5 0.9 copy-done
  2.4 1.9 collective-permute-start.2
  4.4 4.0 %collective-permute-start.1 = (bf16[64,1152]{1,0:T(8,128)(2,1)S(1)}, bf16[64,1152]{1,0:T(8,128)(2,1)S(1)}, u32[]{:S(2)}, u32[]{:S(2)}) collective-permute-start(bf16[64,1152]{1,0:T(8,128)(2,1)S(1)} %shard_map.136), channel_id=1, source_target_pairs={{0,28},{4,0},{8,4},{12,8},{16,12},{20,16},{24,20},{28,24},{1,29},{... | collective-permute-start | bytes 442376 | tf_op jit(solution)/shard_map/ppermute | solution.py:36
  8.4 1.3 collective-permute-start
  9.7 2.5 %collective-permute-done.2 = bf16[64,1152]{1,0:T(8,128)(2,1)S(1)} collective-permute-done((bf16[64,1152]{1,0:T(8,128)(2,1)S(1)}, bf16[64,1152]{1,0:T(8,128)(2,1)S(1)}, u32[]{:S(2)}, u32[]{:S(2)}) %collective-permute-start.2) | collective-permute-done | bytes 147488 | tf_op jit(solution)/shard_map/ppermute | solution.py:36
  12.2 1.4 collective-permute-start.3
  13.6 3.2 %collective-permute-start.4 = (bf16[64,1152]{1,0:T(8,128)(2,1)S(1)}, bf16[64,1152]{1,0:T(8,128)(2,1)S(1)}, u32[]{:S(2)}, u32[]{:S(2)}) collective-permute-start(bf16[64,1152]{1,0:T(8,128)(2,1)S(1)} %collective-permute-done.1), channel_id=1, source_target_pairs={{0,28},{4,0},{8,4},{12,8},{16,12},{20,16},{24,20},{28,24},{1,29},{... | collective-permute-start | bytes 442376 | tf_op jit(solution)/shard_map/ppermute | solution.py:36
  16.9 3.0 %collective-permute-done.5 = bf16[64,1152]{1,0:T(8,128)(2,1)S(1)} collective-permute-done((bf16[64,1152]{1,0:T(8,128)(2,1)S(1)}, bf16[64,1152]{1,0:T(8,128)(2,1)S(1)}, u32[]{:S(2)}, u32[]{:S(2)}) %collective-permute-start.5) | collective-permute-done | bytes 147488 | tf_op jit(solution)/shard_map/ppermute | solution.py:36
  19.9 3.2 %collective-permute-start.7 = (bf16[64,1152]{1,0:T(8,128)(2,1)S(1)}, bf16[64,1152]{1,0:T(8,128)(2,1)S(1)}, u32[]{:S(2)}, u32[]{:S(2)}) collective-permute-start(bf16[64,1152]{1,0:T(8,128)(2,1)S(1)} %collective-permute-done.4), channel_id=1, source_target_pairs={{0,28},{4,0},{8,4},{12,8},{16,12},{20,16},{24,20},{28,24},{1,29},{... | collective-permute-start | bytes 442376 | tf_op jit(solution)/shard_map/ppermute | solution.py:36
  23.2 0.8 collective-permute-start.6
  24.0 2.2 collective-permute-done.8
  26.3 0.8 collective-permute-start.9
  27.2 1.4 collective-permute-start.10
  28.7 4.8 %collective-permute-done.10 = bf16[64,1152]{1,0:T(8,128)(2,1)S(1)} collective-permute-done((bf16[64,1152]{1,0:T(8,128)(2,1)S(1)}, bf16[64,1152]{1,0:T(8,128)(2,1)S(1)}, u32[]{:S(2)}, u32[]{:S(2)}) %collective-permute-start.10) | collective-permute-done | bytes 147488 | tf_op jit(solution)/shard_map/ppermute | solution.py:36
  33.5 1.3 collective-permute-start.11
  35.0 2.4 %collective-permute-done.9 = bf16[2,64,1152]{2,1,0:T(8,128)(2,1)S(1)} collective-permute-done((bf16[2,64,1152]{2,1,0:T(8,128)(2,1)S(1)}, bf16[2,64,1152]{2,1,0:T(8,128)(2,1)S(1)}, u32[]{:S(2)}, u32[]{:S(2)}) %collective-permute-start.9) | collective-permute-done | bytes 294944 | tf_op jit(solution)/shard_map/ppermute | solution.py:31
  37.4 1.5 collective-permute-done.11
  39.3 0.9 copy.16
  40.8 8.2 %shard_map.137 = (bf16[1024,640]{1,0:T(8,128)(2,1)}, bf16[1024,512]{1,0:T(8,128)(2,1)}, f32[2,1,512]{2,1,0:T(1,128)}, bf16[32,64,256]{2,1,0:T(8,128)(2,1)}) custom-call(s32[6]{0:T(128)} %stack.65.me_ref, bf16[1024,512]{1,0:T(8,128)(2,1)} %bitcast.52, bf16[1024,64]{1,0:T(8,128)(2,1)} %bitcast.54, bf16[1024,512]{1,0:T(8,128)(2,1)} %bitcast.53, ...), custom_call_target="tpu_custom_call" | custom-call | flops 1000 | bytes 4194304 | tf_op jit(solution)/shard_map/pallas_call | solution.py:67
  49.0 0.9 copy-done.12
  49.9 22.8 %shard_map.138 = (bf16[1024,512]{1,0:T(8,128)(2,1)}, bf16[1024,64]{1,0:T(8,128)(2,1)}, bf16[16,64,1408]{2,1,0:T(8,128)(2,1)}, bf16[16,64,1408]{2,1,0:T(8,128)(2,1)}) custom-call(s32[6]{0:T(128)} %stack.65.me_ref, s32[64]{0:T(128)} %blocks_ref.1, bf16[10,64,1152]{2,1,0:T(8,128)(2,1)} %copy-done.10, bf16[6,64,1152]{2,1,0:T(8,128)(2,1)} %copy-done.9, ...), custom_call_target="tpu_custom_call" | custom-call | flops 13421772800 | bytes 4194304 | tf_op jit(solution)/shard_map/pallas_call | solution.py:67
  72.7 13.6 %collective-permute-start.14 = (bf16[16,64,1408]{2,1,0:T(8,128)(2,1)}, bf16[16,64,1408]{2,1,0:T(8,128)(2,1)S(1)}, u32[]{:S(2)}, u32[]{:S(2)}) collective-permute-start(bf16[16,64,1408]{2,1,0:T(8,128)(2,1)} %get-tuple-element.26), channel_id=1, source_target_pairs={{0,1},{1,0},{2,3},{3,2},{4,5},{5,4},{6,7},{7,6},{8,9},{9,8},{10,11... | collective-permute-start | bytes 8650760 | tf_op jit(solution)/shard_map/ppermute | solution.py:31
  86.3 2.4 %convert_element_type.205 = f32[16,64,1408]{2,1,0:T(8,128)S(1)} convert(bf16[16,64,1408]{2,1,0:T(8,128)(2,1)} %get-tuple-element.25) | non-fusion elementwise | flops 1441792 | bytes 8650752 | tf_op jit(solution)/shard_map/convert_element_type | solution.py:410
  88.7 2.7 %collective-permute-done.14 = bf16[16,64,1408]{2,1,0:T(8,128)(2,1)S(1)} collective-permute-done((bf16[16,64,1408]{2,1,0:T(8,128)(2,1)}, bf16[16,64,1408]{2,1,0:T(8,128)(2,1)S(1)}, u32[]{:S(2)}, u32[]{:S(2)}) %collective-permute-start.14) | collective-permute-done | bytes 2883616 | tf_op jit(solution)/shard_map/ppermute | solution.py:31
  91.4 0.6 convert_element_type.206
  92.2 11.9 %collective-permute-done.15 = bf16[2,64,1408]{2,1,0:T(8,128)(2,1)S(1)} collective-permute-done((bf16[2,64,1408]{2,1,0:T(8,128)(2,1)S(1)}, bf16[2,64,1408]{2,1,0:T(8,128)(2,1)S(1)}, u32[]{:S(2)}, u32[]{:S(2)}) %collective-permute-start.15) | collective-permute-done | bytes 360480 | tf_op jit(solution)/shard_map/ppermute | solution.py:36
  104.2 5.6 %collective-permute-start.16 = (bf16[2,64,1408]{2,1,0:T(8,128)(2,1)S(1)}, bf16[2,64,1408]{2,1,0:T(8,128)(2,1)S(1)}, u32[]{:S(2)}, u32[]{:S(2)}) collective-permute-start(bf16[2,64,1408]{2,1,0:T(8,128)(2,1)S(1)} %add_convert_fusion.6), channel_id=1, source_target_pairs={{0,4},{4,8},{8,12},{12,16},{16,20},{20,24},{24,28},{28,0},{1,5},{5... | collective-permute-start | bytes 1081352 | tf_op jit(solution)/shard_map/ppermute | solution.py:36
  109.8 8.7 %collective-permute-done.16 = bf16[2,64,1408]{2,1,0:T(8,128)(2,1)S(1)} collective-permute-done((bf16[2,64,1408]{2,1,0:T(8,128)(2,1)S(1)}, bf16[2,64,1408]{2,1,0:T(8,128)(2,1)S(1)}, u32[]{:S(2)}, u32[]{:S(2)}) %collective-permute-start.16) | collective-permute-done | bytes 360480 | tf_op jit(solution)/shard_map/ppermute | solution.py:36
  118.6 7.9 %collective-permute-start.17 = (bf16[2,64,1408]{2,1,0:T(8,128)(2,1)S(1)}, bf16[2,64,1408]{2,1,0:T(8,128)(2,1)S(1)}, u32[]{:S(2)}, u32[]{:S(2)}) collective-permute-start(bf16[2,64,1408]{2,1,0:T(8,128)(2,1)S(1)} %add_convert_fusion.5), channel_id=1, source_target_pairs={{0,4},{4,8},{8,12},{12,16},{16,20},{20,24},{24,28},{28,0},{1,5},{5... | collective-permute-start | bytes 1081352 | tf_op jit(solution)/shard_map/ppermute | solution.py:36
  126.5 6.3 %collective-permute-done.17 = bf16[2,64,1408]{2,1,0:T(8,128)(2,1)S(1)} collective-permute-done((bf16[2,64,1408]{2,1,0:T(8,128)(2,1)S(1)}, bf16[2,64,1408]{2,1,0:T(8,128)(2,1)S(1)}, u32[]{:S(2)}, u32[]{:S(2)}) %collective-permute-start.17) | collective-permute-done | bytes 360480 | tf_op jit(solution)/shard_map/ppermute | solution.py:36
  133.1 8.6 %collective-permute-done.19 = bf16[2,64,1408]{2,1,0:T(8,128)(2,1)S(1)} collective-permute-done((bf16[2,64,1408]{2,1,0:T(8,128)(2,1)S(1)}, bf16[2,64,1408]{2,1,0:T(8,128)(2,1)S(1)}, u32[]{:S(2)}, u32[]{:S(2)}) %collective-permute-start.19) | collective-permute-done | bytes 360480 | tf_op jit(solution)/shard_map/ppermute | solution.py:36
  141.8 4.0 %collective-permute-start.20 = (bf16[2,64,1408]{2,1,0:T(8,128)(2,1)S(1)}, bf16[2,64,1408]{2,1,0:T(8,128)(2,1)S(1)}, u32[]{:S(2)}, u32[]{:S(2)}) collective-permute-start(bf16[2,64,1408]{2,1,0:T(8,128)(2,1)S(1)} %add_convert_fusion.3), channel_id=1, source_target_pairs={{0,28},{4,0},{8,4},{12,8},{16,12},{20,16},{24,20},{28,24},{1,29},{... | collective-permute-start | bytes 1081352 | tf_op jit(solution)/shard_map/ppermute | solution.py:36
  145.8 5.4 %collective-permute-done.20 = bf16[2,64,1408]{2,1,0:T(8,128)(2,1)S(1)} collective-permute-done((bf16[2,64,1408]{2,1,0:T(8,128)(2,1)S(1)}, bf16[2,64,1408]{2,1,0:T(8,128)(2,1)S(1)}, u32[]{:S(2)}, u32[]{:S(2)}) %collective-permute-start.20) | collective-permute-done | bytes 360480 | tf_op jit(solution)/shard_map/ppermute | solution.py:36
  151.3 3.8 %collective-permute-start.21 = (bf16[2,64,1408]{2,1,0:T(8,128)(2,1)S(1)}, bf16[2,64,1408]{2,1,0:T(8,128)(2,1)S(1)}, u32[]{:S(2)}, u32[]{:S(2)}) collective-permute-start(bf16[2,64,1408]{2,1,0:T(8,128)(2,1)S(1)} %add_convert_fusion.2), channel_id=1, source_target_pairs={{0,28},{4,0},{8,4},{12,8},{16,12},{20,16},{24,20},{28,24},{1,29},{... | collective-permute-start | bytes 1081352 | tf_op jit(solution)/shard_map/ppermute | solution.py:36
  155.0 4.9 %collective-permute-done.21 = bf16[2,64,1408]{2,1,0:T(8,128)(2,1)S(1)} collective-permute-done((bf16[2,64,1408]{2,1,0:T(8,128)(2,1)S(1)}, bf16[2,64,1408]{2,1,0:T(8,128)(2,1)S(1)}, u32[]{:S(2)}, u32[]{:S(2)}) %collective-permute-start.21) | collective-permute-done | bytes 360480 | tf_op jit(solution)/shard_map/ppermute | solution.py:36
  160.1 5.8 %collective-permute-start.22 = (bf16[64,1408]{1,0:T(8,128)(2,1)S(1)}, bf16[64,1408]{1,0:T(8,128)(2,1)S(1)}, u32[]{:S(2)}, u32[]{:S(2)}) collective-permute-start(bf16[64,1408]{1,0:T(8,128)(2,1)S(1)} %get-tuple-element.45), channel_id=1, source_target_pairs={{0,2},{2,0},{1,3},{3,1},{4,6},{6,4},{5,7},{7,5},{8,10},{10,8},{9,1... | collective-permute-start | bytes 540680 | tf_op jit(solution)/shard_map/ppermute | solution.py:31
  165.9 2.2 collective-permute-start.23
  168.1 1.9 collective-permute-done.22
  170.0 3.0 %collective-permute-done.23 = bf16[64,1408]{1,0:T(8,128)(2,1)S(1)} collective-permute-done((bf16[64,1408]{1,0:T(8,128)(2,1)S(1)}, bf16[64,1408]{1,0:T(8,128)(2,1)S(1)}, u32[]{:S(2)}, u32[]{:S(2)}) %collective-permute-start.23) | collective-permute-done | bytes 180256 | tf_op jit(solution)/shard_map/ppermute | solution.py:31
  173.4 1.6 collective-permute-start.26
  175.0 1.7 collective-permute-start.25
  176.7 7.3 %collective-permute-done.26.refs_2_ = bf16[2,64,1408]{2,1,0:T(8,128)(2,1)S(1)} collective-permute-done((bf16[2,64,1408]{2,1,0:T(8,128)(2,1)S(1)}, bf16[2,64,1408]{2,1,0:T(8,128)(2,1)S(1)}, u32[]{:S(2)}, u32[]{:S(2)}) %collective-permute-start.26) | collective-permute-done | bytes 360480 | tf_op jit(solution)/shard_map/ppermute | solution.py:36
  184.5 3.0 %collective-permute-start.28 = (bf16[1,64,1408]{2,1,0:T(8,128)(2,1)S(1)}, bf16[1,64,1408]{2,1,0:T(8,128)(2,1)S(1)}, u32[]{:S(2)}, u32[]{:S(2)}) collective-permute-start(bf16[1,64,1408]{2,1,0:T(8,128)(2,1)S(1)} %slice.170), channel_id=1, source_target_pairs={{0,96},{32,0},{64,32},{96,64},{1,97},{33,1},{65,33},{97,65},{2,98}... | collective-permute-start | bytes 540680 | tf_op jit(solution)/shard_map/ppermute | solution.py:36
  187.5 3.4 %collective-permute-done.27.refs_3_ = bf16[1,64,1408]{2,1,0:T(8,128)(2,1)S(1)} collective-permute-done((bf16[1,64,1408]{2,1,0:T(8,128)(2,1)S(1)}, bf16[1,64,1408]{2,1,0:T(8,128)(2,1)S(1)}, u32[]{:S(2)}, u32[]{:S(2)}) %collective-permute-start.27) | collective-permute-done | bytes 180256 | tf_op jit(solution)/shard_map/ppermute | solution.py:36
  190.9 0.6 copy-done.5
  191.6 0.7 copy-done.6
  192.2 5.4 %shard_map.139 = (bf16[16,32,576]{2,1,0:T(8,128)(2,1)}, bf16[16,32,576]{2,1,0:T(8,128)(2,1)}, bf16[128,512]{1,0:T(8,128)(2,1)}, bf16[128,64]{1,0:T(8,128)(2,1)}, f32[2,8,128]{2,1,0:T(8,128)}) custom-call(s32[6]{0:T(128)} %stack.65.me_ref, bf16[2,64,1408]{2,1,0:T(8,128)(2,1)} %copy-done.1, bf16[2,64,1408]{2,1,0:T(8,128)(2,1)} %copy-done.3, ...), custom_call_target="tpu_custom_call" | custom-call | flops 1000 | bytes 4194304 | tf_op jit(solution)/shard_map/pallas_call | solution.py:67
  197.6 2.3 collective-permute-done.29
  199.9 1.3 add_convert_fusion
  201.2 1.3 collective-permute-start.30
  202.5 5.3 %collective-permute-done.30 = bf16[2,32,576]{2,1,0:T(8,128)(2,1)S(1)} collective-permute-done((bf16[2,32,576]{2,1,0:T(8,128)(2,1)S(1)}, bf16[2,32,576]{2,1,0:T(8,128)(2,1)S(1)}, u32[]{:S(2)}, u32[]{:S(2)}) %collective-permute-start.30) | collective-permute-done | bytes 73760 | tf_op jit(solution)/shard_map/ppermute | solution.py:36
  207.8 3.2 %collective-permute-start.34 = (bf16[2,32,576]{2,1,0:T(8,128)(2,1)S(1)}, bf16[2,32,576]{2,1,0:T(8,128)(2,1)S(1)}, u32[]{:S(2)}, u32[]{:S(2)}) collective-permute-start(bf16[2,32,576]{2,1,0:T(8,128)(2,1)S(1)} %get-tuple-element.43), channel_id=1, source_target_pairs={{0,28},{4,0},{8,4},{12,8},{16,12},{20,16},{24,20},{28,24},{1,29},{... | collective-permute-start | bytes 221192 | tf_op jit(solution)/shard_map/ppermute | solution.py:36
  211.1 2.4 %collective-permute-done.31 = bf16[2,32,576]{2,1,0:T(8,128)(2,1)S(1)} collective-permute-done((bf16[2,32,576]{2,1,0:T(8,128)(2,1)S(1)}, bf16[2,32,576]{2,1,0:T(8,128)(2,1)S(1)}, u32[]{:S(2)}, u32[]{:S(2)}) %collective-permute-start.31) | collective-permute-done | bytes 73760 | tf_op jit(solution)/shard_map/ppermute | solution.py:36
  213.6 5.6 %collective-permute-done.32 = bf16[2,32,576]{2,1,0:T(8,128)(2,1)S(1)} collective-permute-done((bf16[2,32,576]{2,1,0:T(8,128)(2,1)S(1)}, bf16[2,32,576]{2,1,0:T(8,128)(2,1)S(1)}, u32[]{:S(2)}, u32[]{:S(2)}) %collective-permute-start.32) | collective-permute-done | bytes 73760 | tf_op jit(solution)/shard_map/ppermute | solution.py:36
  219.4 2.0 collective-permute-start.33
  221.4 3.0 %collective-permute-done.35 = bf16[2,32,576]{2,1,0:T(8,128)(2,1)S(1)} collective-permute-done((bf16[2,32,576]{2,1,0:T(8,128)(2,1)S(1)}, bf16[2,32,576]{2,1,0:T(8,128)(2,1)S(1)}, u32[]{:S(2)}, u32[]{:S(2)}) %collective-permute-start.35) | collective-permute-done | bytes 73760 | tf_op jit(solution)/shard_map/ppermute | solution.py:36
  224.4 0.7 collective-permute-start.36
  225.1 0.8 copy.17
  226.0 0.7 copy.18
  227.3 1.6 collective-permute-done.36
  229.0 1.5 collective-permute-start.37
  230.5 2.6 %collective-permute-done.37 = bf16[32,576]{1,0:T(8,128)(2,1)S(1)} collective-permute-done((bf16[32,576]{1,0:T(8,128)(2,1)S(1)}, bf16[32,576]{1,0:T(8,128)(2,1)S(1)}, u32[]{:S(2)}, u32[]{:S(2)}) %collective-permute-start.37) | collective-permute-done | bytes 36896 | tf_op jit(solution)/shard_map/ppermute | solution.py:31
  233.1 0.6 slice_add_fusion.8
  (89 shorter events, 4.4 us)
Async XLA Ops:
  1.5 0.9 copy-start
  2.4 9.7 %collective-permute-start.2 = (bf16[64,1152]{1,0:T(8,128)(2,1)S(1)}, bf16[64,1152]{1,0:T(8,128)(2,1)S(1)}, u32[]{:S(2)}, u32[]{:S(2)}) collective-permute-start(bf16[64,1152]{1,0:T(8,128)(2,1)S(1)} %shard_map.136), channel_id=1, source_target_pairs={{0,4},{4,8},{8,12},{12,16},{16,20},{20,24},{24,28},{28,0},{1,5},{5... | collective-permute-start | bytes 442376 | tf_op jit(solution)/shard_map/ppermute | solution.py:36
  4.4 7.8 %collective-permute-start.1 = (bf16[64,1152]{1,0:T(8,128)(2,1)S(1)}, bf16[64,1152]{1,0:T(8,128)(2,1)S(1)}, u32[]{:S(2)}, u32[]{:S(2)}) collective-permute-start(bf16[64,1152]{1,0:T(8,128)(2,1)S(1)} %shard_map.136), channel_id=1, source_target_pairs={{0,28},{4,0},{8,4},{12,8},{16,12},{20,16},{24,20},{28,24},{1,29},{... | collective-permute-start | bytes 442376 | tf_op jit(solution)/shard_map/ppermute | solution.py:36
  8.4 8.4 %collective-permute-start = (bf16[1,64,1152]{2,1,0:T(8,128)(2,1)S(1)}, bf16[1,64,1152]{2,1,0:T(8,128)(2,1)S(1)}, u32[]{:S(2)}, u32[]{:S(2)}) collective-permute-start(bf16[1,64,1152]{2,1,0:T(8,128)(2,1)S(1)} %bitcast.49), channel_id=1, source_target_pairs={{0,2},{2,0},{1,3},{3,1},{4,6},{6,4},{5,7},{7,5},{8,10},{10,8},{9,1... | collective-permute-start | bytes 442376 | tf_op jit(solution)/shard_map/ppermute | solution.py:31
  12.2 16.4 %collective-permute-start.3 = (bf16[2,64,1152]{2,1,0:T(8,128)(2,1)S(1)}, bf16[2,64,1152]{2,1,0:T(8,128)(2,1)S(1)}, u32[]{:S(2)}, u32[]{:S(2)}) collective-permute-start(bf16[2,64,1152]{2,1,0:T(8,128)(2,1)S(1)} %pad_maximum_fusion.1), channel_id=1, source_target_pairs={{0,2},{2,0},{1,3},{3,1},{4,6},{6,4},{5,7},{7,5},{8,10},{10,8},{9,1... | collective-permute-start | bytes 884744 | tf_op jit(solution)/shard_map/ppermute | solution.py:31
  13.6 6.4 %collective-permute-start.5 = (bf16[64,1152]{1,0:T(8,128)(2,1)S(1)}, bf16[64,1152]{1,0:T(8,128)(2,1)S(1)}, u32[]{:S(2)}, u32[]{:S(2)}) collective-permute-start(bf16[64,1152]{1,0:T(8,128)(2,1)S(1)} %collective-permute-done.2), channel_id=1, source_target_pairs={{0,4},{4,8},{8,12},{12,16},{16,20},{20,24},{24,28},{28,0},{1,5},{5... | collective-permute-start | bytes 442376 | tf_op jit(solution)/shard_map/ppermute | solution.py:36
  13.6 6.4 %collective-permute-start.4 = (bf16[64,1152]{1,0:T(8,128)(2,1)S(1)}, bf16[64,1152]{1,0:T(8,128)(2,1)S(1)}, u32[]{:S(2)}, u32[]{:S(2)}) collective-permute-start(bf16[64,1152]{1,0:T(8,128)(2,1)S(1)} %collective-permute-done.1), channel_id=1, source_target_pairs={{0,28},{4,0},{8,4},{12,8},{16,12},{20,16},{24,20},{28,24},{1,29},{... | collective-permute-start | bytes 442376 | tf_op jit(solution)/shard_map/ppermute | solution.py:36
  19.9 6.4 %collective-permute-start.8 = (bf16[64,1152]{1,0:T(8,128)(2,1)S(1)}, bf16[64,1152]{1,0:T(8,128)(2,1)S(1)}, u32[]{:S(2)}, u32[]{:S(2)}) collective-permute-start(bf16[64,1152]{1,0:T(8,128)(2,1)S(1)} %collective-permute-done.5), channel_id=1, source_target_pairs={{0,4},{4,8},{8,12},{12,16},{16,20},{20,24},{24,28},{28,0},{1,5},{5... | collective-permute-start | bytes 442376 | tf_op jit(solution)/shard_map/ppermute | solution.py:36
  19.9 6.4 %collective-permute-start.7 = (bf16[64,1152]{1,0:T(8,128)(2,1)S(1)}, bf16[64,1152]{1,0:T(8,128)(2,1)S(1)}, u32[]{:S(2)}, u32[]{:S(2)}) collective-permute-start(bf16[64,1152]{1,0:T(8,128)(2,1)S(1)} %collective-permute-done.4), channel_id=1, source_target_pairs={{0,28},{4,0},{8,4},{12,8},{16,12},{20,16},{24,20},{28,24},{1,29},{... | collective-permute-start | bytes 442376 | tf_op jit(solution)/shard_map/ppermute | solution.py:36
  23.2 11.6 %collective-permute-start.6 = (bf16[2,64,1152]{2,1,0:T(8,128)(2,1)S(1)}, bf16[2,64,1152]{2,1,0:T(8,128)(2,1)S(1)}, u32[]{:S(2)}, u32[]{:S(2)}) collective-permute-start(bf16[2,64,1152]{2,1,0:T(8,128)(2,1)S(1)} %pad_maximum_fusion.2), channel_id=1, source_target_pairs={{0,2},{2,0},{1,3},{3,1},{4,6},{6,4},{5,7},{7,5},{8,10},{10,8},{9,1... | collective-permute-start | bytes 884744 | tf_op jit(solution)/shard_map/ppermute | solution.py:31
  26.3 11.1 %collective-permute-start.9 = (bf16[2,64,1152]{2,1,0:T(8,128)(2,1)S(1)}, bf16[2,64,1152]{2,1,0:T(8,128)(2,1)S(1)}, u32[]{:S(2)}, u32[]{:S(2)}) collective-permute-start(bf16[2,64,1152]{2,1,0:T(8,128)(2,1)S(1)} %pad_maximum_fusion.3), channel_id=1, source_target_pairs={{0,2},{2,0},{1,3},{3,1},{4,6},{6,4},{5,7},{7,5},{8,10},{10,8},{9,1... | collective-permute-start | bytes 884744 | tf_op jit(solution)/shard_map/ppermute | solution.py:31
  27.2 6.4 %collective-permute-start.10 = (bf16[64,1152]{1,0:T(8,128)(2,1)S(1)}, bf16[64,1152]{1,0:T(8,128)(2,1)S(1)}, u32[]{:S(2)}, u32[]{:S(2)}) collective-permute-start(bf16[64,1152]{1,0:T(8,128)(2,1)S(1)} %collective-permute-done.8), channel_id=1, source_target_pairs={{0,4},{4,8},{8,12},{12,16},{16,20},{20,24},{24,28},{28,0},{1,5},{5... | collective-permute-start | bytes 442376 | tf_op jit(solution)/shard_map/ppermute | solution.py:36
  28.6 10.7 %copy-start.7 = (bf16[1,128,8,64]{1,3,2,0:T(8,128)(2,1)S(1)}, bf16[1,128,8,64]{1,3,2,0:T(8,128)(2,1)}, u32[]{:S(2)}) copy-start(bf16[1,128,8,64]{1,3,2,0:T(8,128)(2,1)} %param.13) | copy-start | bytes 393220
  33.5 5.4 %collective-permute-start.11 = (bf16[1,64,1152]{2,1,0:T(8,128)(2,1)S(1)}, bf16[1,64,1152]{2,1,0:T(8,128)(2,1)S(1)}, u32[]{:S(2)}, u32[]{:S(2)}) collective-permute-start(bf16[1,64,1152]{2,1,0:T(8,128)(2,1)S(1)} %bitcast.63), channel_id=1, source_target_pairs={{0,2},{2,0},{1,3},{3,1},{4,6},{6,4},{5,7},{7,5},{8,10},{10,8},{9,1... | collective-permute-start | bytes 442376 | tf_op jit(solution)/shard_map/ppermute | solution.py:31
  34.8 14.1 %copy-start.10 = (bf16[10,64,1152]{2,1,0:T(8,128)(2,1)}, bf16[10,64,1152]{2,1,0:T(8,128)(2,1)S(1)}, u32[]{:S(2)}) copy-start(bf16[10,64,1152]{2,1,0:T(8,128)(2,1)S(1)} %constant_dynamic-update-slice_fusion.refs_0_) | copy-start | bytes 4423684
  34.8 14.1 %collective-permute-start.12 = (bf16[10,64,1152]{2,1,0:T(8,128)(2,1)S(1)}, bf16[10,64,1152]{2,1,0:T(8,128)(2,1)}, u32[]{:S(2)}, u32[]{:S(2)}) collective-permute-start(bf16[10,64,1152]{2,1,0:T(8,128)(2,1)S(1)} %constant_dynamic-update-slice_fusion.refs_0_), channel_id=1, source_target_pairs={{0,1},{1,0},{2,3},{3,2},{4,5},{5,4},{6,7},{7,6},{8,9},{9,8},{10,11... | collective-permute-start | bytes 4423688 | tf_op jit(solution)/shard_map/ppermute | solution.py:31
  39.0 10.0 %copy-start.9 = (bf16[6,64,1152]{2,1,0:T(8,128)(2,1)}, bf16[6,64,1152]{2,1,0:T(8,128)(2,1)S(1)}, u32[]{:S(2)}) copy-start(bf16[6,64,1152]{2,1,0:T(8,128)(2,1)S(1)} %constant_dynamic-update-slice_fusion.8.refs_1_) | copy-start | bytes 2654212
  39.0 10.0 %collective-permute-start.13 = (bf16[6,64,1152]{2,1,0:T(8,128)(2,1)S(1)}, bf16[6,64,1152]{2,1,0:T(8,128)(2,1)S(1)}, u32[]{:S(2)}, u32[]{:S(2)}) collective-permute-start(bf16[6,64,1152]{2,1,0:T(8,128)(2,1)S(1)} %constant_dynamic-update-slice_fusion.8.refs_1_), channel_id=1, source_target_pairs={{0,1},{1,0},{2,3},{3,2},{4,5},{5,4},{6,7},{7,6},{8,9},{9,8},{10,11... | collective-permute-start | bytes 2654216 | tf_op jit(solution)/shard_map/ppermute | solution.py:31
  49.0 0.9 copy-start.12
  72.7 18.7 %collective-permute-start.14 = (bf16[16,64,1408]{2,1,0:T(8,128)(2,1)}, bf16[16,64,1408]{2,1,0:T(8,128)(2,1)S(1)}, u32[]{:S(2)}, u32[]{:S(2)}) collective-permute-start(bf16[16,64,1408]{2,1,0:T(8,128)(2,1)} %get-tuple-element.26), channel_id=1, source_target_pairs={{0,1},{1,0},{2,3},{3,2},{4,5},{5,4},{6,7},{7,6},{8,9},{9,8},{10,11... | collective-permute-start | bytes 8650760 | tf_op jit(solution)/shard_map/ppermute | solution.py:31
  92.1 12.0 %collective-permute-start.15 = (bf16[2,64,1408]{2,1,0:T(8,128)(2,1)S(1)}, bf16[2,64,1408]{2,1,0:T(8,128)(2,1)S(1)}, u32[]{:S(2)}, u32[]{:S(2)}) collective-permute-start(bf16[2,64,1408]{2,1,0:T(8,128)(2,1)S(1)} %fusion.3), channel_id=1, source_target_pairs={{0,4},{4,8},{8,12},{12,16},{16,20},{20,24},{24,28},{28,0},{1,5},{5... | collective-permute-start | bytes 1081352 | tf_op jit(solution)/shard_map/ppermute | solution.py:36
  104.2 14.4 %collective-permute-start.16 = (bf16[2,64,1408]{2,1,0:T(8,128)(2,1)S(1)}, bf16[2,64,1408]{2,1,0:T(8,128)(2,1)S(1)}, u32[]{:S(2)}, u32[]{:S(2)}) collective-permute-start(bf16[2,64,1408]{2,1,0:T(8,128)(2,1)S(1)} %add_convert_fusion.6), channel_id=1, source_target_pairs={{0,4},{4,8},{8,12},{12,16},{16,20},{20,24},{24,28},{28,0},{1,5},{5... | collective-permute-start | bytes 1081352 | tf_op jit(solution)/shard_map/ppermute | solution.py:36
  118.6 14.1 %collective-permute-start.17 = (bf16[2,64,1408]{2,1,0:T(8,128)(2,1)S(1)}, bf16[2,64,1408]{2,1,0:T(8,128)(2,1)S(1)}, u32[]{:S(2)}, u32[]{:S(2)}) collective-permute-start(bf16[2,64,1408]{2,1,0:T(8,128)(2,1)S(1)} %add_convert_fusion.5), channel_id=1, source_target_pairs={{0,4},{4,8},{8,12},{12,16},{16,20},{20,24},{24,28},{28,0},{1,5},{5... | collective-permute-start | bytes 1081352 | tf_op jit(solution)/shard_map/ppermute | solution.py:36
  133.0 8.7 %collective-permute-start.19 = (bf16[2,64,1408]{2,1,0:T(8,128)(2,1)S(1)}, bf16[2,64,1408]{2,1,0:T(8,128)(2,1)S(1)}, u32[]{:S(2)}, u32[]{:S(2)}) collective-permute-start(bf16[2,64,1408]{2,1,0:T(8,128)(2,1)S(1)} %get-tuple-element.39), channel_id=1, source_target_pairs={{0,28},{4,0},{8,4},{12,8},{16,12},{20,16},{24,20},{28,24},{1,29},{... | collective-permute-start | bytes 1081352 | tf_op jit(solution)/shard_map/ppermute | solution.py:36
  141.8 9.4 %collective-permute-start.20 = (bf16[2,64,1408]{2,1,0:T(8,128)(2,1)S(1)}, bf16[2,64,1408]{2,1,0:T(8,128)(2,1)S(1)}, u32[]{:S(2)}, u32[]{:S(2)}) collective-permute-start(bf16[2,64,1408]{2,1,0:T(8,128)(2,1)S(1)} %add_convert_fusion.3), channel_id=1, source_target_pairs={{0,28},{4,0},{8,4},{12,8},{16,12},{20,16},{24,20},{28,24},{1,29},{... | collective-permute-start | bytes 1081352 | tf_op jit(solution)/shard_map/ppermute | solution.py:36
  145.8 9.3 %collective-permute-start.18 = (bf16[2,64,1408]{2,1,0:T(8,128)(2,1)S(1)}, bf16[2,64,1408]{2,1,0:T(8,128)(2,1)S(1)}, u32[]{:S(2)}, u32[]{:S(2)}) collective-permute-start(bf16[2,64,1408]{2,1,0:T(8,128)(2,1)S(1)} %get-tuple-element.38), channel_id=1, source_target_pairs={{0,4},{4,8},{8,12},{12,16},{16,20},{20,24},{24,28},{28,0},{1,5},{5... | collective-permute-start | bytes 1081352 | tf_op jit(solution)/shard_map/ppermute | solution.py:36
  151.3 8.7 %collective-permute-start.21 = (bf16[2,64,1408]{2,1,0:T(8,128)(2,1)S(1)}, bf16[2,64,1408]{2,1,0:T(8,128)(2,1)S(1)}, u32[]{:S(2)}, u32[]{:S(2)}) collective-permute-start(bf16[2,64,1408]{2,1,0:T(8,128)(2,1)S(1)} %add_convert_fusion.2), channel_id=1, source_target_pairs={{0,28},{4,0},{8,4},{12,8},{16,12},{20,16},{24,20},{28,24},{1,29},{... | collective-permute-start | bytes 1081352 | tf_op jit(solution)/shard_map/ppermute | solution.py:36
  160.1 9.8 %collective-permute-start.22 = (bf16[64,1408]{1,0:T(8,128)(2,1)S(1)}, bf16[64,1408]{1,0:T(8,128)(2,1)S(1)}, u32[]{:S(2)}, u32[]{:S(2)}) collective-permute-start(bf16[64,1408]{1,0:T(8,128)(2,1)S(1)} %get-tuple-element.45), channel_id=1, source_target_pairs={{0,2},{2,0},{1,3},{3,1},{4,6},{6,4},{5,7},{7,5},{8,10},{10,8},{9,1... | collective-permute-start | bytes 540680 | tf_op jit(solution)/shard_map/ppermute | solution.py:31
  165.9 7.4 %collective-permute-start.24 = (bf16[64,1408]{1,0:T(8,128)(2,1)S(1)}, bf16[64,1408]{1,0:T(8,128)(2,1)S(1)}, u32[]{:S(2)}, u32[]{:S(2)}) collective-permute-start(bf16[64,1408]{1,0:T(8,128)(2,1)S(1)} %get-tuple-element.45), channel_id=1, source_target_pairs={{0,130},{2,128},{128,2},{130,0},{1,131},{3,129},{129,3},{131,1},{4... | collective-permute-start | bytes 540680 | tf_op jit(solution)/shard_map/ppermute | solution.py:419
  165.9 7.1 %collective-permute-start.23 = (bf16[64,1408]{1,0:T(8,128)(2,1)S(1)}, bf16[64,1408]{1,0:T(8,128)(2,1)S(1)}, u32[]{:S(2)}, u32[]{:S(2)}) collective-permute-start(bf16[64,1408]{1,0:T(8,128)(2,1)S(1)} %get-tuple-element.44), channel_id=1, source_target_pairs={{0,128},{128,0},{1,129},{129,1},{2,130},{130,2},{3,131},{131,3},{4... | collective-permute-start | bytes 540680 | tf_op jit(solution)/shard_map/ppermute | solution.py:31
  173.4 17.5 %copy-start.1 = (bf16[2,64,1408]{2,1,0:T(8,128)(2,1)}, bf16[2,64,1408]{2,1,0:T(8,128)(2,1)S(1)}, u32[]{:S(2)}) copy-start(bf16[2,64,1408]{2,1,0:T(8,128)(2,1)S(1)} %pad_maximum_fusion.refs_0_) | copy-start | bytes 1081348
  173.4 10.6 %collective-permute-start.26 = (bf16[2,64,1408]{2,1,0:T(8,128)(2,1)S(1)}, bf16[2,64,1408]{2,1,0:T(8,128)(2,1)S(1)}, u32[]{:S(2)}, u32[]{:S(2)}) collective-permute-start(bf16[2,64,1408]{2,1,0:T(8,128)(2,1)S(1)} %pad_maximum_fusion.refs_0_), channel_id=1, source_target_pairs={{0,32},{32,64},{64,96},{96,0},{1,33},{33,65},{65,97},{97,1},{2,34}... | collective-permute-start | bytes 1081352 | tf_op jit(solution)/shard_map/ppermute | solution.py:36
  175.0 9.5 %collective-permute-start.25 = (bf16[2,64,1408]{2,1,0:T(8,128)(2,1)S(1)}, bf16[2,64,1408]{2,1,0:T(8,128)(2,1)S(1)}, u32[]{:S(2)}, u32[]{:S(2)}) collective-permute-start(bf16[2,64,1408]{2,1,0:T(8,128)(2,1)S(1)} %pad_maximum_fusion.refs_0_), channel_id=1, source_target_pairs={{0,96},{32,0},{64,32},{96,64},{1,97},{33,1},{65,33},{97,65},{2,98}... | collective-permute-start | bytes 1081352 | tf_op jit(solution)/shard_map/ppermute | solution.py:36
  184.1 6.8 %copy-start.2 = (bf16[2,64,1408]{2,1,0:T(8,128)(2,1)}, bf16[2,64,1408]{2,1,0:T(8,128)(2,1)S(1)}, u32[]{:S(2)}) copy-start(bf16[2,64,1408]{2,1,0:T(8,128)(2,1)S(1)} %collective-permute-done.26.refs_2_) | copy-start | bytes 1081348
  184.1 6.8 %collective-permute-start.27 = (bf16[1,64,1408]{2,1,0:T(8,128)(2,1)S(1)}, bf16[1,64,1408]{2,1,0:T(8,128)(2,1)S(1)}, u32[]{:S(2)}, u32[]{:S(2)}) collective-permute-start(bf16[1,64,1408]{2,1,0:T(8,128)(2,1)S(1)} %slice.169), channel_id=1, source_target_pairs={{0,32},{32,64},{64,96},{96,0},{1,33},{33,65},{65,97},{97,1},{2,34}... | collective-permute-start | bytes 540680 | tf_op jit(solution)/shard_map/ppermute | solution.py:36
  184.5 6.4 %copy-start.3 = (bf16[2,64,1408]{2,1,0:T(8,128)(2,1)}, bf16[2,64,1408]{2,1,0:T(8,128)(2,1)S(1)}, u32[]{:S(2)}) copy-start(bf16[2,64,1408]{2,1,0:T(8,128)(2,1)S(1)} %collective-permute-done.25.refs_1_) | copy-start | bytes 1081348
  184.5 6.4 %collective-permute-start.28 = (bf16[1,64,1408]{2,1,0:T(8,128)(2,1)S(1)}, bf16[1,64,1408]{2,1,0:T(8,128)(2,1)S(1)}, u32[]{:S(2)}, u32[]{:S(2)}) collective-permute-start(bf16[1,64,1408]{2,1,0:T(8,128)(2,1)S(1)} %slice.170), channel_id=1, source_target_pairs={{0,96},{32,0},{64,32},{96,64},{1,97},{33,1},{65,33},{97,65},{2,98}... | collective-permute-start | bytes 540680 | tf_op jit(solution)/shard_map/ppermute | solution.py:36
  190.9 0.7 copy-start.5
  191.5 0.7 copy-start.6
  197.6 2.3 collective-permute-start.29
  199.9 25.2 %copy-start.4 = (bf16[1024,64]{1,0:T(8,128)(2,1)S(1)}, bf16[1024,64]{1,0:T(8,128)(2,1)}, u32[]{:S(2)}) copy-start(bf16[1024,64]{1,0:T(8,128)(2,1)} %get-tuple-element.24) | copy-start | bytes 393220
  199.9 26.1 %copy-start.8 = (bf16[128,64]{1,0:T(8,128)(2,1)S(1)}, bf16[128,64]{1,0:T(8,128)(2,1)}, u32[]{:S(2)}) copy-start(bf16[128,64]{1,0:T(8,128)(2,1)} %get-tuple-element.28) | copy-start | bytes 49156
  201.2 25.5 %copy-start.11 = (f32[2,8,128]{2,1,0:T(8,128)S(1)}, f32[2,8,128]{2,1,0:T(8,128)}, u32[]{:S(2)}) copy-start(f32[2,8,128]{2,1,0:T(8,128)} %get-tuple-element.31) | copy-start | bytes 24580
  201.2 6.5 %collective-permute-start.30 = (bf16[2,32,576]{2,1,0:T(8,128)(2,1)S(1)}, bf16[2,32,576]{2,1,0:T(8,128)(2,1)S(1)}, u32[]{:S(2)}, u32[]{:S(2)}) collective-permute-start(bf16[2,32,576]{2,1,0:T(8,128)(2,1)S(1)} %get-tuple-element.42), channel_id=1, source_target_pairs={{0,4},{4,8},{8,12},{12,16},{16,20},{20,24},{24,28},{28,0},{1,5},{5... | collective-permute-start | bytes 221192 | tf_op jit(solution)/shard_map/ppermute | solution.py:36
  207.8 5.7 %collective-permute-start.31 = (bf16[2,32,576]{2,1,0:T(8,128)(2,1)S(1)}, bf16[2,32,576]{2,1,0:T(8,128)(2,1)S(1)}, u32[]{:S(2)}, u32[]{:S(2)}) collective-permute-start(bf16[2,32,576]{2,1,0:T(8,128)(2,1)S(1)} %add_convert_fusion.13), channel_id=1, source_target_pairs={{0,4},{4,8},{8,12},{12,16},{16,20},{20,24},{24,28},{28,0},{1,5},{5... | collective-permute-start | bytes 221192 | tf_op jit(solution)/shard_map/ppermute | solution.py:36
  207.8 5.8 %collective-permute-start.34 = (bf16[2,32,576]{2,1,0:T(8,128)(2,1)S(1)}, bf16[2,32,576]{2,1,0:T(8,128)(2,1)S(1)}, u32[]{:S(2)}, u32[]{:S(2)}) collective-permute-start(bf16[2,32,576]{2,1,0:T(8,128)(2,1)S(1)} %get-tuple-element.43), channel_id=1, source_target_pairs={{0,28},{4,0},{8,4},{12,8},{16,12},{20,16},{24,20},{28,24},{1,29},{... | collective-permute-start | bytes 221192 | tf_op jit(solution)/shard_map/ppermute | solution.py:36
  213.5 5.7 %collective-permute-start.32 = (bf16[2,32,576]{2,1,0:T(8,128)(2,1)S(1)}, bf16[2,32,576]{2,1,0:T(8,128)(2,1)S(1)}, u32[]{:S(2)}, u32[]{:S(2)}) collective-permute-start(bf16[2,32,576]{2,1,0:T(8,128)(2,1)S(1)} %add_convert_fusion.12), channel_id=1, source_target_pairs={{0,4},{4,8},{8,12},{12,16},{16,20},{20,24},{24,28},{28,0},{1,5},{5... | collective-permute-start | bytes 221192 | tf_op jit(solution)/shard_map/ppermute | solution.py:36
  219.3 5.1 %collective-permute-start.35 = (bf16[2,32,576]{2,1,0:T(8,128)(2,1)S(1)}, bf16[2,32,576]{2,1,0:T(8,128)(2,1)S(1)}, u32[]{:S(2)}, u32[]{:S(2)}) collective-permute-start(bf16[2,32,576]{2,1,0:T(8,128)(2,1)S(1)} %get-tuple-element.41), channel_id=1, source_target_pairs={{0,28},{4,0},{8,4},{12,8},{16,12},{20,16},{24,20},{28,24},{1,29},{... | collective-permute-start | bytes 221192 | tf_op jit(solution)/shard_map/ppermute | solution.py:36
  219.4 7.9 %collective-permute-start.33 = (bf16[2,32,576]{2,1,0:T(8,128)(2,1)S(1)}, bf16[2,32,576]{2,1,0:T(8,128)(2,1)S(1)}, u32[]{:S(2)}, u32[]{:S(2)}) collective-permute-start(bf16[2,32,576]{2,1,0:T(8,128)(2,1)S(1)} %get-tuple-element.40), channel_id=1, source_target_pairs={{0,4},{4,8},{8,12},{12,16},{16,20},{20,24},{24,28},{28,0},{1,5},{5... | collective-permute-start | bytes 221192 | tf_op jit(solution)/shard_map/ppermute | solution.py:36
  224.4 4.5 %collective-permute-start.36 = (bf16[2,32,576]{2,1,0:T(8,128)(2,1)S(1)}, bf16[2,32,576]{2,1,0:T(8,128)(2,1)S(1)}, u32[]{:S(2)}, u32[]{:S(2)}) collective-permute-start(bf16[2,32,576]{2,1,0:T(8,128)(2,1)S(1)} %add_convert_fusion.9), channel_id=1, source_target_pairs={{0,28},{4,0},{8,4},{12,8},{16,12},{20,16},{24,20},{28,24},{1,29},{... | collective-permute-start | bytes 221192 | tf_op jit(solution)/shard_map/ppermute | solution.py:36
  229.0 4.1 %collective-permute-start.37 = (bf16[32,576]{1,0:T(8,128)(2,1)S(1)}, bf16[32,576]{1,0:T(8,128)(2,1)S(1)}, u32[]{:S(2)}, u32[]{:S(2)}) collective-permute-start(bf16[32,576]{1,0:T(8,128)(2,1)S(1)} %fusion.10), channel_id=1, source_target_pairs={{0,2},{2,0},{1,3},{3,1},{4,6},{6,4},{5,7},{7,5},{8,10},{10,8},{9,1... | collective-permute-start | bytes 110600 | tf_op jit(solution)/shard_map/ppermute | solution.py:31

commit v2 on v1

--- a/solution.py
+++ b/solution.py
@@ -36,27 +36,35 @@
     return lax.ppermute(x, axis, [(i, (i + by) % n) for i in range(n)])
 
 
-def added(a, b):
-    return (a.astype(jnp.float32) + b.astype(jnp.float32)).astype(a.dtype)
-
-
 def ring_sum(parts, axis):
     n = lax.axis_size(axis)
-    up = parts[n // 2]
-    for k in range(n // 2 - 1, 0, -1):
-        up = added(parts[k], shifted(up, axis, 1))
-    up = shifted(up, axis, 1)
-    down = parts[n // 2 + 1]
-    for k in range(n // 2 + 2, n):
-        down = added(parts[k], shifted(down, axis, -1))
-    down = shifted(down, axis, -1)
-    f32 = jnp.float32
+    f32, bf16 = jnp.float32, jnp.bfloat16
+    up, down = (parts[k].astype(bf16) for k in (n // 2, n // 2 + 1))
+    for k in range(n // 2 - 1, -1, -1):
+        if k:
+            up = (parts[k].astype(f32) + shifted(up, axis, 1).astype(f32)).astype(bf16)
+        if 0 < k < n // 2 - 1:
+            down = (parts[n - k].astype(f32) + shifted(down, axis, -1).astype(f32)).astype(bf16)
+    up, down = shifted(up, axis, 1), shifted(down, axis, -1)
     return parts[0].astype(f32) + up.astype(f32) + down.astype(f32)
 
 
 def owner_at(me, core, ahead, y):
     n_z, my_z, my_y, my_core = me[0], me[1], me[2], me[3]
     return (lax.rem(my_z + ahead, n_z) * 2 + (my_y ^ y)) * 2 + (my_core ^ core)
+
+
+def batches():
+    n = N_CTX // 4
+    far = [[n // 2]] + [[k, n - k] for k in range(n // 2 - 1, 0, -1)]
+    return far[:-1] + [far[-1] + [0]]
+
+
+def fill_owners(table, me):
+    places = [(z, y) for batch in batches() for y in range(2) for z in batch]
+    for core in range(2):
+        for i, place in enumerate(places):
+            table[core * len(places) + i] = owner_at(me, core, *place)
 
 
 vmem = pl.BlockSpec(memory_space=pltpu.VMEM)
@@ -88,7 +96,7 @@
     return call(kernel, [shape], 0, (lat, rope), [], 1000, 8)[0]
 
 
-def prepare(me, queries, query_rope, outputs, grad_out, weight):
+def prepare(queries, query_rope, outputs, grad_out, weight):
     rows, latent = queries.shape
     rope = query_rope.shape[1]
     tokens = grad_out.shape[0]
@@ -96,29 +104,19 @@
     value = grad_out.shape[1] // heads
     wide = latent + 128
     f32, bf16 = jnp.float32, jnp.bfloat16
-    n_dp, n_z = N_DP, N_CTX // 4
-    each = latent // (n_dp * N_CTX)
-
-    def kernel(me_ref, q_ref, qr_ref, out_ref, d_ref, w_ref, wide_ref, g_ref, delta_ref, v_ref,
-               out_wide, g_wide, v_wide):
+    lanes = [slice(k, k + 128) for k in range(0, latent, 128)]
+
+    def kernel(q_ref, qr_ref, out_ref, d_ref, w_ref, wide_ref, g_ref, delta_ref, g_wide):
         wide_ref[:, :latent] = q_ref[...]
         wide_ref[:, latent:] = jnp.concatenate(
             [qr_ref[...], jnp.zeros((rows, wide - latent - rope), bf16)], axis=1
         )
-        lanes = [slice(k, k + 128) for k in range(0, latent, 128)]
-        for k, lane in enumerate(lanes):
-            out_wide[k] = out_ref[:, lane].astype(f32)
 
         def head_step(h, carry):
-            at = pl.ds(h, tokens, stride=heads)
             column = pl.ds(pl.multiple_of(h * value, value), value)
-            d = d_ref[:, column]
-            g = nt(d, w_ref[:, column])
+            g = nt(d_ref[:, column], w_ref[:, column])
             for k, lane in enumerate(lanes):
-                g_wide[k, at, :] = g[:, lane]
-                v_wide[pl.ds(h + k * 128 * heads, 128, stride=heads), :] = tn(
-                    out_wide[k, at, :].astype(bf16), d
-                )
+                g_wide[k, pl.ds(h, tokens, stride=heads), :] = g[:, lane]
             return carry
 
         lax.fori_loop(0, heads, head_step, 0)
@@ -126,15 +124,48 @@
         for k, lane in enumerate(lanes):
             g = g_wide[k].astype(bf16)
             g_ref[:, lane] = g
-            delta += g.astype(f32) * out_wide[k]
+            delta += g.astype(f32) * out_ref[:, lane].astype(f32)
         delta = jnp.sum(delta, axis=1, keepdims=True)
         delta = jnp.broadcast_to(delta, (rows, 128)).T[:1]
         delta_ref[0] = delta[:, : rows // 2]
         delta_ref[1] = delta[:, rows // 2 :]
-        me = [me_ref[i] for i in range(4)]
+
+    return call(
+        kernel,
+        [((rows, wide), bf16), ((rows, latent), bf16), ((2, 1, rows // 2), f32)],
+        0,
+        (queries, query_rope, outputs, grad_out, weight),
+        [pltpu.VMEM((latent // 128, rows, 128), f32)],
+        1000,
+    )
+
+
+def value_parts(me, outputs, grad_out):
+    rows, latent = outputs.shape
+    tokens = grad_out.shape[0]
+    heads = rows // tokens
+    value = grad_out.shape[1] // heads
+    f32, bf16 = jnp.float32, jnp.bfloat16
+    lanes = [slice(k, k + 128) for k in range(0, latent, 128)]
+    n_dp = N_DP
+    each = latent // (n_dp * N_CTX)
+
+    def kernel(me_ref, out_ref, d_ref, v_ref, out_wide, v_wide, table):
+        fill_owners(table, [me_ref[i] for i in range(4)])
+        for k, lane in enumerate(lanes):
+            out_wide[k] = out_ref[:, lane].astype(f32)
+
+        def head_step(h, carry):
+            d = d_ref[:, pl.ds(pl.multiple_of(h * value, value), value)]
+            for k in range(len(lanes)):
+                out = out_wide[k, pl.ds(h, tokens, stride=heads), :].astype(bf16)
+                v_wide[pl.ds(h + k * 128 * heads, 128, stride=heads), :] = tn(out, d)
+            return carry
+
+        lax.fori_loop(0, heads, head_step, 0)
 
         def slot_step(slot, carry):
-            owner = owner_at(me, slot // (2 * n_z), slot // 2 % n_z, slot % 2)
+            owner = table[slot]
             for r in range(each):
                 parts = []
                 for dp in range(n_dp):
@@ -149,21 +180,16 @@
 
     return call(
         kernel,
-        [
-            ((rows, wide), bf16),
-            ((rows, latent), bf16),
-            ((2, 1, rows // 2), f32),
-            ((N_CTX, n_dp * heads, each * value), bf16),
-        ],
+        [((N_CTX, n_dp * heads, each * value), bf16)],
         1,
-        (me, queries, query_rope, outputs, grad_out, weight),
+        (me, outputs, grad_out),
         [
             pltpu.VMEM((latent // 128, rows, 128), f32),
-            pltpu.VMEM((latent // 128, rows, 128), f32),
             pltpu.VMEM((latent * heads, value), f32),
+            pltpu.SMEM((N_CTX,), jnp.int32),
         ],
         1000,
-    )
+    )[0]
 
 
 def attention(me, blocks, pieces, items, queries, grads, delta, values):
@@ -260,10 +286,11 @@
             return carry
 
         lax.fori_loop(0, 2, block_step, 0)
+        fill_owners(table, me)
 
         def unsort_step(j, carry):
             for core, out in enumerate((near_ref, far_ref)):
-                owner = owner_at(me, core, j // 2, j % 2)
+                owner = table[core * 2 * n_z + j]
                 for side in range(2):
                     place = blocks_ref[2 * owner + side]
                     at = pl.ds(pl.multiple_of(place * half, half), half)
@@ -393,32 +420,36 @@
             groups.append(jnp.concatenate(group, axis=0))
             items.append(places)
             group, places = [], []
-    pieces = groups + [swapped(x, "core") for x in groups]
+    pieces = list(groups)
+    for x in groups:
+        pieces.append(swapped(x, "core"))
     items = [[(core, *place) for place in p] for core in range(2) for p in items]
 
-    queries, grads, delta, values = prepare(
-        me,
-        q_latent.reshape(-1, latent),
-        q_rope.reshape(-1, rope),
-        saved_output.reshape(-1, latent),
-        d_out[0],
-        w_uv,
-    )
+    outputs = saved_output.reshape(-1, latent)
+    queries, grads, delta = prepare(
+        q_latent.reshape(-1, latent), q_rope.reshape(-1, rope), outputs, d_out[0], w_uv
+    )
+    values = value_parts(me, outputs, d_out[0])
     d_q, d_qr, near_dk, far_dk = attention(
         me, blocks, pieces, items, queries, grads, delta, values
     )
-    near_dk = near_dk.reshape(n_z, 2, *near_dk.shape[1:]).astype(wide)
-    far_dk = swapped(far_dk, "core").reshape(near_dk.shape).astype(wide)
-    summed = ring_sum([(near_dk[k] + far_dk[k]).astype(bf16) for k in range(n_z)], "z")
-    summed = summed.astype(bf16)
-
-    flipped = [(i, 3 - i) for i in range(4)]
-    summed = jnp.stack(
-        [
-            added(summed[0], swapped(summed[1], "ylo")),
-            added(swapped(summed[0], "yhi"), lax.ppermute(summed[1], ("yhi", "ylo"), flipped)),
-        ]
-    )
+    there_dk = swapped(far_dk, "core")
+    sums = {}
+    at = 0
+    for batch in batches():
+        n = len(batch)
+        mine, other = (
+            near_dk[k : k + n].astype(wide) + there_dk[k : k + n].astype(wide)
+            for k in (at, at + n)
+        )
+        other = other.astype(bf16)
+        other = swapped(other, "ylo")
+        part = mine + other.astype(wide)
+        for k, z in enumerate(batch):
+            sums[z] = part[k]
+        at += 2 * n
+    summed = ring_sum([sums[k] for k in range(n_z)], "z").astype(bf16)
+    summed = jnp.stack([summed, swapped(summed, "yhi")])
 
     n_x = lax.axis_size("x")
     after, before = shifted(summed, "x", -1), shifted(summed, "x", 1)

time: 236 us -> 224 us (0.949)
  waiting for transfers between devices: 104 us -> 89.3 us
    ppermute x25, waiting for transfers between devices: 87 us -> 46.4 us  [shifted(): return lax.ppermute(x, axis, [(i, (i + by) % n) for i in range(n)])]
    ppermute x12 -> x15, waiting for transfers between devices: 16.5 us -> 42.9 us  [swapped(): return lax.ppermute(x, axis, [(0, 1), (1, 0)])]
    ppermute x12 -> x15, starting transfers between devices: 28.9 us -> 40.3 us  [swapped(): return lax.ppermute(x, axis, [(0, 1), (1, 0)])]
    ppermute x25, starting transfers between devices: 49.4 us -> 40 us  [shifted(): return lax.ppermute(x, axis, [(i, (i + by) % n) for i in range(n)])]
    pallas_call x4 -> x5, Pallas kernels: 36.4 us -> 38.3 us  [call(): pl.pallas_call(kernel, out_shape=tuple((jax.ShapeDtypeStruct(*o) for o in...]
    unnamed x42 -> x44, local copies, waits for them, and re-layouts: 7.24 us -> 6.85 us
  transfers between devices with their start and end apart: 38 -> 40, of which waited for: 25 -> 26; matrix products, arithmetic and copies ran while one was open for 3% -> 3% of each run, Pallas kernels for 3% -> 5%
where the time goes in v2:
time: 224 us; the launch traced here: 223 us
  waiting for transfers between devices  89.3 us (40%)
  starting transfers between devices  80.3 us (36%)
  Pallas kernels  38.3 us (17%)
  local copies, waits for them, and re-layouts  7.66 us (3%)
  other arithmetic  6.37 us (3%)
    ppermute x25, waiting for transfers between devices, shifted(): return lax.ppermute(x, axis, [(i, (i + by) % n) for i in range(n)])  46.4 us
    ppermute x15, waiting for transfers between devices, swapped(): return lax.ppermute(x, axis, [(0, 1), (1, 0)])  42.9 us
    ppermute x15, starting transfers between devices, swapped(): return lax.ppermute(x, axis, [(0, 1), (1, 0)])  40.3 us
    ppermute x25, starting transfers between devices, shifted(): return lax.ppermute(x, axis, [(i, (i + by) % n) for i in range(n)])  40 us
    pallas_call x5, Pallas kernels, call(): pl.pallas_call(kernel, out_shape=tuple((jax.ShapeDtypeStruct(*o) for o in...  38.3 us
    unnamed x44, local copies, waits for them, and re-layouts  6.85 us
  transfers between devices with their start and end apart: 40, of which 26 were waited for; matrix products, arithmetic and copies ran while one was open for 3% of the time, Pallas kernels for 5%

profile of v2, /device:TPU:16, one launch (start us, length us, event | category | flops | bytes accessed | tf_op | source)
XLA Modules:
  0.0 222.9 jit_solution(16793189514659126197)
XLA Ops:
  0.6 0.8 copy.15
  1.5 0.9 copy-done
  2.4 1.9 collective-permute-start.2
  4.4 4.0 %collective-permute-start.1 = (bf16[64,1152]{1,0:T(8,128)(2,1)S(1)}, bf16[64,1152]{1,0:T(8,128)(2,1)S(1)}, u32[]{:S(2)}, u32[]{:S(2)}) collective-permute-start(bf16[64,1152]{1,0:T(8,128)(2,1)S(1)} %shard_map.136), channel_id=1, source_target_pairs={{0,28},{4,0},{8,4},{12,8},{16,12},{20,16},{24,20},{28,24},{1,29},{... | collective-permute-start | bytes 442376 | tf_op jit(solution)/shard_map/ppermute | solution.py:36
  8.4 1.3 collective-permute-start
  9.7 2.5 %collective-permute-done.2 = bf16[64,1152]{1,0:T(8,128)(2,1)S(1)} collective-permute-done((bf16[64,1152]{1,0:T(8,128)(2,1)S(1)}, bf16[64,1152]{1,0:T(8,128)(2,1)S(1)}, u32[]{:S(2)}, u32[]{:S(2)}) %collective-permute-start.2) | collective-permute-done | bytes 147488 | tf_op jit(solution)/shard_map/ppermute | solution.py:36
  12.2 1.4 collective-permute-start.3
  13.6 3.2 %collective-permute-start.4 = (bf16[64,1152]{1,0:T(8,128)(2,1)S(1)}, bf16[64,1152]{1,0:T(8,128)(2,1)S(1)}, u32[]{:S(2)}, u32[]{:S(2)}) collective-permute-start(bf16[64,1152]{1,0:T(8,128)(2,1)S(1)} %collective-permute-done.1), channel_id=1, source_target_pairs={{0,28},{4,0},{8,4},{12,8},{16,12},{20,16},{24,20},{28,24},{1,29},{... | collective-permute-start | bytes 442376 | tf_op jit(solution)/shard_map/ppermute | solution.py:36
  16.9 3.0 %collective-permute-done.5 = bf16[64,1152]{1,0:T(8,128)(2,1)S(1)} collective-permute-done((bf16[64,1152]{1,0:T(8,128)(2,1)S(1)}, bf16[64,1152]{1,0:T(8,128)(2,1)S(1)}, u32[]{:S(2)}, u32[]{:S(2)}) %collective-permute-start.5) | collective-permute-done | bytes 147488 | tf_op jit(solution)/shard_map/ppermute | solution.py:36
  19.9 3.2 %collective-permute-start.7 = (bf16[64,1152]{1,0:T(8,128)(2,1)S(1)}, bf16[64,1152]{1,0:T(8,128)(2,1)S(1)}, u32[]{:S(2)}, u32[]{:S(2)}) collective-permute-start(bf16[64,1152]{1,0:T(8,128)(2,1)S(1)} %collective-permute-done.4), channel_id=1, source_target_pairs={{0,28},{4,0},{8,4},{12,8},{16,12},{20,16},{24,20},{28,24},{1,29},{... | collective-permute-start | bytes 442376 | tf_op jit(solution)/shard_map/ppermute | solution.py:36
  23.2 0.8 collective-permute-start.6
  24.0 2.2 %collective-permute-done.8 = bf16[64,1152]{1,0:T(8,128)(2,1)S(1)} collective-permute-done((bf16[64,1152]{1,0:T(8,128)(2,1)S(1)}, bf16[64,1152]{1,0:T(8,128)(2,1)S(1)}, u32[]{:S(2)}, u32[]{:S(2)}) %collective-permute-start.8) | collective-permute-done | bytes 147488 | tf_op jit(solution)/shard_map/ppermute | solution.py:36
  26.3 0.8 collective-permute-start.9
  27.2 1.4 collective-permute-start.10
  28.7 4.8 %collective-permute-done.10 = bf16[64,1152]{1,0:T(8,128)(2,1)S(1)} collective-permute-done((bf16[64,1152]{1,0:T(8,128)(2,1)S(1)}, bf16[64,1152]{1,0:T(8,128)(2,1)S(1)}, u32[]{:S(2)}, u32[]{:S(2)}) %collective-permute-start.10) | collective-permute-done | bytes 147488 | tf_op jit(solution)/shard_map/ppermute | solution.py:36
  33.5 1.3 collective-permute-start.11
  35.0 2.4 %collective-permute-done.9 = bf16[2,64,1152]{2,1,0:T(8,128)(2,1)S(1)} collective-permute-done((bf16[2,64,1152]{2,1,0:T(8,128)(2,1)S(1)}, bf16[2,64,1152]{2,1,0:T(8,128)(2,1)S(1)}, u32[]{:S(2)}, u32[]{:S(2)}) %collective-permute-start.9) | collective-permute-done | bytes 294944 | tf_op jit(solution)/shard_map/ppermute | solution.py:31
  37.5 1.5 collective-permute-done.11
  40.0 5.0 %shard_map.138.refs_7_ = bf16[32,64,256]{2,1,0:T(8,128)(2,1)} custom-call(s32[6]{0:T(128)} %stack.65.me_ref, bf16[1024,512]{1,0:T(8,128)(2,1)} %bitcast.86, bf16[128,1024]{1,0:T(8,128)(2,1)} %bitcast.88), custom_call_target="tpu_custom_call" | custom-call | flops 1000 | bytes 4194304 | tf_op jit(solution)/shard_map/pallas_call | solution.py:75
  44.9 0.9 copy.16
  45.8 5.2 %shard_map.137 = (bf16[1024,640]{1,0:T(8,128)(2,1)}, bf16[1024,512]{1,0:T(8,128)(2,1)}, f32[2,1,512]{2,1,0:T(1,128)}) custom-call(bf16[1024,512]{1,0:T(8,128)(2,1)} %bitcast.91, bf16[1024,64]{1,0:T(8,128)(2,1)} %bitcast.90, bf16[1024,512]{1,0:T(8,128)(2,1)} %bitcast.87, bf16[128,1024]{1,0:T(8,128)(2,1)} %bitcast.89, bf16[512,1024]{1,0:T(8,128)(2,1)} %w_ref.1), custom_call_target="tpu_custom_call" | custom-call | flops 1000 | bytes 4194304 | tf_op jit(solution)/shard_map/pallas_call | solution.py:75
  51.1 0.9 copy-done.13
  51.9 22.7 %shard_map.139 = (bf16[1024,512]{1,0:T(8,128)(2,1)}, bf16[1024,64]{1,0:T(8,128)(2,1)}, bf16[16,64,1408]{2,1,0:T(8,128)(2,1)}, bf16[16,64,1408]{2,1,0:T(8,128)(2,1)}) custom-call(s32[6]{0:T(128)} %stack.65.me_ref, s32[64]{0:T(128)} %blocks_ref.1, bf16[10,64,1152]{2,1,0:T(8,128)(2,1)} %copy-done.11, bf16[6,64,1152]{2,1,0:T(8,128)(2,1)} %copy-done.10, ...), custom_call_target="tpu_custom_call" | custom-call | flops 13421772800 | bytes 4194304 | tf_op jit(solution)/shard_map/pallas_call | solution.py:75
  74.6 13.6 %collective-permute-start.14 = (bf16[16,64,1408]{2,1,0:T(8,128)(2,1)}, bf16[16,64,1408]{2,1,0:T(8,128)(2,1)S(1)}, u32[]{:S(2)}, u32[]{:S(2)}) collective-permute-start(bf16[16,64,1408]{2,1,0:T(8,128)(2,1)} %get-tuple-element.24), channel_id=1, source_target_pairs={{0,1},{1,0},{2,3},{3,2},{4,5},{5,4},{6,7},{7,6},{8,9},{9,8},{10,11... | collective-permute-start | bytes 8650760 | tf_op jit(solution)/shard_map/ppermute | solution.py:31
  88.2 5.1 %collective-permute-done.14 = bf16[16,64,1408]{2,1,0:T(8,128)(2,1)S(1)} collective-permute-done((bf16[16,64,1408]{2,1,0:T(8,128)(2,1)}, bf16[16,64,1408]{2,1,0:T(8,128)(2,1)S(1)}, u32[]{:S(2)}, u32[]{:S(2)}) %collective-permute-start.14) | collective-permute-done | bytes 2883616 | tf_op jit(solution)/shard_map/ppermute | solution.py:31
  93.3 1.1 add_convert_fusion.5
  94.5 14.0 %collective-permute-start.18 = (bf16[1,64,1408]{2,1,0:T(8,128)(2,1)S(1)}, bf16[1,64,1408]{2,1,0:T(8,128)(2,1)S(1)}, u32[]{:S(2)}, u32[]{:S(2)}) collective-permute-start(bf16[1,64,1408]{2,1,0:T(8,128)(2,1)S(1)} %add_convert_fusion.5), channel_id=1, source_target_pairs={{0,2},{2,0},{1,3},{3,1},{4,6},{6,4},{5,7},{7,5},{8,10},{10,8},{9,1... | collective-permute-start | bytes 540680 | tf_op jit(solution)/shard_map/ppermute | solution.py:31
  108.5 1.1 add_convert_fusion.2
  109.7 1.2 add_convert_fusion.1
  110.8 2.1 collective-permute-start.15
  112.9 0.9 collective-permute-done.18
  114.0 7.6 %collective-permute-done.17 = bf16[2,64,1408]{2,1,0:T(8,128)(2,1)S(1)} collective-permute-done((bf16[2,64,1408]{2,1,0:T(8,128)(2,1)S(1)}, bf16[2,64,1408]{2,1,0:T(8,128)(2,1)S(1)}, u32[]{:S(2)}, u32[]{:S(2)}) %collective-permute-start.17) | collective-permute-done | bytes 360480 | tf_op jit(solution)/shard_map/ppermute | solution.py:31
  121.9 2.1 collective-permute-start.16
  124.1 2.0 collective-permute-start.20
  126.1 14.3 %collective-permute-done.16 = bf16[2,64,1408]{2,1,0:T(8,128)(2,1)S(1)} collective-permute-done((bf16[2,64,1408]{2,1,0:T(8,128)(2,1)S(1)}, bf16[2,64,1408]{2,1,0:T(8,128)(2,1)S(1)}, u32[]{:S(2)}, u32[]{:S(2)}) %collective-permute-start.16) | collective-permute-done | bytes 360480 | tf_op jit(solution)/shard_map/ppermute | solution.py:31
  140.7 3.2 %collective-permute-start.24 = (bf16[64,1408]{1,0:T(8,128)(2,1)S(1)}, bf16[64,1408]{1,0:T(8,128)(2,1)S(1)}, u32[]{:S(2)}, u32[]{:S(2)}) collective-permute-start(bf16[64,1408]{1,0:T(8,128)(2,1)S(1)} %get-tuple-element.41), channel_id=1, source_target_pairs={{0,28},{4,0},{8,4},{12,8},{16,12},{20,16},{24,20},{28,24},{1,29},{... | collective-permute-start | bytes 540680 | tf_op jit(solution)/shard_map/ppermute | solution.py:36
  144.1 3.8 %collective-permute-done.21 = bf16[64,1408]{1,0:T(8,128)(2,1)S(1)} collective-permute-done((bf16[64,1408]{1,0:T(8,128)(2,1)S(1)}, bf16[64,1408]{1,0:T(8,128)(2,1)S(1)}, u32[]{:S(2)}, u32[]{:S(2)}) %collective-permute-start.21) | collective-permute-done | bytes 180256 | tf_op jit(solution)/shard_map/ppermute | solution.py:36
  148.5 2.7 %collective-permute-start.22 = (bf16[64,1408]{1,0:T(8,128)(2,1)S(1)}, bf16[64,1408]{1,0:T(8,128)(2,1)S(1)}, u32[]{:S(2)}, u32[]{:S(2)}) collective-permute-start(bf16[64,1408]{1,0:T(8,128)(2,1)S(1)} %get-tuple-element.38), channel_id=1, source_target_pairs={{0,4},{4,8},{8,12},{12,16},{16,20},{20,24},{24,28},{28,0},{1,5},{5... | collective-permute-start | bytes 540680 | tf_op jit(solution)/shard_map/ppermute | solution.py:36
  151.8 3.5 %collective-permute-done.22 = bf16[64,1408]{1,0:T(8,128)(2,1)S(1)} collective-permute-done((bf16[64,1408]{1,0:T(8,128)(2,1)S(1)}, bf16[64,1408]{1,0:T(8,128)(2,1)S(1)}, u32[]{:S(2)}, u32[]{:S(2)}) %collective-permute-start.22) | collective-permute-done | bytes 180256 | tf_op jit(solution)/shard_map/ppermute | solution.py:36
  155.3 2.5 %collective-permute-done.25 = bf16[64,1408]{1,0:T(8,128)(2,1)S(1)} collective-permute-done((bf16[64,1408]{1,0:T(8,128)(2,1)S(1)}, bf16[64,1408]{1,0:T(8,128)(2,1)S(1)}, u32[]{:S(2)}, u32[]{:S(2)}) %collective-permute-start.25) | collective-permute-done | bytes 180256 | tf_op jit(solution)/shard_map/ppermute | solution.py:36
  158.5 6.4 %collective-permute-done.26 = bf16[64,1408]{1,0:T(8,128)(2,1)S(1)} collective-permute-done((bf16[64,1408]{1,0:T(8,128)(2,1)S(1)}, bf16[64,1408]{1,0:T(8,128)(2,1)S(1)}, u32[]{:S(2)}, u32[]{:S(2)}) %collective-permute-start.26) | collective-permute-done | bytes 180256 | tf_op jit(solution)/shard_map/ppermute | solution.py:31
  164.9 1.6 collective-permute-start.28
  166.5 1.7 collective-permute-start.27
  168.3 6.0 %collective-permute-done.28.refs_2_ = bf16[2,64,1408]{2,1,0:T(8,128)(2,1)S(1)} collective-permute-done((bf16[2,64,1408]{2,1,0:T(8,128)(2,1)S(1)}, bf16[2,64,1408]{2,1,0:T(8,128)(2,1)S(1)}, u32[]{:S(2)}, u32[]{:S(2)}) %collective-permute-start.28) | collective-permute-done | bytes 360480 | tf_op jit(solution)/shard_map/ppermute | solution.py:36
  174.3 1.6 collective-permute-start.29
  175.9 1.9 collective-permute-start.30
  177.8 3.3 %collective-permute-done.29.refs_3_ = bf16[1,64,1408]{2,1,0:T(8,128)(2,1)S(1)} collective-permute-done((bf16[1,64,1408]{2,1,0:T(8,128)(2,1)S(1)}, bf16[1,64,1408]{2,1,0:T(8,128)(2,1)S(1)}, u32[]{:S(2)}, u32[]{:S(2)}) %collective-permute-start.29) | collective-permute-done | bytes 180256 | tf_op jit(solution)/shard_map/ppermute | solution.py:36
  182.4 5.4 %shard_map.140 = (bf16[16,32,576]{2,1,0:T(8,128)(2,1)}, bf16[16,32,576]{2,1,0:T(8,128)(2,1)}, bf16[128,512]{1,0:T(8,128)(2,1)}, bf16[128,64]{1,0:T(8,128)(2,1)}, f32[2,8,128]{2,1,0:T(8,128)}) custom-call(s32[6]{0:T(128)} %stack.65.me_ref, bf16[2,64,1408]{2,1,0:T(8,128)(2,1)} %copy-done.2, bf16[2,64,1408]{2,1,0:T(8,128)(2,1)} %copy-done.4, ...), custom_call_target="tpu_custom_call" | custom-call | flops 1000 | bytes 4194304 | tf_op jit(solution)/shard_map/pallas_call | solution.py:75
  187.8 2.3 %collective-permute-done.31 = bf16[16,32,576]{2,1,0:T(8,128)(2,1)S(1)} collective-permute-done((bf16[16,32,576]{2,1,0:T(8,128)(2,1)}, bf16[16,32,576]{2,1,0:T(8,128)(2,1)S(1)}, u32[]{:S(2)}, u32[]{:S(2)}) %collective-permute-start.31) | collective-permute-done | bytes 589856 | tf_op jit(solution)/shard_map/ppermute | solution.py:31
  190.1 1.3 add_convert_fusion
  191.4 3.3 %collective-permute-start.32 = (bf16[2,32,576]{2,1,0:T(8,128)(2,1)S(1)}, bf16[2,32,576]{2,1,0:T(8,128)(2,1)S(1)}, u32[]{:S(2)}, u32[]{:S(2)}) collective-permute-start(bf16[2,32,576]{2,1,0:T(8,128)(2,1)S(1)} %get-tuple-element.44), channel_id=1, source_target_pairs={{0,4},{4,8},{8,12},{12,16},{16,20},{20,24},{24,28},{28,0},{1,5},{5... | collective-permute-start | bytes 221192 | tf_op jit(solution)/shard_map/ppermute | solution.py:36
  194.7 2.5 %collective-permute-done.32 = bf16[2,32,576]{2,1,0:T(8,128)(2,1)S(1)} collective-permute-done((bf16[2,32,576]{2,1,0:T(8,128)(2,1)S(1)}, bf16[2,32,576]{2,1,0:T(8,128)(2,1)S(1)}, u32[]{:S(2)}, u32[]{:S(2)}) %collective-permute-start.32) | collective-permute-done | bytes 73760 | tf_op jit(solution)/shard_map/ppermute | solution.py:36
  197.2 2.1 collective-permute-start.33
  199.3 1.2 collective-permute-start.36
  200.5 2.4 %collective-permute-done.33 = bf16[2,32,576]{2,1,0:T(8,128)(2,1)S(1)} collective-permute-done((bf16[2,32,576]{2,1,0:T(8,128)(2,1)S(1)}, bf16[2,32,576]{2,1,0:T(8,128)(2,1)S(1)}, u32[]{:S(2)}, u32[]{:S(2)}) %collective-permute-start.33) | collective-permute-done | bytes 73760 | tf_op jit(solution)/shard_map/ppermute | solution.py:36
  203.0 0.9 collective-permute-start.34
  204.0 4.7 %collective-permute-done.34 = bf16[2,32,576]{2,1,0:T(8,128)(2,1)S(1)} collective-permute-done((bf16[2,32,576]{2,1,0:T(8,128)(2,1)S(1)}, bf16[2,32,576]{2,1,0:T(8,128)(2,1)S(1)}, u32[]{:S(2)}, u32[]{:S(2)}) %collective-permute-start.34) | collective-permute-done | bytes 73760 | tf_op jit(solution)/shard_map/ppermute | solution.py:36
  208.8 2.0 collective-permute-start.35
  210.8 2.7 %collective-permute-done.37 = bf16[2,32,576]{2,1,0:T(8,128)(2,1)S(1)} collective-permute-done((bf16[2,32,576]{2,1,0:T(8,128)(2,1)S(1)}, bf16[2,32,576]{2,1,0:T(8,128)(2,1)S(1)}, u32[]{:S(2)}, u32[]{:S(2)}) %collective-permute-start.37) | collective-permute-done | bytes 73760 | tf_op jit(solution)/shard_map/ppermute | solution.py:36
  213.6 1.0 collective-permute-start.38
  214.6 0.8 copy.17
  216.7 1.4 collective-permute-done.38
  218.1 1.7 collective-permute-start.39
  219.9 2.4 %collective-permute-done.39 = bf16[32,576]{1,0:T(8,128)(2,1)S(1)} collective-permute-done((bf16[32,576]{1,0:T(8,128)(2,1)S(1)}, bf16[32,576]{1,0:T(8,128)(2,1)S(1)}, u32[]{:S(2)}, u32[]{:S(2)}) %collective-permute-start.39) | collective-permute-done | bytes 36896 | tf_op jit(solution)/shard_map/ppermute | solution.py:31
  (96 shorter events, 8.4 us)
Async XLA Ops:
  1.5 0.9 copy-start
  2.4 9.7 %collective-permute-start.2 = (bf16[64,1152]{1,0:T(8,128)(2,1)S(1)}, bf16[64,1152]{1,0:T(8,128)(2,1)S(1)}, u32[]{:S(2)}, u32[]{:S(2)}) collective-permute-start(bf16[64,1152]{1,0:T(8,128)(2,1)S(1)} %shard_map.136), channel_id=1, source_target_pairs={{0,4},{4,8},{8,12},{12,16},{16,20},{20,24},{24,28},{28,0},{1,5},{5... | collective-permute-start | bytes 442376 | tf_op jit(solution)/shard_map/ppermute | solution.py:36
  4.4 7.8 %collective-permute-start.1 = (bf16[64,1152]{1,0:T(8,128)(2,1)S(1)}, bf16[64,1152]{1,0:T(8,128)(2,1)S(1)}, u32[]{:S(2)}, u32[]{:S(2)}) collective-permute-start(bf16[64,1152]{1,0:T(8,128)(2,1)S(1)} %shard_map.136), channel_id=1, source_target_pairs={{0,28},{4,0},{8,4},{12,8},{16,12},{20,16},{24,20},{28,24},{1,29},{... | collective-permute-start | bytes 442376 | tf_op jit(solution)/shard_map/ppermute | solution.py:36
  8.4 8.4 %collective-permute-start = (bf16[1,64,1152]{2,1,0:T(8,128)(2,1)S(1)}, bf16[1,64,1152]{2,1,0:T(8,128)(2,1)S(1)}, u32[]{:S(2)}, u32[]{:S(2)}) collective-permute-start(bf16[1,64,1152]{2,1,0:T(8,128)(2,1)S(1)} %bitcast.83), channel_id=1, source_target_pairs={{0,2},{2,0},{1,3},{3,1},{4,6},{6,4},{5,7},{7,5},{8,10},{10,8},{9,1... | collective-permute-start | bytes 442376 | tf_op jit(solution)/shard_map/ppermute | solution.py:31
  12.2 16.4 %collective-permute-start.3 = (bf16[2,64,1152]{2,1,0:T(8,128)(2,1)S(1)}, bf16[2,64,1152]{2,1,0:T(8,128)(2,1)S(1)}, u32[]{:S(2)}, u32[]{:S(2)}) collective-permute-start(bf16[2,64,1152]{2,1,0:T(8,128)(2,1)S(1)} %pad_maximum_fusion.1), channel_id=1, source_target_pairs={{0,2},{2,0},{1,3},{3,1},{4,6},{6,4},{5,7},{7,5},{8,10},{10,8},{9,1... | collective-permute-start | bytes 884744 | tf_op jit(solution)/shard_map/ppermute | solution.py:31
  13.6 6.4 %collective-permute-start.5 = (bf16[64,1152]{1,0:T(8,128)(2,1)S(1)}, bf16[64,1152]{1,0:T(8,128)(2,1)S(1)}, u32[]{:S(2)}, u32[]{:S(2)}) collective-permute-start(bf16[64,1152]{1,0:T(8,128)(2,1)S(1)} %collective-permute-done.2), channel_id=1, source_target_pairs={{0,4},{4,8},{8,12},{12,16},{16,20},{20,24},{24,28},{28,0},{1,5},{5... | collective-permute-start | bytes 442376 | tf_op jit(solution)/shard_map/ppermute | solution.py:36
  13.6 6.4 %collective-permute-start.4 = (bf16[64,1152]{1,0:T(8,128)(2,1)S(1)}, bf16[64,1152]{1,0:T(8,128)(2,1)S(1)}, u32[]{:S(2)}, u32[]{:S(2)}) collective-permute-start(bf16[64,1152]{1,0:T(8,128)(2,1)S(1)} %collective-permute-done.1), channel_id=1, source_target_pairs={{0,28},{4,0},{8,4},{12,8},{16,12},{20,16},{24,20},{28,24},{1,29},{... | collective-permute-start | bytes 442376 | tf_op jit(solution)/shard_map/ppermute | solution.py:36
  19.9 6.4 %collective-permute-start.8 = (bf16[64,1152]{1,0:T(8,128)(2,1)S(1)}, bf16[64,1152]{1,0:T(8,128)(2,1)S(1)}, u32[]{:S(2)}, u32[]{:S(2)}) collective-permute-start(bf16[64,1152]{1,0:T(8,128)(2,1)S(1)} %collective-permute-done.5), channel_id=1, source_target_pairs={{0,4},{4,8},{8,12},{12,16},{16,20},{20,24},{24,28},{28,0},{1,5},{5... | collective-permute-start | bytes 442376 | tf_op jit(solution)/shard_map/ppermute | solution.py:36
  19.9 6.4 %collective-permute-start.7 = (bf16[64,1152]{1,0:T(8,128)(2,1)S(1)}, bf16[64,1152]{1,0:T(8,128)(2,1)S(1)}, u32[]{:S(2)}, u32[]{:S(2)}) collective-permute-start(bf16[64,1152]{1,0:T(8,128)(2,1)S(1)} %collective-permute-done.4), channel_id=1, source_target_pairs={{0,28},{4,0},{8,4},{12,8},{16,12},{20,16},{24,20},{28,24},{1,29},{... | collective-permute-start | bytes 442376 | tf_op jit(solution)/shard_map/ppermute | solution.py:36
  23.2 11.6 %collective-permute-start.6 = (bf16[2,64,1152]{2,1,0:T(8,128)(2,1)S(1)}, bf16[2,64,1152]{2,1,0:T(8,128)(2,1)S(1)}, u32[]{:S(2)}, u32[]{:S(2)}) collective-permute-start(bf16[2,64,1152]{2,1,0:T(8,128)(2,1)S(1)} %pad_maximum_fusion.2), channel_id=1, source_target_pairs={{0,2},{2,0},{1,3},{3,1},{4,6},{6,4},{5,7},{7,5},{8,10},{10,8},{9,1... | collective-permute-start | bytes 884744 | tf_op jit(solution)/shard_map/ppermute | solution.py:31
  26.3 11.1 %collective-permute-start.9 = (bf16[2,64,1152]{2,1,0:T(8,128)(2,1)S(1)}, bf16[2,64,1152]{2,1,0:T(8,128)(2,1)S(1)}, u32[]{:S(2)}, u32[]{:S(2)}) collective-permute-start(bf16[2,64,1152]{2,1,0:T(8,128)(2,1)S(1)} %pad_maximum_fusion.3), channel_id=1, source_target_pairs={{0,2},{2,0},{1,3},{3,1},{4,6},{6,4},{5,7},{7,5},{8,10},{10,8},{9,1... | collective-permute-start | bytes 884744 | tf_op jit(solution)/shard_map/ppermute | solution.py:31
  27.2 6.4 %collective-permute-start.10 = (bf16[64,1152]{1,0:T(8,128)(2,1)S(1)}, bf16[64,1152]{1,0:T(8,128)(2,1)S(1)}, u32[]{:S(2)}, u32[]{:S(2)}) collective-permute-start(bf16[64,1152]{1,0:T(8,128)(2,1)S(1)} %collective-permute-done.8), channel_id=1, source_target_pairs={{0,4},{4,8},{8,12},{12,16},{16,20},{20,24},{24,28},{28,0},{1,5},{5... | collective-permute-start | bytes 442376 | tf_op jit(solution)/shard_map/ppermute | solution.py:36
  33.5 5.4 %collective-permute-start.11 = (bf16[1,64,1152]{2,1,0:T(8,128)(2,1)S(1)}, bf16[1,64,1152]{2,1,0:T(8,128)(2,1)S(1)}, u32[]{:S(2)}, u32[]{:S(2)}) collective-permute-start(bf16[1,64,1152]{2,1,0:T(8,128)(2,1)S(1)} %bitcast.101), channel_id=1, source_target_pairs={{0,2},{2,0},{1,3},{3,1},{4,6},{6,4},{5,7},{7,5},{8,10},{10,8},{9,1... | collective-permute-start | bytes 442376 | tf_op jit(solution)/shard_map/ppermute | solution.py:31
  34.8 10.1 %copy-start.11 = (bf16[10,64,1152]{2,1,0:T(8,128)(2,1)}, bf16[10,64,1152]{2,1,0:T(8,128)(2,1)S(1)}, u32[]{:S(2)}) copy-start(bf16[10,64,1152]{2,1,0:T(8,128)(2,1)S(1)} %constant_dynamic-update-slice_fusion.refs_0_) | copy-start | bytes 4423684
  34.8 16.2 %collective-permute-start.12 = (bf16[10,64,1152]{2,1,0:T(8,128)(2,1)S(1)}, bf16[10,64,1152]{2,1,0:T(8,128)(2,1)}, u32[]{:S(2)}, u32[]{:S(2)}) collective-permute-start(bf16[10,64,1152]{2,1,0:T(8,128)(2,1)S(1)} %constant_dynamic-update-slice_fusion.refs_0_), channel_id=1, source_target_pairs={{0,1},{1,0},{2,3},{3,2},{4,5},{5,4},{6,7},{7,6},{8,9},{9,8},{10,11... | collective-permute-start | bytes 4423688 | tf_op jit(solution)/shard_map/ppermute | solution.py:31
  37.4 7.5 %copy-start.8 = (bf16[1,128,8,64]{1,3,2,0:T(8,128)(2,1)S(1)}, bf16[1,128,8,64]{1,3,2,0:T(8,128)(2,1)}, u32[]{:S(2)}) copy-start(bf16[1,128,8,64]{1,3,2,0:T(8,128)(2,1)} %param.13) | copy-start | bytes 393220
  39.0 12.0 %copy-start.10 = (bf16[6,64,1152]{2,1,0:T(8,128)(2,1)}, bf16[6,64,1152]{2,1,0:T(8,128)(2,1)S(1)}, u32[]{:S(2)}) copy-start(bf16[6,64,1152]{2,1,0:T(8,128)(2,1)S(1)} %constant_dynamic-update-slice_fusion.8.refs_1_) | copy-start | bytes 2654212
  39.0 12.0 %collective-permute-start.13 = (bf16[6,64,1152]{2,1,0:T(8,128)(2,1)S(1)}, bf16[6,64,1152]{2,1,0:T(8,128)(2,1)S(1)}, u32[]{:S(2)}, u32[]{:S(2)}) collective-permute-start(bf16[6,64,1152]{2,1,0:T(8,128)(2,1)S(1)} %constant_dynamic-update-slice_fusion.8.refs_1_), channel_id=1, source_target_pairs={{0,1},{1,0},{2,3},{3,2},{4,5},{5,4},{6,7},{7,6},{8,9},{9,8},{10,11... | collective-permute-start | bytes 2654216 | tf_op jit(solution)/shard_map/ppermute | solution.py:31
  51.0 0.9 copy-start.13
  74.6 18.7 %collective-permute-start.14 = (bf16[16,64,1408]{2,1,0:T(8,128)(2,1)}, bf16[16,64,1408]{2,1,0:T(8,128)(2,1)S(1)}, u32[]{:S(2)}, u32[]{:S(2)}) collective-permute-start(bf16[16,64,1408]{2,1,0:T(8,128)(2,1)} %get-tuple-element.24), channel_id=1, source_target_pairs={{0,1},{1,0},{2,3},{3,2},{4,5},{5,4},{6,7},{7,6},{8,9},{9,8},{10,11... | collective-permute-start | bytes 8650760 | tf_op jit(solution)/shard_map/ppermute | solution.py:31
  93.3 20.5 %copy-start.1 = (bf16[16,64,1408]{2,1,0:T(8,128)(2,1)S(1)}, bf16[16,64,1408]{2,1,0:T(8,128)(2,1)}, u32[]{:S(2)}) copy-start(bf16[16,64,1408]{2,1,0:T(8,128)(2,1)} %get-tuple-element.23) | copy-start | bytes 8650756
  94.5 19.4 %collective-permute-start.18 = (bf16[1,64,1408]{2,1,0:T(8,128)(2,1)S(1)}, bf16[1,64,1408]{2,1,0:T(8,128)(2,1)S(1)}, u32[]{:S(2)}, u32[]{:S(2)}) collective-permute-start(bf16[1,64,1408]{2,1,0:T(8,128)(2,1)S(1)} %add_convert_fusion.5), channel_id=1, source_target_pairs={{0,2},{2,0},{1,3},{3,1},{4,6},{6,4},{5,7},{7,5},{8,10},{10,8},{9,1... | collective-permute-start | bytes 540680 | tf_op jit(solution)/shard_map/ppermute | solution.py:31
  109.5 12.1 %collective-permute-start.17 = (bf16[2,64,1408]{2,1,0:T(8,128)(2,1)S(1)}, bf16[2,64,1408]{2,1,0:T(8,128)(2,1)S(1)}, u32[]{:S(2)}, u32[]{:S(2)}) collective-permute-start(bf16[2,64,1408]{2,1,0:T(8,128)(2,1)S(1)} %add_convert_fusion.2), channel_id=1, source_target_pairs={{0,2},{2,0},{1,3},{3,1},{4,6},{6,4},{5,7},{7,5},{8,10},{10,8},{9,1... | collective-permute-start | bytes 1081352 | tf_op jit(solution)/shard_map/ppermute | solution.py:31
  110.8 33.1 %collective-permute-start.15 = (bf16[3,64,1408]{2,1,0:T(8,128)(2,1)S(1)}, bf16[3,64,1408]{2,1,0:T(8,128)(2,1)S(1)}, u32[]{:S(2)}, u32[]{:S(2)}) collective-permute-start(bf16[3,64,1408]{2,1,0:T(8,128)(2,1)S(1)} %add_convert_fusion.1), channel_id=1, source_target_pairs={{0,2},{2,0},{1,3},{3,1},{4,6},{6,4},{5,7},{7,5},{8,10},{10,8},{9,1... | collective-permute-start | bytes 1622024 | tf_op jit(solution)/shard_map/ppermute | solution.py:31
  114.0 10.1 %collective-permute-start.19 = (bf16[64,1408]{1,0:T(8,128)(2,1)S(1)}, bf16[64,1408]{1,0:T(8,128)(2,1)S(1)}, u32[]{:S(2)}, u32[]{:S(2)}) collective-permute-start(bf16[64,1408]{1,0:T(8,128)(2,1)S(1)} %fusion.13), channel_id=1, source_target_pairs={{0,4},{4,8},{8,12},{12,16},{16,20},{20,24},{24,28},{28,0},{1,5},{5... | collective-permute-start | bytes 540680 | tf_op jit(solution)/shard_map/ppermute | solution.py:36
  121.8 18.6 %collective-permute-start.23 = (bf16[64,1408]{1,0:T(8,128)(2,1)S(1)}, bf16[64,1408]{1,0:T(8,128)(2,1)S(1)}, u32[]{:S(2)}, u32[]{:S(2)}) collective-permute-start(bf16[64,1408]{1,0:T(8,128)(2,1)S(1)} %fusion.14), channel_id=1, source_target_pairs={{0,28},{4,0},{8,4},{12,8},{16,12},{20,16},{24,20},{28,24},{1,29},{... | collective-permute-start | bytes 540680 | tf_op jit(solution)/shard_map/ppermute | solution.py:36
  121.9 18.4 %collective-permute-start.16 = (bf16[2,64,1408]{2,1,0:T(8,128)(2,1)S(1)}, bf16[2,64,1408]{2,1,0:T(8,128)(2,1)S(1)}, u32[]{:S(2)}, u32[]{:S(2)}) collective-permute-start(bf16[2,64,1408]{2,1,0:T(8,128)(2,1)S(1)} %get-tuple-element.37), channel_id=1, source_target_pairs={{0,2},{2,0},{1,3},{3,1},{4,6},{6,4},{5,7},{7,5},{8,10},{10,8},{9,1... | collective-permute-start | bytes 1081352 | tf_op jit(solution)/shard_map/ppermute | solution.py:31
  124.1 16.4 %collective-permute-start.20 = (bf16[64,1408]{1,0:T(8,128)(2,1)S(1)}, bf16[64,1408]{1,0:T(8,128)(2,1)S(1)}, u32[]{:S(2)}, u32[]{:S(2)}) collective-permute-start(bf16[64,1408]{1,0:T(8,128)(2,1)S(1)} %fusion.5), channel_id=1, source_target_pairs={{0,4},{4,8},{8,12},{12,16},{16,20},{20,24},{24,28},{28,0},{1,5},{5... | collective-permute-start | bytes 540680 | tf_op jit(solution)/shard_map/ppermute | solution.py:36
  140.6 7.3 %collective-permute-start.21 = (bf16[64,1408]{1,0:T(8,128)(2,1)S(1)}, bf16[64,1408]{1,0:T(8,128)(2,1)S(1)}, u32[]{:S(2)}, u32[]{:S(2)}) collective-permute-start(bf16[64,1408]{1,0:T(8,128)(2,1)S(1)} %get-tuple-element.40), channel_id=1, source_target_pairs={{0,4},{4,8},{8,12},{12,16},{16,20},{20,24},{24,28},{28,0},{1,5},{5... | collective-permute-start | bytes 540680 | tf_op jit(solution)/shard_map/ppermute | solution.py:36
  140.7 7.7 %collective-permute-start.24 = (bf16[64,1408]{1,0:T(8,128)(2,1)S(1)}, bf16[64,1408]{1,0:T(8,128)(2,1)S(1)}, u32[]{:S(2)}, u32[]{:S(2)}) collective-permute-start(bf16[64,1408]{1,0:T(8,128)(2,1)S(1)} %get-tuple-element.41), channel_id=1, source_target_pairs={{0,28},{4,0},{8,4},{12,8},{16,12},{20,16},{24,20},{28,24},{1,29},{... | collective-permute-start | bytes 540680 | tf_op jit(solution)/shard_map/ppermute | solution.py:36
  148.5 6.8 %collective-permute-start.22 = (bf16[64,1408]{1,0:T(8,128)(2,1)S(1)}, bf16[64,1408]{1,0:T(8,128)(2,1)S(1)}, u32[]{:S(2)}, u32[]{:S(2)}) collective-permute-start(bf16[64,1408]{1,0:T(8,128)(2,1)S(1)} %get-tuple-element.38), channel_id=1, source_target_pairs={{0,4},{4,8},{8,12},{12,16},{16,20},{20,24},{24,28},{28,0},{1,5},{5... | collective-permute-start | bytes 540680 | tf_op jit(solution)/shard_map/ppermute | solution.py:36
  151.2 6.5 %collective-permute-start.25 = (bf16[64,1408]{1,0:T(8,128)(2,1)S(1)}, bf16[64,1408]{1,0:T(8,128)(2,1)S(1)}, u32[]{:S(2)}, u32[]{:S(2)}) collective-permute-start(bf16[64,1408]{1,0:T(8,128)(2,1)S(1)} %get-tuple-element.39), channel_id=1, source_target_pairs={{0,28},{4,0},{8,4},{12,8},{16,12},{20,16},{24,20},{28,24},{1,29},{... | collective-permute-start | bytes 540680 | tf_op jit(solution)/shard_map/ppermute | solution.py:36
  157.8 7.1 %collective-permute-start.26 = (bf16[64,1408]{1,0:T(8,128)(2,1)S(1)}, bf16[64,1408]{1,0:T(8,128)(2,1)S(1)}, u32[]{:S(2)}, u32[]{:S(2)}) collective-permute-start(bf16[64,1408]{1,0:T(8,128)(2,1)S(1)} %fusion.12), channel_id=1, source_target_pairs={{0,128},{128,0},{1,129},{129,1},{2,130},{130,2},{3,131},{131,3},{4... | collective-permute-start | bytes 540680 | tf_op jit(solution)/shard_map/ppermute | solution.py:31
  164.9 16.5 %copy-start.2 = (bf16[2,64,1408]{2,1,0:T(8,128)(2,1)}, bf16[2,64,1408]{2,1,0:T(8,128)(2,1)S(1)}, u32[]{:S(2)}) copy-start(bf16[2,64,1408]{2,1,0:T(8,128)(2,1)S(1)} %pad_maximum_fusion.refs_0_) | copy-start | bytes 1081348
  164.9 9.3 %collective-permute-start.28 = (bf16[2,64,1408]{2,1,0:T(8,128)(2,1)S(1)}, bf16[2,64,1408]{2,1,0:T(8,128)(2,1)S(1)}, u32[]{:S(2)}, u32[]{:S(2)}) collective-permute-start(bf16[2,64,1408]{2,1,0:T(8,128)(2,1)S(1)} %pad_maximum_fusion.refs_0_), channel_id=1, source_target_pairs={{0,32},{32,64},{64,96},{96,0},{1,33},{33,65},{65,97},{97,1},{2,34}... | collective-permute-start | bytes 1081352 | tf_op jit(solution)/shard_map/ppermute | solution.py:36
  166.5 9.4 %collective-permute-start.27 = (bf16[2,64,1408]{2,1,0:T(8,128)(2,1)S(1)}, bf16[2,64,1408]{2,1,0:T(8,128)(2,1)S(1)}, u32[]{:S(2)}, u32[]{:S(2)}) collective-permute-start(bf16[2,64,1408]{2,1,0:T(8,128)(2,1)S(1)} %pad_maximum_fusion.refs_0_), channel_id=1, source_target_pairs={{0,96},{32,0},{64,32},{96,64},{1,97},{33,1},{65,33},{97,65},{2,98}... | collective-permute-start | bytes 1081352 | tf_op jit(solution)/shard_map/ppermute | solution.py:36
  174.3 7.2 %copy-start.3 = (bf16[2,64,1408]{2,1,0:T(8,128)(2,1)}, bf16[2,64,1408]{2,1,0:T(8,128)(2,1)S(1)}, u32[]{:S(2)}) copy-start(bf16[2,64,1408]{2,1,0:T(8,128)(2,1)S(1)} %collective-permute-done.28.refs_2_) | copy-start | bytes 1081348
  174.3 6.8 %collective-permute-start.29 = (bf16[1,64,1408]{2,1,0:T(8,128)(2,1)S(1)}, bf16[1,64,1408]{2,1,0:T(8,128)(2,1)S(1)}, u32[]{:S(2)}, u32[]{:S(2)}) collective-permute-start(bf16[1,64,1408]{2,1,0:T(8,128)(2,1)S(1)} %slice.169), channel_id=1, source_target_pairs={{0,32},{32,64},{64,96},{96,0},{1,33},{33,65},{65,97},{97,1},{2,34}... | collective-permute-start | bytes 540680 | tf_op jit(solution)/shard_map/ppermute | solution.py:36
  175.9 5.6 %copy-start.4 = (bf16[2,64,1408]{2,1,0:T(8,128)(2,1)}, bf16[2,64,1408]{2,1,0:T(8,128)(2,1)S(1)}, u32[]{:S(2)}) copy-start(bf16[2,64,1408]{2,1,0:T(8,128)(2,1)S(1)} %collective-permute-done.27.refs_1_) | copy-start | bytes 1081348
  175.9 5.6 %collective-permute-start.30 = (bf16[1,64,1408]{2,1,0:T(8,128)(2,1)S(1)}, bf16[1,64,1408]{2,1,0:T(8,128)(2,1)S(1)}, u32[]{:S(2)}, u32[]{:S(2)}) collective-permute-start(bf16[1,64,1408]{2,1,0:T(8,128)(2,1)S(1)} %slice.170), channel_id=1, source_target_pairs={{0,96},{32,0},{64,32},{96,64},{1,97},{33,1},{65,33},{97,65},{2,98}... | collective-permute-start | bytes 540680 | tf_op jit(solution)/shard_map/ppermute | solution.py:36
  181.1 0.7 copy-start.6
  181.7 0.7 copy-start.7
  187.8 2.3 %collective-permute-start.31 = (bf16[16,32,576]{2,1,0:T(8,128)(2,1)}, bf16[16,32,576]{2,1,0:T(8,128)(2,1)S(1)}, u32[]{:S(2)}, u32[]{:S(2)}) collective-permute-start(bf16[16,32,576]{2,1,0:T(8,128)(2,1)} %get-tuple-element.28), channel_id=1, source_target_pairs={{0,1},{1,0},{2,3},{3,2},{4,5},{5,4},{6,7},{7,6},{8,9},{9,8},{10,11... | collective-permute-start | bytes 1769480 | tf_op jit(solution)/shard_map/ppermute | solution.py:31
  190.1 24.5 %copy-start.5 = (bf16[1024,64]{1,0:T(8,128)(2,1)S(1)}, bf16[1024,64]{1,0:T(8,128)(2,1)}, u32[]{:S(2)}) copy-start(bf16[1024,64]{1,0:T(8,128)(2,1)} %get-tuple-element.22) | copy-start | bytes 393220
  190.1 25.3 %copy-start.9 = (bf16[128,64]{1,0:T(8,128)(2,1)S(1)}, bf16[128,64]{1,0:T(8,128)(2,1)}, u32[]{:S(2)}) copy-start(bf16[128,64]{1,0:T(8,128)(2,1)} %get-tuple-element.26) | copy-start | bytes 49156
  191.4 24.8 %copy-start.12 = (f32[2,8,128]{2,1,0:T(8,128)S(1)}, f32[2,8,128]{2,1,0:T(8,128)}, u32[]{:S(2)}) copy-start(f32[2,8,128]{2,1,0:T(8,128)} %get-tuple-element.29) | copy-start | bytes 24580
  191.4 5.8 %collective-permute-start.32 = (bf16[2,32,576]{2,1,0:T(8,128)(2,1)S(1)}, bf16[2,32,576]{2,1,0:T(8,128)(2,1)S(1)}, u32[]{:S(2)}, u32[]{:S(2)}) collective-permute-start(bf16[2,32,576]{2,1,0:T(8,128)(2,1)S(1)} %get-tuple-element.44), channel_id=1, source_target_pairs={{0,4},{4,8},{8,12},{12,16},{16,20},{20,24},{24,28},{28,0},{1,5},{5... | collective-permute-start | bytes 221192 | tf_op jit(solution)/shard_map/ppermute | solution.py:36
  197.2 5.7 %collective-permute-start.33 = (bf16[2,32,576]{2,1,0:T(8,128)(2,1)S(1)}, bf16[2,32,576]{2,1,0:T(8,128)(2,1)S(1)}, u32[]{:S(2)}, u32[]{:S(2)}) collective-permute-start(bf16[2,32,576]{2,1,0:T(8,128)(2,1)S(1)} %add_convert_fusion.10), channel_id=1, source_target_pairs={{0,4},{4,8},{8,12},{12,16},{16,20},{20,24},{24,28},{28,0},{1,5},{5... | collective-permute-start | bytes 221192 | tf_op jit(solution)/shard_map/ppermute | solution.py:36
  199.3 4.7 %collective-permute-start.36 = (bf16[2,32,576]{2,1,0:T(8,128)(2,1)S(1)}, bf16[2,32,576]{2,1,0:T(8,128)(2,1)S(1)}, u32[]{:S(2)}, u32[]{:S(2)}) collective-permute-start(bf16[2,32,576]{2,1,0:T(8,128)(2,1)S(1)} %get-tuple-element.45), channel_id=1, source_target_pairs={{0,28},{4,0},{8,4},{12,8},{16,12},{20,16},{24,20},{28,24},{1,29},{... | collective-permute-start | bytes 221192 | tf_op jit(solution)/shard_map/ppermute | solution.py:36
  203.0 5.7 %collective-permute-start.34 = (bf16[2,32,576]{2,1,0:T(8,128)(2,1)S(1)}, bf16[2,32,576]{2,1,0:T(8,128)(2,1)S(1)}, u32[]{:S(2)}, u32[]{:S(2)}) collective-permute-start(bf16[2,32,576]{2,1,0:T(8,128)(2,1)S(1)} %add_convert_fusion.9), channel_id=1, source_target_pairs={{0,4},{4,8},{8,12},{12,16},{16,20},{20,24},{24,28},{28,0},{1,5},{5... | collective-permute-start | bytes 221192 | tf_op jit(solution)/shard_map/ppermute | solution.py:36
  208.7 4.8 %collective-permute-start.37 = (bf16[2,32,576]{2,1,0:T(8,128)(2,1)S(1)}, bf16[2,32,576]{2,1,0:T(8,128)(2,1)S(1)}, u32[]{:S(2)}, u32[]{:S(2)}) collective-permute-start(bf16[2,32,576]{2,1,0:T(8,128)(2,1)S(1)} %get-tuple-element.43), channel_id=1, source_target_pairs={{0,28},{4,0},{8,4},{12,8},{16,12},{20,16},{24,20},{28,24},{1,29},{... | collective-permute-start | bytes 221192 | tf_op jit(solution)/shard_map/ppermute | solution.py:36
  208.8 7.9 %collective-permute-start.35 = (bf16[2,32,576]{2,1,0:T(8,128)(2,1)S(1)}, bf16[2,32,576]{2,1,0:T(8,128)(2,1)S(1)}, u32[]{:S(2)}, u32[]{:S(2)}) collective-permute-start(bf16[2,32,576]{2,1,0:T(8,128)(2,1)S(1)} %get-tuple-element.42), channel_id=1, source_target_pairs={{0,4},{4,8},{8,12},{12,16},{16,20},{20,24},{24,28},{28,0},{1,5},{5... | collective-permute-start | bytes 221192 | tf_op jit(solution)/shard_map/ppermute | solution.py:36
  213.6 4.5 %collective-permute-start.38 = (bf16[2,32,576]{2,1,0:T(8,128)(2,1)S(1)}, bf16[2,32,576]{2,1,0:T(8,128)(2,1)S(1)}, u32[]{:S(2)}, u32[]{:S(2)}) collective-permute-start(bf16[2,32,576]{2,1,0:T(8,128)(2,1)S(1)} %add_convert_fusion.6), channel_id=1, source_target_pairs={{0,28},{4,0},{8,4},{12,8},{16,12},{20,16},{24,20},{28,24},{1,29},{... | collective-permute-start | bytes 221192 | tf_op jit(solution)/shard_map/ppermute | solution.py:36
  218.1 4.1 %collective-permute-start.39 = (bf16[32,576]{1,0:T(8,128)(2,1)S(1)}, bf16[32,576]{1,0:T(8,128)(2,1)S(1)}, u32[]{:S(2)}, u32[]{:S(2)}) collective-permute-start(bf16[32,576]{1,0:T(8,128)(2,1)S(1)} %fusion.15), channel_id=1, source_target_pairs={{0,2},{2,0},{1,3},{3,1},{4,6},{6,4},{5,7},{7,5},{8,10},{10,8},{9,1... | collective-permute-start | bytes 110600 | tf_op jit(solution)/shard_map/ppermute | solution.py:31

commit v3 on v2

--- a/solution.py
+++ b/solution.py
@@ -1,3 +1,4 @@
+import functools
 import math
 
 import jax
@@ -11,6 +12,7 @@
 softmax_scale = 1.0 / math.sqrt(192.0)
 log2e = 1.0 / math.log(2.0)
 TILE = 256
+FIRST = 6
 N_DP = 8
 N_CTX = 32
 
@@ -57,7 +59,7 @@
 def batches():
     n = N_CTX // 4
     far = [[n // 2]] + [[k, n - k] for k in range(n // 2 - 1, 0, -1)]
-    return far[:-1] + [far[-1] + [0]]
+    return far + [[0]]
 
 
 def fill_owners(table, me):
@@ -209,7 +211,7 @@
 
     def kernel(me_ref, blocks_ref, *refs):
         piece_refs, refs = refs[:n], refs[n:]
-        q_ref, g_ref, delta_ref, v_ref, dq_ref, dqr_ref, near_ref, far_ref, *refs = refs
+        q_ref, g_ref, delta_ref, v_ref, dq_ref, dqr_ref, near_ref, first_ref, rest_ref, *refs = refs
         keys_ref, table, scores, dk_acc, dq_acc = refs
         me = [me_ref[i] for i in range(4)]
         zero_pad = jnp.zeros((half, wide - cols), bf16)
@@ -288,25 +290,28 @@
         lax.fori_loop(0, 2, block_step, 0)
         fill_owners(table, me)
 
-        def unsort_step(j, carry):
-            for core, out in enumerate((near_ref, far_ref)):
+        def unsort_step(j, carry, far_ref, start):
+            for core, out, k in ((0, near_ref, j), (1, far_ref, j - start)):
                 owner = table[core * 2 * n_z + j]
                 for side in range(2):
                     place = blocks_ref[2 * owner + side]
                     at = pl.ds(pl.multiple_of(place * half, half), half)
                     part = jnp.where(place // per <= top, dk_acc[at, :], 0.0).astype(bf16)
-                    out[j, :, side * latent : (side + 1) * latent] = part[:, :latent]
-                    start = 2 * latent + side * rope
-                    out[j, :, start : start + rope] = part[:, latent:cols]
-                out[j, :, packed:] = v_ref[core * 2 * n_z + j]
+                    out[k, :, side * latent : (side + 1) * latent] = part[:, :latent]
+                    column = 2 * latent + side * rope
+                    out[k, :, column : column + rope] = part[:, latent:cols]
+                out[k, :, packed:] = v_ref[core * 2 * n_z + j]
             return carry
 
-        lax.fori_loop(0, 2 * n_z, unsort_step, 0)
-
-    dk_shape = ((2 * n_z, half, packed + extra), bf16)
+        for far_ref, start, stop in ((first_ref, 0, FIRST), (rest_ref, FIRST, 2 * n_z)):
+            lax.fori_loop(
+                start, stop, functools.partial(unsort_step, far_ref=far_ref, start=start), 0
+            )
+
+    dk_shapes = [((k, half, packed + extra), bf16) for k in (2 * n_z, FIRST, 2 * n_z - FIRST)]
     return call(
         kernel,
-        [((rows, latent), bf16), ((rows, rope), bf16), dk_shape, dk_shape],
+        [((rows, latent), bf16), ((rows, rope), bf16), *dk_shapes],
         2,
         (me, blocks, *pieces, queries, grads, delta, values),
         [
@@ -328,6 +333,7 @@
     n = len(pieces)
     each = width // N_CTX
     room = -(-each // 16) * 16
+    n_z = N_CTX // 4
     f32, bf16 = jnp.float32, jnp.bfloat16
     lanes = packed - 2 * cols
     n_x = N_DP // 2
@@ -366,7 +372,7 @@
 
         def slot_step(slot, carry):
             for core, ref in enumerate((near_ref, far_ref)):
-                owner = owner_at(me, core, slot // 2, slot % 2)
+                owner = owner_at(me, core, lax.rem(slot, n_z), slot // n_z)
                 ref[slot] = placed[owner, :, :cols].astype(bf16)
             return carry
 
@@ -430,21 +436,25 @@
         q_latent.reshape(-1, latent), q_rope.reshape(-1, rope), outputs, d_out[0], w_uv
     )
     values = value_parts(me, outputs, d_out[0])
-    d_q, d_qr, near_dk, far_dk = attention(
+    d_q, d_qr, near_dk, *far_dk = attention(
         me, blocks, pieces, items, queries, grads, delta, values
     )
-    there_dk = swapped(far_dk, "core")
-    sums = {}
+    first_dk = swapped(far_dk[0], "core")
+    rest_dk = swapped(far_dk[1], "core")
+    sums, sent = {}, []
     at = 0
-    for batch in batches():
+    for i, batch in enumerate(batches()):
         n = len(batch)
+        if at == FIRST:
+            rest_dk, *_ = lax.optimization_barrier((rest_dk, *sent))
+        there_dk, start = (first_dk, at) if at < FIRST else (rest_dk, at - FIRST)
         mine, other = (
-            near_dk[k : k + n].astype(wide) + there_dk[k : k + n].astype(wide)
-            for k in (at, at + n)
+            near_dk[at + k : at + k + n].astype(wide)
+            + there_dk[start + k : start + k + n].astype(wide)
+            for k in (0, n)
         )
-        other = other.astype(bf16)
-        other = swapped(other, "ylo")
-        part = mine + other.astype(wide)
+        sent.append(other.astype(bf16))
+        part = mine + swapped(sent[i], "ylo").astype(wide)
         for k, z in enumerate(batch):
             sums[z] = part[k]
         at += 2 * n
@@ -459,10 +469,15 @@
     near_part, far_part, d_lat, d_rope, grad_uv = down_part(
         me, dp_pieces, dp_items, layer_input, latent, rope, heads
     )
-    parts = (near_part.astype(wide) + swapped(far_part, "core").astype(wide)).astype(bf16)
-    parts = parts.reshape(n_z, 2, *parts.shape[1:])
-    part = ring_sum([parts[k] for k in range(n_z)], "z")
-    grad_down = part[0] + swapped(part[1].astype(bf16), "ylo").astype(wide)
+    there_part = swapped(far_part, "core")
+    mine, other = (
+        near_part[k : k + n_z].astype(wide) + there_part[k : k + n_z].astype(wide)
+        for k in (0, n_z)
+    )
+    parts = mine + swapped(other.astype(bf16), "ylo").astype(wide)
+    grad_down = parts[0]
+    for k in range(1, n_z):
+        grad_down = grad_down + shifted(parts[k].astype(bf16), "z", k).astype(wide)
     return (
         d_q.reshape(q_latent.shape),
         d_qr.reshape(q_rope.shape),

time: 224 us -> 221 us (0.987)
  waiting for transfers between devices: 89.3 us -> 78 us
  starting transfers between devices: 80.3 us -> 88 us
    ppermute x25, waiting for transfers between devices: 46.4 us -> 31.2 us  [shifted(): return lax.ppermute(x, axis, [(i, (i + by) % n) for i in range(n)])]
    ppermute x25, starting transfers between devices: 40 us -> 49.3 us  [shifted(): return lax.ppermute(x, axis, [(i, (i + by) % n) for i in range(n)])]
    ppermute x15 -> x17, waiting for transfers between devices: 42.9 us -> 46.8 us  [swapped(): return lax.ppermute(x, axis, [(0, 1), (1, 0)])]
    ppermute x15 -> x17, starting transfers between devices: 40.3 us -> 38.7 us  [swapped(): return lax.ppermute(x, axis, [(0, 1), (1, 0)])]
    convert_element_type x6 -> x5, other arithmetic: 4.74 us -> 4.22 us  [the longest x3 3.15 us: body(): sent.append(other.astype(bf16))]
  transfers between devices with their start and end apart: 40 -> 42, of which waited for: 26 -> 21; matrix products, arithmetic and copies ran while one was open for 3% -> 4% of each run, Pallas kernels for 5% -> 5%
where the time goes in v3:
time: 221 us; the launch traced here: 220 us
  starting transfers between devices  88 us (40%)
  waiting for transfers between devices  78 us (35%)
  Pallas kernels  38.3 us (17%)
  local copies, waits for them, and re-layouts  7.97 us (4%)
  other arithmetic  6.93 us (3%)
    ppermute x25, starting transfers between devices, shifted(): return lax.ppermute(x, axis, [(i, (i + by) % n) for i in range(n)])  49.3 us
    ppermute x17, waiting for transfers between devices, swapped(): return lax.ppermute(x, axis, [(0, 1), (1, 0)])  46.8 us
    ppermute x17, starting transfers between devices, swapped(): return lax.ppermute(x, axis, [(0, 1), (1, 0)])  38.7 us
    pallas_call x5, Pallas kernels, call(): pl.pallas_call(kernel, out_shape=tuple((jax.ShapeDtypeStruct(*o) for o in...  38.3 us
    ppermute x25, waiting for transfers between devices, shifted(): return lax.ppermute(x, axis, [(i, (i + by) % n) for i in range(n)])  31.2 us
    unnamed x44, local copies, waits for them, and re-layouts  7.22 us
  transfers between devices with their start and end apart: 42, of which 21 were waited for; matrix products, arithmetic and copies ran while one was open for 4% of the time, Pallas kernels for 5%

profile of v3, /device:TPU:16, one launch (start us, length us, event | category | flops | bytes accessed | tf_op | source)
XLA Modules:
  0.0 220.2 jit_solution(5751126096527730075)
XLA Ops:
  0.6 0.8 copy.15
  1.5 0.9 copy-done
  2.4 1.9 collective-permute-start.2
  4.4 4.0 %collective-permute-start.1 = (bf16[64,1152]{1,0:T(8,128)(2,1)S(1)}, bf16[64,1152]{1,0:T(8,128)(2,1)S(1)}, u32[]{:S(2)}, u32[]{:S(2)}) collective-permute-start(bf16[64,1152]{1,0:T(8,128)(2,1)S(1)} %shard_map.136), channel_id=1, source_target_pairs={{0,28},{4,0},{8,4},{12,8},{16,12},{20,16},{24,20},{28,24},{1,29},{... | collective-permute-start | bytes 442376 | tf_op jit(solution)/shard_map/ppermute | solution.py:38
  8.4 1.3 collective-permute-start
  9.7 2.5 %collective-permute-done.2 = bf16[64,1152]{1,0:T(8,128)(2,1)S(1)} collective-permute-done((bf16[64,1152]{1,0:T(8,128)(2,1)S(1)}, bf16[64,1152]{1,0:T(8,128)(2,1)S(1)}, u32[]{:S(2)}, u32[]{:S(2)}) %collective-permute-start.2) | collective-permute-done | bytes 147488 | tf_op jit(solution)/shard_map/ppermute | solution.py:38
  12.2 1.4 collective-permute-start.3
  13.6 3.2 %collective-permute-start.4 = (bf16[64,1152]{1,0:T(8,128)(2,1)S(1)}, bf16[64,1152]{1,0:T(8,128)(2,1)S(1)}, u32[]{:S(2)}, u32[]{:S(2)}) collective-permute-start(bf16[64,1152]{1,0:T(8,128)(2,1)S(1)} %collective-permute-done.1), channel_id=1, source_target_pairs={{0,28},{4,0},{8,4},{12,8},{16,12},{20,16},{24,20},{28,24},{1,29},{... | collective-permute-start | bytes 442376 | tf_op jit(solution)/shard_map/ppermute | solution.py:38
  16.9 3.0 %collective-permute-done.5 = bf16[64,1152]{1,0:T(8,128)(2,1)S(1)} collective-permute-done((bf16[64,1152]{1,0:T(8,128)(2,1)S(1)}, bf16[64,1152]{1,0:T(8,128)(2,1)S(1)}, u32[]{:S(2)}, u32[]{:S(2)}) %collective-permute-start.5) | collective-permute-done | bytes 147488 | tf_op jit(solution)/shard_map/ppermute | solution.py:38
  19.9 3.2 %collective-permute-start.7 = (bf16[64,1152]{1,0:T(8,128)(2,1)S(1)}, bf16[64,1152]{1,0:T(8,128)(2,1)S(1)}, u32[]{:S(2)}, u32[]{:S(2)}) collective-permute-start(bf16[64,1152]{1,0:T(8,128)(2,1)S(1)} %collective-permute-done.4), channel_id=1, source_target_pairs={{0,28},{4,0},{8,4},{12,8},{16,12},{20,16},{24,20},{28,24},{1,29},{... | collective-permute-start | bytes 442376 | tf_op jit(solution)/shard_map/ppermute | solution.py:38
  23.2 0.8 collective-permute-start.6
  24.0 2.2 %collective-permute-done.8 = bf16[64,1152]{1,0:T(8,128)(2,1)S(1)} collective-permute-done((bf16[64,1152]{1,0:T(8,128)(2,1)S(1)}, bf16[64,1152]{1,0:T(8,128)(2,1)S(1)}, u32[]{:S(2)}, u32[]{:S(2)}) %collective-permute-start.8) | collective-permute-done | bytes 147488 | tf_op jit(solution)/shard_map/ppermute | solution.py:38
  26.3 0.8 collective-permute-start.9
  27.2 1.4 collective-permute-start.10
  28.7 4.8 %collective-permute-done.10 = bf16[64,1152]{1,0:T(8,128)(2,1)S(1)} collective-permute-done((bf16[64,1152]{1,0:T(8,128)(2,1)S(1)}, bf16[64,1152]{1,0:T(8,128)(2,1)S(1)}, u32[]{:S(2)}, u32[]{:S(2)}) %collective-permute-start.10) | collective-permute-done | bytes 147488 | tf_op jit(solution)/shard_map/ppermute | solution.py:38
  33.5 1.3 collective-permute-start.11
  35.0 2.4 %collective-permute-done.9 = bf16[2,64,1152]{2,1,0:T(8,128)(2,1)S(1)} collective-permute-done((bf16[2,64,1152]{2,1,0:T(8,128)(2,1)S(1)}, bf16[2,64,1152]{2,1,0:T(8,128)(2,1)S(1)}, u32[]{:S(2)}, u32[]{:S(2)}) %collective-permute-start.9) | collective-permute-done | bytes 294944 | tf_op jit(solution)/shard_map/ppermute | solution.py:33
  37.5 1.5 collective-permute-done.11
  39.9 5.0 %shard_map.138.refs_7_ = bf16[32,64,256]{2,1,0:T(8,128)(2,1)} custom-call(s32[6]{0:T(128)} %stack.65.me_ref, bf16[1024,512]{1,0:T(8,128)(2,1)} %bitcast.98, bf16[128,1024]{1,0:T(8,128)(2,1)} %bitcast.100), custom_call_target="tpu_custom_call" | custom-call | flops 1000 | bytes 4194304 | tf_op jit(solution)/shard_map/pallas_call | solution.py:77
  44.9 0.9 copy.16
  45.8 5.2 %shard_map.137 = (bf16[1024,640]{1,0:T(8,128)(2,1)}, bf16[1024,512]{1,0:T(8,128)(2,1)}, f32[2,1,512]{2,1,0:T(1,128)}) custom-call(bf16[1024,512]{1,0:T(8,128)(2,1)} %bitcast.103, bf16[1024,64]{1,0:T(8,128)(2,1)} %bitcast.102, bf16[1024,512]{1,0:T(8,128)(2,1)} %bitcast.99, bf16[128,1024]{1,0:T(8,128)(2,1)} %bitcast.101, bf16[512,1024]{1,0:T(8,128)(2,1)} %w_ref.1), custom_call_target="tpu_custom_call" | custom-call | flops 1000 | bytes 4194304 | tf_op jit(solution)/shard_map/pallas_call | solution.py:77
  51.0 0.9 copy-done.13
  51.9 22.7 %shard_map.139 = (bf16[1024,512]{1,0:T(8,128)(2,1)}, bf16[1024,64]{1,0:T(8,128)(2,1)}, bf16[16,64,1408]{2,1,0:T(8,128)(2,1)}, bf16[6,64,1408]{2,1,0:T(8,128)(2,1)}, bf16[10,64,1408]{2,1,0:T(8,128)(2,1)}) custom-call(s32[6]{0:T(128)} %stack.65.me_ref, s32[64]{0:T(128)} %blocks_ref.1, bf16[10,64,1152]{2,1,0:T(8,128)(2,1)} %copy-done.11, ...), custom_call_target="tpu_custom_call" | custom-call | flops 13421772800 | bytes 4194304 | tf_op jit(solution)/shard_map/pallas_call | solution.py:77
  74.6 13.6 %collective-permute-start.15 = (bf16[6,64,1408]{2,1,0:T(8,128)(2,1)}, bf16[6,64,1408]{2,1,0:T(8,128)(2,1)S(1)}, u32[]{:S(2)}, u32[]{:S(2)}) collective-permute-start(bf16[6,64,1408]{2,1,0:T(8,128)(2,1)} %get-tuple-element.27), channel_id=1, source_target_pairs={{0,1},{1,0},{2,3},{3,2},{4,5},{5,4},{6,7},{7,6},{8,9},{9,8},{10,11... | collective-permute-start | bytes 3244040 | tf_op jit(solution)/shard_map/ppermute | solution.py:33
  88.3 2.4 %collective-permute-done.15 = bf16[6,64,1408]{2,1,0:T(8,128)(2,1)S(1)} collective-permute-done((bf16[6,64,1408]{2,1,0:T(8,128)(2,1)}, bf16[6,64,1408]{2,1,0:T(8,128)(2,1)S(1)}, u32[]{:S(2)}, u32[]{:S(2)}) %collective-permute-start.15) | collective-permute-done | bytes 1081376 | tf_op jit(solution)/shard_map/ppermute | solution.py:33
  90.7 1.0 add_convert_fusion.6
  91.7 14.0 %collective-permute-start.20 = (bf16[1,64,1408]{2,1,0:T(8,128)(2,1)S(1)}, bf16[1,64,1408]{2,1,0:T(8,128)(2,1)S(1)}, u32[]{:S(2)}, u32[]{:S(2)}) collective-permute-start(bf16[1,64,1408]{2,1,0:T(8,128)(2,1)S(1)} %add_convert_fusion.6), channel_id=1, source_target_pairs={{0,2},{2,0},{1,3},{3,1},{4,6},{6,4},{5,7},{7,5},{8,10},{10,8},{9,1... | collective-permute-start | bytes 540680 | tf_op jit(solution)/shard_map/ppermute | solution.py:33
  105.7 1.1 add_convert_fusion.2
  106.9 4.2 %collective-permute-done.20 = bf16[1,64,1408]{2,1,0:T(8,128)(2,1)S(1)} collective-permute-done((bf16[1,64,1408]{2,1,0:T(8,128)(2,1)S(1)}, bf16[1,64,1408]{2,1,0:T(8,128)(2,1)S(1)}, u32[]{:S(2)}, u32[]{:S(2)}) %collective-permute-start.20) | collective-permute-done | bytes 180256 | tf_op jit(solution)/shard_map/ppermute | solution.py:33
  111.1 1.1 add_convert_fusion.5
  112.3 6.0 %collective-permute-done.19 = bf16[2,64,1408]{2,1,0:T(8,128)(2,1)S(1)} collective-permute-done((bf16[2,64,1408]{2,1,0:T(8,128)(2,1)S(1)}, bf16[2,64,1408]{2,1,0:T(8,128)(2,1)S(1)}, u32[]{:S(2)}, u32[]{:S(2)}) %collective-permute-start.19) | collective-permute-done | bytes 360480 | tf_op jit(solution)/shard_map/ppermute | solution.py:33
  118.6 1.8 collective-permute-start.16
  120.8 2.0 collective-permute-start.22
  122.8 9.7 %collective-permute-done.18 = bf16[2,64,1408]{2,1,0:T(8,128)(2,1)S(1)} collective-permute-done((bf16[2,64,1408]{2,1,0:T(8,128)(2,1)S(1)}, bf16[2,64,1408]{2,1,0:T(8,128)(2,1)S(1)}, u32[]{:S(2)}, u32[]{:S(2)}) %collective-permute-start.18) | collective-permute-done | bytes 360480 | tf_op jit(solution)/shard_map/ppermute | solution.py:33
  132.7 1.5 collective-permute-start.17
  134.3 1.7 collective-permute-start.23
  136.0 3.2 %collective-permute-start.26 = (bf16[64,1408]{1,0:T(8,128)(2,1)S(1)}, bf16[64,1408]{1,0:T(8,128)(2,1)S(1)}, u32[]{:S(2)}, u32[]{:S(2)}) collective-permute-start(bf16[64,1408]{1,0:T(8,128)(2,1)S(1)} %get-tuple-element.51), channel_id=1, source_target_pairs={{0,28},{4,0},{8,4},{12,8},{16,12},{20,16},{24,20},{28,24},{1,29},{... | collective-permute-start | bytes 540680 | tf_op jit(solution)/shard_map/ppermute | solution.py:38
  139.2 2.6 %collective-permute-done.17 = bf16[2,64,1408]{2,1,0:T(8,128)(2,1)S(1)} collective-permute-done((bf16[2,64,1408]{2,1,0:T(8,128)(2,1)S(1)}, bf16[2,64,1408]{2,1,0:T(8,128)(2,1)S(1)}, u32[]{:S(2)}, u32[]{:S(2)}) %collective-permute-start.17) | collective-permute-done | bytes 360480 | tf_op jit(solution)/shard_map/ppermute | solution.py:33
  142.6 1.4 collective-permute-start.24
  144.0 3.1 %collective-permute-start.27 = (bf16[64,1408]{1,0:T(8,128)(2,1)S(1)}, bf16[64,1408]{1,0:T(8,128)(2,1)S(1)}, u32[]{:S(2)}, u32[]{:S(2)}) collective-permute-start(bf16[64,1408]{1,0:T(8,128)(2,1)S(1)} %get-tuple-element.49), channel_id=1, source_target_pairs={{0,28},{4,0},{8,4},{12,8},{16,12},{20,16},{24,20},{28,24},{1,29},{... | collective-permute-start | bytes 540680 | tf_op jit(solution)/shard_map/ppermute | solution.py:38
  147.1 3.4 %collective-permute-done.24 = bf16[64,1408]{1,0:T(8,128)(2,1)S(1)} collective-permute-done((bf16[64,1408]{1,0:T(8,128)(2,1)S(1)}, bf16[64,1408]{1,0:T(8,128)(2,1)S(1)}, u32[]{:S(2)}, u32[]{:S(2)}) %collective-permute-start.24) | collective-permute-done | bytes 180256 | tf_op jit(solution)/shard_map/ppermute | solution.py:38
  150.4 0.7 collective-permute-done.27
  151.3 0.7 collective-permute-start.28
  152.0 6.4 %collective-permute-done.28 = bf16[64,1408]{1,0:T(8,128)(2,1)S(1)} collective-permute-done((bf16[64,1408]{1,0:T(8,128)(2,1)S(1)}, bf16[64,1408]{1,0:T(8,128)(2,1)S(1)}, u32[]{:S(2)}, u32[]{:S(2)}) %collective-permute-start.28) | collective-permute-done | bytes 180256 | tf_op jit(solution)/shard_map/ppermute | solution.py:33
  158.4 1.6 collective-permute-start.30
  160.0 1.8 collective-permute-start.29
  161.7 7.3 %collective-permute-done.30.refs_2_ = bf16[2,64,1408]{2,1,0:T(8,128)(2,1)S(1)} collective-permute-done((bf16[2,64,1408]{2,1,0:T(8,128)(2,1)S(1)}, bf16[2,64,1408]{2,1,0:T(8,128)(2,1)S(1)}, u32[]{:S(2)}, u32[]{:S(2)}) %collective-permute-start.30) | collective-permute-done | bytes 360480 | tf_op jit(solution)/shard_map/ppermute | solution.py:38
  169.5 3.0 %collective-permute-start.32 = (bf16[1,64,1408]{2,1,0:T(8,128)(2,1)S(1)}, bf16[1,64,1408]{2,1,0:T(8,128)(2,1)S(1)}, u32[]{:S(2)}, u32[]{:S(2)}) collective-permute-start(bf16[1,64,1408]{2,1,0:T(8,128)(2,1)S(1)} %slice.183), channel_id=1, source_target_pairs={{0,96},{32,0},{64,32},{96,64},{1,97},{33,1},{65,33},{97,65},{2,98}... | collective-permute-start | bytes 540680 | tf_op jit(solution)/shard_map/ppermute | solution.py:38
  172.5 3.4 %collective-permute-done.31.refs_3_ = bf16[1,64,1408]{2,1,0:T(8,128)(2,1)S(1)} collective-permute-done((bf16[1,64,1408]{2,1,0:T(8,128)(2,1)S(1)}, bf16[1,64,1408]{2,1,0:T(8,128)(2,1)S(1)}, u32[]{:S(2)}, u32[]{:S(2)}) %collective-permute-start.31) | collective-permute-done | bytes 180256 | tf_op jit(solution)/shard_map/ppermute | solution.py:38
  176.5 0.7 copy-done.7
  177.2 5.3 %shard_map.140 = (bf16[16,32,576]{2,1,0:T(8,128)(2,1)}, bf16[16,32,576]{2,1,0:T(8,128)(2,1)}, bf16[128,512]{1,0:T(8,128)(2,1)}, bf16[128,64]{1,0:T(8,128)(2,1)}, f32[2,8,128]{2,1,0:T(8,128)}) custom-call(s32[6]{0:T(128)} %stack.65.me_ref, bf16[2,64,1408]{2,1,0:T(8,128)(2,1)} %copy-done.2, bf16[2,64,1408]{2,1,0:T(8,128)(2,1)} %copy-done.4, ...), custom_call_target="tpu_custom_call" | custom-call | flops 1000 | bytes 4194304 | tf_op jit(solution)/shard_map/pallas_call | solution.py:77
  182.5 2.3 %collective-permute-done.33 = bf16[16,32,576]{2,1,0:T(8,128)(2,1)S(1)} collective-permute-done((bf16[16,32,576]{2,1,0:T(8,128)(2,1)}, bf16[16,32,576]{2,1,0:T(8,128)(2,1)S(1)}, u32[]{:S(2)}, u32[]{:S(2)}) %collective-permute-start.33) | collective-permute-done | bytes 589856 | tf_op jit(solution)/shard_map/ppermute | solution.py:33
  184.8 1.1 add_convert_fusion.3
  186.5 9.3 %collective-permute-done.34 = bf16[8,32,576]{2,1,0:T(8,128)(2,1)S(1)} collective-permute-done((bf16[8,32,576]{2,1,0:T(8,128)(2,1)S(1)}, bf16[8,32,576]{2,1,0:T(8,128)(2,1)S(1)}, u32[]{:S(2)}, u32[]{:S(2)}) %collective-permute-start.34) | collective-permute-done | bytes 294944 | tf_op jit(solution)/shard_map/ppermute | solution.py:33
  195.8 1.1 fusion.20
  196.9 4.8 %collective-permute-start.36 = (bf16[32,576]{1,0:T(8,128)(2,1)S(1)}, bf16[32,576]{1,0:T(8,128)(2,1)S(1)}, u32[]{:S(2)}, u32[]{:S(2)}) collective-permute-start(bf16[32,576]{1,0:T(8,128)(2,1)S(1)} %get-tuple-element.57), channel_id=1, source_target_pairs={{0,8},{4,12},{8,16},{12,20},{16,24},{20,28},{24,0},{28,4},{1,9},{5... | collective-permute-start | bytes 110600 | tf_op jit(solution)/shard_map/ppermute | solution.py:38
  201.7 1.7 collective-permute-start.35
  203.4 0.8 copy.17
  204.3 0.7 copy.18
  205.8 2.6 %collective-permute-start.41 = (bf16[32,576]{1,0:T(8,128)(2,1)S(1)}, bf16[32,576]{1,0:T(8,128)(2,1)S(1)}, u32[]{:S(2)}, u32[]{:S(2)}) collective-permute-start(bf16[32,576]{1,0:T(8,128)(2,1)S(1)} %get-tuple-element.53), channel_id=1, source_target_pairs={{0,28},{4,0},{8,4},{12,8},{16,12},{20,16},{24,20},{28,24},{1,29},{... | collective-permute-start | bytes 110600 | tf_op jit(solution)/shard_map/ppermute | solution.py:38
  208.4 2.8 %collective-permute-start.40 = (bf16[32,576]{1,0:T(8,128)(2,1)S(1)}, bf16[32,576]{1,0:T(8,128)(2,1)S(1)}, u32[]{:S(2)}, u32[]{:S(2)}) collective-permute-start(bf16[32,576]{1,0:T(8,128)(2,1)S(1)} %get-tuple-element.54), channel_id=1, source_target_pairs={{0,24},{4,28},{8,0},{12,4},{16,8},{20,12},{24,16},{28,20},{1,25},{... | collective-permute-start | bytes 110600 | tf_op jit(solution)/shard_map/ppermute | solution.py:38
  211.5 4.8 %collective-permute-start.38 = (bf16[32,576]{1,0:T(8,128)(2,1)S(1)}, bf16[32,576]{1,0:T(8,128)(2,1)S(1)}, u32[]{:S(2)}, u32[]{:S(2)}) collective-permute-start(bf16[32,576]{1,0:T(8,128)(2,1)S(1)} %get-tuple-element.56), channel_id=1, source_target_pairs={{0,16},{4,20},{8,24},{12,28},{16,0},{20,4},{24,8},{28,12},{1,17},{... | collective-permute-start | bytes 110600 | tf_op jit(solution)/shard_map/ppermute | solution.py:38
  217.0 2.6 %collective-permute-done.38 = bf16[32,576]{1,0:T(8,128)(2,1)S(1)} collective-permute-done((bf16[32,576]{1,0:T(8,128)(2,1)S(1)}, bf16[32,576]{1,0:T(8,128)(2,1)S(1)}, u32[]{:S(2)}, u32[]{:S(2)}) %collective-permute-start.38) | collective-permute-done | bytes 36896 | tf_op jit(solution)/shard_map/ppermute | solution.py:38
  219.6 0.7 fusion.18
  (95 shorter events, 7.1 us)
Async XLA Ops:
  1.5 0.9 copy-start
  2.4 9.7 %collective-permute-start.2 = (bf16[64,1152]{1,0:T(8,128)(2,1)S(1)}, bf16[64,1152]{1,0:T(8,128)(2,1)S(1)}, u32[]{:S(2)}, u32[]{:S(2)}) collective-permute-start(bf16[64,1152]{1,0:T(8,128)(2,1)S(1)} %shard_map.136), channel_id=1, source_target_pairs={{0,4},{4,8},{8,12},{12,16},{16,20},{20,24},{24,28},{28,0},{1,5},{5... | collective-permute-start | bytes 442376 | tf_op jit(solution)/shard_map/ppermute | solution.py:38
  4.4 7.8 %collective-permute-start.1 = (bf16[64,1152]{1,0:T(8,128)(2,1)S(1)}, bf16[64,1152]{1,0:T(8,128)(2,1)S(1)}, u32[]{:S(2)}, u32[]{:S(2)}) collective-permute-start(bf16[64,1152]{1,0:T(8,128)(2,1)S(1)} %shard_map.136), channel_id=1, source_target_pairs={{0,28},{4,0},{8,4},{12,8},{16,12},{20,16},{24,20},{28,24},{1,29},{... | collective-permute-start | bytes 442376 | tf_op jit(solution)/shard_map/ppermute | solution.py:38
  8.4 8.4 %collective-permute-start = (bf16[1,64,1152]{2,1,0:T(8,128)(2,1)S(1)}, bf16[1,64,1152]{2,1,0:T(8,128)(2,1)S(1)}, u32[]{:S(2)}, u32[]{:S(2)}) collective-permute-start(bf16[1,64,1152]{2,1,0:T(8,128)(2,1)S(1)} %bitcast.95), channel_id=1, source_target_pairs={{0,2},{2,0},{1,3},{3,1},{4,6},{6,4},{5,7},{7,5},{8,10},{10,8},{9,1... | collective-permute-start | bytes 442376 | tf_op jit(solution)/shard_map/ppermute | solution.py:33
  12.2 16.4 %collective-permute-start.3 = (bf16[2,64,1152]{2,1,0:T(8,128)(2,1)S(1)}, bf16[2,64,1152]{2,1,0:T(8,128)(2,1)S(1)}, u32[]{:S(2)}, u32[]{:S(2)}) collective-permute-start(bf16[2,64,1152]{2,1,0:T(8,128)(2,1)S(1)} %pad_maximum_fusion.1), channel_id=1, source_target_pairs={{0,2},{2,0},{1,3},{3,1},{4,6},{6,4},{5,7},{7,5},{8,10},{10,8},{9,1... | collective-permute-start | bytes 884744 | tf_op jit(solution)/shard_map/ppermute | solution.py:33
  13.6 6.4 %collective-permute-start.5 = (bf16[64,1152]{1,0:T(8,128)(2,1)S(1)}, bf16[64,1152]{1,0:T(8,128)(2,1)S(1)}, u32[]{:S(2)}, u32[]{:S(2)}) collective-permute-start(bf16[64,1152]{1,0:T(8,128)(2,1)S(1)} %collective-permute-done.2), channel_id=1, source_target_pairs={{0,4},{4,8},{8,12},{12,16},{16,20},{20,24},{24,28},{28,0},{1,5},{5... | collective-permute-start | bytes 442376 | tf_op jit(solution)/shard_map/ppermute | solution.py:38
  13.6 6.4 %collective-permute-start.4 = (bf16[64,1152]{1,0:T(8,128)(2,1)S(1)}, bf16[64,1152]{1,0:T(8,128)(2,1)S(1)}, u32[]{:S(2)}, u32[]{:S(2)}) collective-permute-start(bf16[64,1152]{1,0:T(8,128)(2,1)S(1)} %collective-permute-done.1), channel_id=1, source_target_pairs={{0,28},{4,0},{8,4},{12,8},{16,12},{20,16},{24,20},{28,24},{1,29},{... | collective-permute-start | bytes 442376 | tf_op jit(solution)/shard_map/ppermute | solution.py:38
  19.9 6.4 %collective-permute-start.8 = (bf16[64,1152]{1,0:T(8,128)(2,1)S(1)}, bf16[64,1152]{1,0:T(8,128)(2,1)S(1)}, u32[]{:S(2)}, u32[]{:S(2)}) collective-permute-start(bf16[64,1152]{1,0:T(8,128)(2,1)S(1)} %collective-permute-done.5), channel_id=1, source_target_pairs={{0,4},{4,8},{8,12},{12,16},{16,20},{20,24},{24,28},{28,0},{1,5},{5... | collective-permute-start | bytes 442376 | tf_op jit(solution)/shard_map/ppermute | solution.py:38
  19.9 6.4 %collective-permute-start.7 = (bf16[64,1152]{1,0:T(8,128)(2,1)S(1)}, bf16[64,1152]{1,0:T(8,128)(2,1)S(1)}, u32[]{:S(2)}, u32[]{:S(2)}) collective-permute-start(bf16[64,1152]{1,0:T(8,128)(2,1)S(1)} %collective-permute-done.4), channel_id=1, source_target_pairs={{0,28},{4,0},{8,4},{12,8},{16,12},{20,16},{24,20},{28,24},{1,29},{... | collective-permute-start | bytes 442376 | tf_op jit(solution)/shard_map/ppermute | solution.py:38
  23.2 11.6 %collective-permute-start.6 = (bf16[2,64,1152]{2,1,0:T(8,128)(2,1)S(1)}, bf16[2,64,1152]{2,1,0:T(8,128)(2,1)S(1)}, u32[]{:S(2)}, u32[]{:S(2)}) collective-permute-start(bf16[2,64,1152]{2,1,0:T(8,128)(2,1)S(1)} %pad_maximum_fusion.2), channel_id=1, source_target_pairs={{0,2},{2,0},{1,3},{3,1},{4,6},{6,4},{5,7},{7,5},{8,10},{10,8},{9,1... | collective-permute-start | bytes 884744 | tf_op jit(solution)/shard_map/ppermute | solution.py:33
  26.3 11.1 %collective-permute-start.9 = (bf16[2,64,1152]{2,1,0:T(8,128)(2,1)S(1)}, bf16[2,64,1152]{2,1,0:T(8,128)(2,1)S(1)}, u32[]{:S(2)}, u32[]{:S(2)}) collective-permute-start(bf16[2,64,1152]{2,1,0:T(8,128)(2,1)S(1)} %pad_maximum_fusion.3), channel_id=1, source_target_pairs={{0,2},{2,0},{1,3},{3,1},{4,6},{6,4},{5,7},{7,5},{8,10},{10,8},{9,1... | collective-permute-start | bytes 884744 | tf_op jit(solution)/shard_map/ppermute | solution.py:33
  27.2 6.4 %collective-permute-start.10 = (bf16[64,1152]{1,0:T(8,128)(2,1)S(1)}, bf16[64,1152]{1,0:T(8,128)(2,1)S(1)}, u32[]{:S(2)}, u32[]{:S(2)}) collective-permute-start(bf16[64,1152]{1,0:T(8,128)(2,1)S(1)} %collective-permute-done.8), channel_id=1, source_target_pairs={{0,4},{4,8},{8,12},{12,16},{16,20},{20,24},{24,28},{28,0},{1,5},{5... | collective-permute-start | bytes 442376 | tf_op jit(solution)/shard_map/ppermute | solution.py:38
  33.5 5.4 %collective-permute-start.11 = (bf16[1,64,1152]{2,1,0:T(8,128)(2,1)S(1)}, bf16[1,64,1152]{2,1,0:T(8,128)(2,1)S(1)}, u32[]{:S(2)}, u32[]{:S(2)}) collective-permute-start(bf16[1,64,1152]{2,1,0:T(8,128)(2,1)S(1)} %bitcast.113), channel_id=1, source_target_pairs={{0,2},{2,0},{1,3},{3,1},{4,6},{6,4},{5,7},{7,5},{8,10},{10,8},{9,1... | collective-permute-start | bytes 442376 | tf_op jit(solution)/shard_map/ppermute | solution.py:33
  34.8 10.1 %copy-start.11 = (bf16[10,64,1152]{2,1,0:T(8,128)(2,1)}, bf16[10,64,1152]{2,1,0:T(8,128)(2,1)S(1)}, u32[]{:S(2)}) copy-start(bf16[10,64,1152]{2,1,0:T(8,128)(2,1)S(1)} %constant_dynamic-update-slice_fusion.refs_0_) | copy-start | bytes 4423684
  34.8 16.1 %collective-permute-start.12 = (bf16[10,64,1152]{2,1,0:T(8,128)(2,1)S(1)}, bf16[10,64,1152]{2,1,0:T(8,128)(2,1)}, u32[]{:S(2)}, u32[]{:S(2)}) collective-permute-start(bf16[10,64,1152]{2,1,0:T(8,128)(2,1)S(1)} %constant_dynamic-update-slice_fusion.refs_0_), channel_id=1, source_target_pairs={{0,1},{1,0},{2,3},{3,2},{4,5},{5,4},{6,7},{7,6},{8,9},{9,8},{10,11... | collective-permute-start | bytes 4423688 | tf_op jit(solution)/shard_map/ppermute | solution.py:33
  37.4 7.5 %copy-start.8 = (bf16[1,128,8,64]{1,3,2,0:T(8,128)(2,1)S(1)}, bf16[1,128,8,64]{1,3,2,0:T(8,128)(2,1)}, u32[]{:S(2)}) copy-start(bf16[1,128,8,64]{1,3,2,0:T(8,128)(2,1)} %param.13) | copy-start | bytes 393220
  39.0 12.0 %copy-start.10 = (bf16[6,64,1152]{2,1,0:T(8,128)(2,1)}, bf16[6,64,1152]{2,1,0:T(8,128)(2,1)S(1)}, u32[]{:S(2)}) copy-start(bf16[6,64,1152]{2,1,0:T(8,128)(2,1)S(1)} %constant_dynamic-update-slice_fusion.8.refs_1_) | copy-start | bytes 2654212
  39.0 12.0 %collective-permute-start.13 = (bf16[6,64,1152]{2,1,0:T(8,128)(2,1)S(1)}, bf16[6,64,1152]{2,1,0:T(8,128)(2,1)S(1)}, u32[]{:S(2)}, u32[]{:S(2)}) collective-permute-start(bf16[6,64,1152]{2,1,0:T(8,128)(2,1)S(1)} %constant_dynamic-update-slice_fusion.8.refs_1_), channel_id=1, source_target_pairs={{0,1},{1,0},{2,3},{3,2},{4,5},{5,4},{6,7},{7,6},{8,9},{9,8},{10,11... | collective-permute-start | bytes 2654216 | tf_op jit(solution)/shard_map/ppermute | solution.py:33
  51.0 0.9 copy-start.13
  74.6 43.7 %copy-start.1 = (bf16[16,64,1408]{2,1,0:T(8,128)(2,1)S(1)}, bf16[16,64,1408]{2,1,0:T(8,128)(2,1)}, u32[]{:S(2)}) copy-start(bf16[16,64,1408]{2,1,0:T(8,128)(2,1)} %get-tuple-element.25) | copy-start | bytes 8650756
  74.6 16.1 %collective-permute-start.15 = (bf16[6,64,1408]{2,1,0:T(8,128)(2,1)}, bf16[6,64,1408]{2,1,0:T(8,128)(2,1)S(1)}, u32[]{:S(2)}, u32[]{:S(2)}) collective-permute-start(bf16[6,64,1408]{2,1,0:T(8,128)(2,1)} %get-tuple-element.27), channel_id=1, source_target_pairs={{0,1},{1,0},{2,3},{3,2},{4,5},{5,4},{6,7},{7,6},{8,9},{9,8},{10,11... | collective-permute-start | bytes 3244040 | tf_op jit(solution)/shard_map/ppermute | solution.py:33
  88.2 18.7 %collective-permute-start.14 = (bf16[10,64,1408]{2,1,0:T(8,128)(2,1)}, bf16[10,64,1408]{2,1,0:T(8,128)(2,1)S(1)}, u32[]{:S(2)}, u32[]{:S(2)}) collective-permute-start(bf16[10,64,1408]{2,1,0:T(8,128)(2,1)} %get-tuple-element.26), channel_id=1, source_target_pairs={{0,1},{1,0},{2,3},{3,2},{4,5},{5,4},{6,7},{7,6},{8,9},{9,8},{10,11... | collective-permute-start | bytes 5406728 | tf_op jit(solution)/shard_map/ppermute | solution.py:33
  91.7 19.4 %collective-permute-start.20 = (bf16[1,64,1408]{2,1,0:T(8,128)(2,1)S(1)}, bf16[1,64,1408]{2,1,0:T(8,128)(2,1)S(1)}, u32[]{:S(2)}, u32[]{:S(2)}) collective-permute-start(bf16[1,64,1408]{2,1,0:T(8,128)(2,1)S(1)} %add_convert_fusion.6), channel_id=1, source_target_pairs={{0,2},{2,0},{1,3},{3,1},{4,6},{6,4},{5,7},{7,5},{8,10},{10,8},{9,1... | collective-permute-start | bytes 540680 | tf_op jit(solution)/shard_map/ppermute | solution.py:33
  106.8 11.5 %collective-permute-start.19 = (bf16[2,64,1408]{2,1,0:T(8,128)(2,1)S(1)}, bf16[2,64,1408]{2,1,0:T(8,128)(2,1)S(1)}, u32[]{:S(2)}, u32[]{:S(2)}) collective-permute-start(bf16[2,64,1408]{2,1,0:T(8,128)(2,1)S(1)} %add_convert_fusion.2), channel_id=1, source_target_pairs={{0,2},{2,0},{1,3},{3,1},{4,6},{6,4},{5,7},{7,5},{8,10},{10,8},{9,1... | collective-permute-start | bytes 1081352 | tf_op jit(solution)/shard_map/ppermute | solution.py:33
  112.2 8.5 %collective-permute-start.21 = (bf16[64,1408]{1,0:T(8,128)(2,1)S(1)}, bf16[64,1408]{1,0:T(8,128)(2,1)S(1)}, u32[]{:S(2)}, u32[]{:S(2)}) collective-permute-start(bf16[64,1408]{1,0:T(8,128)(2,1)S(1)} %get-tuple-element.45), channel_id=1, source_target_pairs={{0,4},{4,8},{8,12},{12,16},{16,20},{20,24},{24,28},{28,0},{1,5},{5... | collective-permute-start | bytes 540680 | tf_op jit(solution)/shard_map/ppermute | solution.py:38
  118.5 15.7 %collective-permute-start.25 = (bf16[64,1408]{1,0:T(8,128)(2,1)S(1)}, bf16[64,1408]{1,0:T(8,128)(2,1)S(1)}, u32[]{:S(2)}, u32[]{:S(2)}) collective-permute-start(bf16[64,1408]{1,0:T(8,128)(2,1)S(1)} %fusion.13), channel_id=1, source_target_pairs={{0,28},{4,0},{8,4},{12,8},{16,12},{20,16},{24,20},{28,24},{1,29},{... | collective-permute-start | bytes 540680 | tf_op jit(solution)/shard_map/ppermute | solution.py:38
  118.6 28.4 %collective-permute-start.16 = (bf16[1,64,1408]{2,1,0:T(8,128)(2,1)S(1)}, bf16[1,64,1408]{2,1,0:T(8,128)(2,1)S(1)}, u32[]{:S(2)}, u32[]{:S(2)}) collective-permute-start(bf16[1,64,1408]{2,1,0:T(8,128)(2,1)S(1)} %get-tuple-element.44), channel_id=1, source_target_pairs={{0,2},{2,0},{1,3},{3,1},{4,6},{6,4},{5,7},{7,5},{8,10},{10,8},{9,1... | collective-permute-start | bytes 540680 | tf_op jit(solution)/shard_map/ppermute | solution.py:33
  120.5 12.0 %collective-permute-start.18 = (bf16[2,64,1408]{2,1,0:T(8,128)(2,1)S(1)}, bf16[2,64,1408]{2,1,0:T(8,128)(2,1)S(1)}, u32[]{:S(2)}, u32[]{:S(2)}) collective-permute-start(bf16[2,64,1408]{2,1,0:T(8,128)(2,1)S(1)} %get-tuple-element.47), channel_id=1, source_target_pairs={{0,2},{2,0},{1,3},{3,1},{4,6},{6,4},{5,7},{7,5},{8,10},{10,8},{9,1... | collective-permute-start | bytes 1081352 | tf_op jit(solution)/shard_map/ppermute | solution.py:33
  120.8 13.4 %collective-permute-start.22 = (bf16[64,1408]{1,0:T(8,128)(2,1)S(1)}, bf16[64,1408]{1,0:T(8,128)(2,1)S(1)}, u32[]{:S(2)}, u32[]{:S(2)}) collective-permute-start(bf16[64,1408]{1,0:T(8,128)(2,1)S(1)} %fusion.5), channel_id=1, source_target_pairs={{0,4},{4,8},{8,12},{12,16},{16,20},{20,24},{24,28},{28,0},{1,5},{5... | collective-permute-start | bytes 540680 | tf_op jit(solution)/shard_map/ppermute | solution.py:38
  132.7 9.1 %collective-permute-start.17 = (bf16[2,64,1408]{2,1,0:T(8,128)(2,1)S(1)}, bf16[2,64,1408]{2,1,0:T(8,128)(2,1)S(1)}, u32[]{:S(2)}, u32[]{:S(2)}) collective-permute-start(bf16[2,64,1408]{2,1,0:T(8,128)(2,1)S(1)} %get-tuple-element.43), channel_id=1, source_target_pairs={{0,2},{2,0},{1,3},{3,1},{4,6},{6,4},{5,7},{7,5},{8,10},{10,8},{9,1... | collective-permute-start | bytes 1081352 | tf_op jit(solution)/shard_map/ppermute | solution.py:33
  134.3 8.3 %collective-permute-start.23 = (bf16[64,1408]{1,0:T(8,128)(2,1)S(1)}, bf16[64,1408]{1,0:T(8,128)(2,1)S(1)}, u32[]{:S(2)}, u32[]{:S(2)}) collective-permute-start(bf16[64,1408]{1,0:T(8,128)(2,1)S(1)} %get-tuple-element.50), channel_id=1, source_target_pairs={{0,4},{4,8},{8,12},{12,16},{16,20},{20,24},{24,28},{28,0},{1,5},{5... | collective-permute-start | bytes 540680 | tf_op jit(solution)/shard_map/ppermute | solution.py:38
  136.0 6.6 %collective-permute-start.26 = (bf16[64,1408]{1,0:T(8,128)(2,1)S(1)}, bf16[64,1408]{1,0:T(8,128)(2,1)S(1)}, u32[]{:S(2)}, u32[]{:S(2)}) collective-permute-start(bf16[64,1408]{1,0:T(8,128)(2,1)S(1)} %get-tuple-element.51), channel_id=1, source_target_pairs={{0,28},{4,0},{8,4},{12,8},{16,12},{20,16},{24,20},{28,24},{1,29},{... | collective-permute-start | bytes 540680 | tf_op jit(solution)/shard_map/ppermute | solution.py:38
  142.6 7.8 %collective-permute-start.24 = (bf16[64,1408]{1,0:T(8,128)(2,1)S(1)}, bf16[64,1408]{1,0:T(8,128)(2,1)S(1)}, u32[]{:S(2)}, u32[]{:S(2)}) collective-permute-start(bf16[64,1408]{1,0:T(8,128)(2,1)S(1)} %get-tuple-element.48), channel_id=1, source_target_pairs={{0,4},{4,8},{8,12},{12,16},{16,20},{20,24},{24,28},{28,0},{1,5},{5... | collective-permute-start | bytes 540680 | tf_op jit(solution)/shard_map/ppermute | solution.py:38
  144.0 7.2 %collective-permute-start.27 = (bf16[64,1408]{1,0:T(8,128)(2,1)S(1)}, bf16[64,1408]{1,0:T(8,128)(2,1)S(1)}, u32[]{:S(2)}, u32[]{:S(2)}) collective-permute-start(bf16[64,1408]{1,0:T(8,128)(2,1)S(1)} %get-tuple-element.49), channel_id=1, source_target_pairs={{0,28},{4,0},{8,4},{12,8},{16,12},{20,16},{24,20},{28,24},{1,29},{... | collective-permute-start | bytes 540680 | tf_op jit(solution)/shard_map/ppermute | solution.py:38
  151.3 7.1 %collective-permute-start.28 = (bf16[64,1408]{1,0:T(8,128)(2,1)S(1)}, bf16[64,1408]{1,0:T(8,128)(2,1)S(1)}, u32[]{:S(2)}, u32[]{:S(2)}) collective-permute-start(bf16[64,1408]{1,0:T(8,128)(2,1)S(1)} %fusion.11), channel_id=1, source_target_pairs={{0,128},{128,0},{1,129},{129,1},{2,130},{130,2},{3,131},{131,3},{4... | collective-permute-start | bytes 540680 | tf_op jit(solution)/shard_map/ppermute | solution.py:33
  158.4 17.5 %copy-start.2 = (bf16[2,64,1408]{2,1,0:T(8,128)(2,1)}, bf16[2,64,1408]{2,1,0:T(8,128)(2,1)S(1)}, u32[]{:S(2)}) copy-start(bf16[2,64,1408]{2,1,0:T(8,128)(2,1)S(1)} %pad_maximum_fusion.refs_0_) | copy-start | bytes 1081348
  158.4 10.6 %collective-permute-start.30 = (bf16[2,64,1408]{2,1,0:T(8,128)(2,1)S(1)}, bf16[2,64,1408]{2,1,0:T(8,128)(2,1)S(1)}, u32[]{:S(2)}, u32[]{:S(2)}) collective-permute-start(bf16[2,64,1408]{2,1,0:T(8,128)(2,1)S(1)} %pad_maximum_fusion.refs_0_), channel_id=1, source_target_pairs={{0,32},{32,64},{64,96},{96,0},{1,33},{33,65},{65,97},{97,1},{2,34}... | collective-permute-start | bytes 1081352 | tf_op jit(solution)/shard_map/ppermute | solution.py:38
  160.0 9.5 %collective-permute-start.29 = (bf16[2,64,1408]{2,1,0:T(8,128)(2,1)S(1)}, bf16[2,64,1408]{2,1,0:T(8,128)(2,1)S(1)}, u32[]{:S(2)}, u32[]{:S(2)}) collective-permute-start(bf16[2,64,1408]{2,1,0:T(8,128)(2,1)S(1)} %pad_maximum_fusion.refs_0_), channel_id=1, source_target_pairs={{0,96},{32,0},{64,32},{96,64},{1,97},{33,1},{65,33},{97,65},{2,98}... | collective-permute-start | bytes 1081352 | tf_op jit(solution)/shard_map/ppermute | solution.py:38
  169.1 6.8 %copy-start.3 = (bf16[2,64,1408]{2,1,0:T(8,128)(2,1)}, bf16[2,64,1408]{2,1,0:T(8,128)(2,1)S(1)}, u32[]{:S(2)}) copy-start(bf16[2,64,1408]{2,1,0:T(8,128)(2,1)S(1)} %collective-permute-done.30.refs_2_) | copy-start | bytes 1081348
  169.1 6.8 %collective-permute-start.31 = (bf16[1,64,1408]{2,1,0:T(8,128)(2,1)S(1)}, bf16[1,64,1408]{2,1,0:T(8,128)(2,1)S(1)}, u32[]{:S(2)}, u32[]{:S(2)}) collective-permute-start(bf16[1,64,1408]{2,1,0:T(8,128)(2,1)S(1)} %slice.182), channel_id=1, source_target_pairs={{0,32},{32,64},{64,96},{96,0},{1,33},{33,65},{65,97},{97,1},{2,34}... | collective-permute-start | bytes 540680 | tf_op jit(solution)/shard_map/ppermute | solution.py:38
  169.4 6.5 %copy-start.4 = (bf16[2,64,1408]{2,1,0:T(8,128)(2,1)}, bf16[2,64,1408]{2,1,0:T(8,128)(2,1)S(1)}, u32[]{:S(2)}) copy-start(bf16[2,64,1408]{2,1,0:T(8,128)(2,1)S(1)} %collective-permute-done.29.refs_1_) | copy-start | bytes 1081348
  169.5 6.4 %collective-permute-start.32 = (bf16[1,64,1408]{2,1,0:T(8,128)(2,1)S(1)}, bf16[1,64,1408]{2,1,0:T(8,128)(2,1)S(1)}, u32[]{:S(2)}, u32[]{:S(2)}) collective-permute-start(bf16[1,64,1408]{2,1,0:T(8,128)(2,1)S(1)} %slice.183), channel_id=1, source_target_pairs={{0,96},{32,0},{64,32},{96,64},{1,97},{33,1},{65,33},{97,65},{2,98}... | collective-permute-start | bytes 540680 | tf_op jit(solution)/shard_map/ppermute | solution.py:38
  175.9 0.7 copy-start.6
  176.5 0.7 copy-start.7
  182.5 2.3 %collective-permute-start.33 = (bf16[16,32,576]{2,1,0:T(8,128)(2,1)}, bf16[16,32,576]{2,1,0:T(8,128)(2,1)S(1)}, u32[]{:S(2)}, u32[]{:S(2)}) collective-permute-start(bf16[16,32,576]{2,1,0:T(8,128)(2,1)} %get-tuple-element.32), channel_id=1, source_target_pairs={{0,1},{1,0},{2,3},{3,2},{4,5},{5,4},{6,7},{7,6},{8,9},{9,8},{10,11... | collective-permute-start | bytes 1769480 | tf_op jit(solution)/shard_map/ppermute | solution.py:33
  185.9 17.5 %copy-start.5 = (bf16[1024,64]{1,0:T(8,128)(2,1)S(1)}, bf16[1024,64]{1,0:T(8,128)(2,1)}, u32[]{:S(2)}) copy-start(bf16[1024,64]{1,0:T(8,128)(2,1)} %get-tuple-element.24) | copy-start | bytes 393220
  185.9 18.4 %copy-start.9 = (bf16[128,64]{1,0:T(8,128)(2,1)S(1)}, bf16[128,64]{1,0:T(8,128)(2,1)}, u32[]{:S(2)}) copy-start(bf16[128,64]{1,0:T(8,128)(2,1)} %get-tuple-element.30) | copy-start | bytes 49156
  185.9 19.0 %copy-start.12 = (f32[2,8,128]{2,1,0:T(8,128)S(1)}, f32[2,8,128]{2,1,0:T(8,128)}, u32[]{:S(2)}) copy-start(f32[2,8,128]{2,1,0:T(8,128)} %get-tuple-element.33) | copy-start | bytes 24580
  185.9 9.8 %collective-permute-start.34 = (bf16[8,32,576]{2,1,0:T(8,128)(2,1)S(1)}, bf16[8,32,576]{2,1,0:T(8,128)(2,1)S(1)}, u32[]{:S(2)}, u32[]{:S(2)}) collective-permute-start(bf16[8,32,576]{2,1,0:T(8,128)(2,1)S(1)} %add_convert_fusion.3), channel_id=1, source_target_pairs={{0,2},{2,0},{1,3},{3,1},{4,6},{6,4},{5,7},{7,5},{8,10},{10,8},{9,1... | collective-permute-start | bytes 884744 | tf_op jit(solution)/shard_map/ppermute | solution.py:33
  196.9 14.3 %collective-permute-start.36 = (bf16[32,576]{1,0:T(8,128)(2,1)S(1)}, bf16[32,576]{1,0:T(8,128)(2,1)S(1)}, u32[]{:S(2)}, u32[]{:S(2)}) collective-permute-start(bf16[32,576]{1,0:T(8,128)(2,1)S(1)} %get-tuple-element.57), channel_id=1, source_target_pairs={{0,8},{4,12},{8,16},{12,20},{16,24},{20,28},{24,0},{28,4},{1,9},{5... | collective-permute-start | bytes 110600 | tf_op jit(solution)/shard_map/ppermute | solution.py:38
  201.7 9.9 %collective-permute-start.35 = (bf16[32,576]{1,0:T(8,128)(2,1)S(1)}, bf16[32,576]{1,0:T(8,128)(2,1)S(1)}, u32[]{:S(2)}, u32[]{:S(2)}) collective-permute-start(bf16[32,576]{1,0:T(8,128)(2,1)S(1)} %get-tuple-element.58), channel_id=1, source_target_pairs={{0,4},{4,8},{8,12},{12,16},{16,20},{20,24},{24,28},{28,0},{1,5},{5... | collective-permute-start | bytes 110600 | tf_op jit(solution)/shard_map/ppermute | solution.py:38
  205.6 10.8 %collective-permute-start.37 = (bf16[32,576]{1,0:T(8,128)(2,1)S(1)}, bf16[32,576]{1,0:T(8,128)(2,1)S(1)}, u32[]{:S(2)}, u32[]{:S(2)}) collective-permute-start(bf16[32,576]{1,0:T(8,128)(2,1)S(1)} %get-tuple-element.52), channel_id=1, source_target_pairs={{0,12},{4,16},{8,20},{12,24},{16,28},{20,0},{24,4},{28,8},{1,13},{... | collective-permute-start | bytes 110600 | tf_op jit(solution)/shard_map/ppermute | solution.py:38
  205.8 10.6 %collective-permute-start.41 = (bf16[32,576]{1,0:T(8,128)(2,1)S(1)}, bf16[32,576]{1,0:T(8,128)(2,1)S(1)}, u32[]{:S(2)}, u32[]{:S(2)}) collective-permute-start(bf16[32,576]{1,0:T(8,128)(2,1)S(1)} %get-tuple-element.53), channel_id=1, source_target_pairs={{0,28},{4,0},{8,4},{12,8},{16,12},{20,16},{24,20},{28,24},{1,29},{... | collective-permute-start | bytes 110600 | tf_op jit(solution)/shard_map/ppermute | solution.py:38
  208.4 8.0 %collective-permute-start.40 = (bf16[32,576]{1,0:T(8,128)(2,1)S(1)}, bf16[32,576]{1,0:T(8,128)(2,1)S(1)}, u32[]{:S(2)}, u32[]{:S(2)}) collective-permute-start(bf16[32,576]{1,0:T(8,128)(2,1)S(1)} %get-tuple-element.54), channel_id=1, source_target_pairs={{0,24},{4,28},{8,0},{12,4},{16,8},{20,12},{24,16},{28,20},{1,25},{... | collective-permute-start | bytes 110600 | tf_op jit(solution)/shard_map/ppermute | solution.py:38
  211.2 5.8 %collective-permute-start.39 = (bf16[32,576]{1,0:T(8,128)(2,1)S(1)}, bf16[32,576]{1,0:T(8,128)(2,1)S(1)}, u32[]{:S(2)}, u32[]{:S(2)}) collective-permute-start(bf16[32,576]{1,0:T(8,128)(2,1)S(1)} %get-tuple-element.55), channel_id=1, source_target_pairs={{0,20},{4,24},{8,28},{12,0},{16,4},{20,8},{24,12},{28,16},{1,21},{... | collective-permute-start | bytes 110600 | tf_op jit(solution)/shard_map/ppermute | solution.py:38
  211.5 8.0 %collective-permute-start.38 = (bf16[32,576]{1,0:T(8,128)(2,1)S(1)}, bf16[32,576]{1,0:T(8,128)(2,1)S(1)}, u32[]{:S(2)}, u32[]{:S(2)}) collective-permute-start(bf16[32,576]{1,0:T(8,128)(2,1)S(1)} %get-tuple-element.56), channel_id=1, source_target_pairs={{0,16},{4,20},{8,24},{12,28},{16,0},{20,4},{24,8},{28,12},{1,17},{... | collective-permute-start | bytes 110600 | tf_op jit(solution)/shard_map/ppermute | solution.py:38

commit v4 on v3

--- a/solution.py
+++ b/solution.py
@@ -372,7 +372,7 @@
 
         def slot_step(slot, carry):
             for core, ref in enumerate((near_ref, far_ref)):
-                owner = owner_at(me, core, lax.rem(slot, n_z), slot // n_z)
+                owner = owner_at(me, core, lax.rem(slot + n_z // 4, n_z), slot // n_z)
                 ref[slot] = placed[owner, :, :cols].astype(bf16)
             return carry
 
@@ -470,20 +470,29 @@
         me, dp_pieces, dp_items, layer_input, latent, rope, heads
     )
     there_part = swapped(far_part, "core")
-    mine, other = (
-        near_part[k : k + n_z].astype(wide) + there_part[k : k + n_z].astype(wide)
-        for k in (0, n_z)
-    )
-    parts = mine + swapped(other.astype(bf16), "ylo").astype(wide)
-    grad_down = parts[0]
-    for k in range(1, n_z):
-        grad_down = grad_down + shifted(parts[k].astype(bf16), "z", k).astype(wide)
+    grad_down, far_parts = 0.0, None
+    for start, stop in ((0, n_z // 2 + 1), (n_z // 2 + 1, n_z)):
+        mine, other = (
+            near_part[k + start : k + stop].astype(wide)
+            + there_part[k + start : k + stop].astype(wide)
+            for k in (0, n_z)
+        )
+        other = swapped(other.astype(bf16), "ylo")
+        if far_parts is not None:
+            other, _ = lax.optimization_barrier((other, far_parts))
+        parts = mine + other.astype(wide)
+        far_parts = parts.astype(bf16)
+        for k in range(start, stop):
+            z = (k + n_z // 4) % n_z
+            part = shifted(far_parts[k - start], "z", z) if z else parts[k - start]
+            grad_down = grad_down + part.astype(wide)
+    grad_down = grad_down[: layer_input.shape[2] // N_CTX]
     return (
         d_q.reshape(q_latent.shape),
         d_qr.reshape(q_rope.shape),
         d_lat[None],
         d_rope[None],
-        grad_down[: layer_input.shape[2] // N_CTX],
+        grad_down,
         grad_uv.reshape(-1, w_uv.shape[1]),
     )
 

time: 221 us -> 224 us (1.014)
  starting transfers between devices: 88 us -> 90.3 us
    ppermute x17 -> x18, waiting for transfers between devices: 46.8 us -> 42.2 us  [swapped(): return lax.ppermute(x, axis, [(0, 1), (1, 0)])]
    ppermute x25, waiting for transfers between devices: 31.2 us -> 34.8 us  [shifted(): return lax.ppermute(x, axis, [(i, (i + by) % n) for i in range(n)])]
    ppermute x17 -> x18, starting transfers between devices: 38.7 us -> 40.4 us  [swapped(): return lax.ppermute(x, axis, [(0, 1), (1, 0)])]
    unnamed x44 -> x42, local copies, waits for them, and re-layouts: 7.22 us -> 8.68 us
  transfers between devices with their start and end apart: 42 -> 43, of which waited for: 21 -> 20; matrix products, arithmetic and copies ran while one was open for 4% -> 5% of each run, Pallas kernels for 5% -> 5%
where the time goes in v4:
time: 224 us; the launch traced here: 223 us
  starting transfers between devices  90.3 us (40%)
  waiting for transfers between devices  77 us (34%)
  Pallas kernels  38.3 us (17%)
  local copies, waits for them, and re-layouts  9.39 us (4%)
  other arithmetic  6.83 us (3%)
    ppermute x25, starting transfers between devices, shifted(): return lax.ppermute(x, axis, [(i, (i + by) % n) for i in range(n)])  49.9 us
    ppermute x18, waiting for transfers between devices, swapped(): return lax.ppermute(x, axis, [(0, 1), (1, 0)])  42.2 us
    ppermute x18, starting transfers between devices, swapped(): return lax.ppermute(x, axis, [(0, 1), (1, 0)])  40.4 us
    pallas_call x5, Pallas kernels, call(): pl.pallas_call(kernel, out_shape=tuple((jax.ShapeDtypeStruct(*o) for o in...  38.3 us
    ppermute x25, waiting for transfers between devices, shifted(): return lax.ppermute(x, axis, [(i, (i + by) % n) for i in range(n)])  34.8 us
    unnamed x42, local copies, waits for them, and re-layouts  8.68 us
  transfers between devices with their start and end apart: 43, of which 20 were waited for; matrix products, arithmetic and copies ran while one was open for 5% of the time, Pallas kernels for 5%

profile of v4, /device:TPU:16, one launch (start us, length us, event | category | flops | bytes accessed | tf_op | source)
XLA Modules:
  0.0 222.8 jit_solution(8519698183119068037)
XLA Ops:
  0.6 0.8 copy.15
  1.5 0.9 copy-done
  2.4 1.9 collective-permute-start.2
  4.4 4.0 %collective-permute-start.1 = (bf16[64,1152]{1,0:T(8,128)(2,1)S(1)}, bf16[64,1152]{1,0:T(8,128)(2,1)S(1)}, u32[]{:S(2)}, u32[]{:S(2)}) collective-permute-start(bf16[64,1152]{1,0:T(8,128)(2,1)S(1)} %shard_map.136), channel_id=1, source_target_pairs={{0,28},{4,0},{8,4},{12,8},{16,12},{20,16},{24,20},{28,24},{1,29},{... | collective-permute-start | bytes 442376 | tf_op jit(solution)/shard_map/ppermute | solution.py:38
  8.4 1.3 collective-permute-start
  9.7 2.5 %collective-permute-done.2 = bf16[64,1152]{1,0:T(8,128)(2,1)S(1)} collective-permute-done((bf16[64,1152]{1,0:T(8,128)(2,1)S(1)}, bf16[64,1152]{1,0:T(8,128)(2,1)S(1)}, u32[]{:S(2)}, u32[]{:S(2)}) %collective-permute-start.2) | collective-permute-done | bytes 147488 | tf_op jit(solution)/shard_map/ppermute | solution.py:38
  12.2 1.4 collective-permute-start.3
  13.6 3.2 %collective-permute-start.4 = (bf16[64,1152]{1,0:T(8,128)(2,1)S(1)}, bf16[64,1152]{1,0:T(8,128)(2,1)S(1)}, u32[]{:S(2)}, u32[]{:S(2)}) collective-permute-start(bf16[64,1152]{1,0:T(8,128)(2,1)S(1)} %collective-permute-done.1), channel_id=1, source_target_pairs={{0,28},{4,0},{8,4},{12,8},{16,12},{20,16},{24,20},{28,24},{1,29},{... | collective-permute-start | bytes 442376 | tf_op jit(solution)/shard_map/ppermute | solution.py:38
  16.9 3.0 %collective-permute-done.5 = bf16[64,1152]{1,0:T(8,128)(2,1)S(1)} collective-permute-done((bf16[64,1152]{1,0:T(8,128)(2,1)S(1)}, bf16[64,1152]{1,0:T(8,128)(2,1)S(1)}, u32[]{:S(2)}, u32[]{:S(2)}) %collective-permute-start.5) | collective-permute-done | bytes 147488 | tf_op jit(solution)/shard_map/ppermute | solution.py:38
  19.9 3.2 %collective-permute-start.7 = (bf16[64,1152]{1,0:T(8,128)(2,1)S(1)}, bf16[64,1152]{1,0:T(8,128)(2,1)S(1)}, u32[]{:S(2)}, u32[]{:S(2)}) collective-permute-start(bf16[64,1152]{1,0:T(8,128)(2,1)S(1)} %collective-permute-done.4), channel_id=1, source_target_pairs={{0,28},{4,0},{8,4},{12,8},{16,12},{20,16},{24,20},{28,24},{1,29},{... | collective-permute-start | bytes 442376 | tf_op jit(solution)/shard_map/ppermute | solution.py:38
  23.2 0.8 collective-permute-start.6
  24.0 2.2 %collective-permute-done.8 = bf16[64,1152]{1,0:T(8,128)(2,1)S(1)} collective-permute-done((bf16[64,1152]{1,0:T(8,128)(2,1)S(1)}, bf16[64,1152]{1,0:T(8,128)(2,1)S(1)}, u32[]{:S(2)}, u32[]{:S(2)}) %collective-permute-start.8) | collective-permute-done | bytes 147488 | tf_op jit(solution)/shard_map/ppermute | solution.py:38
  26.3 0.8 collective-permute-start.9
  27.2 1.4 collective-permute-start.10
  28.7 4.8 %collective-permute-done.10 = bf16[64,1152]{1,0:T(8,128)(2,1)S(1)} collective-permute-done((bf16[64,1152]{1,0:T(8,128)(2,1)S(1)}, bf16[64,1152]{1,0:T(8,128)(2,1)S(1)}, u32[]{:S(2)}, u32[]{:S(2)}) %collective-permute-start.10) | collective-permute-done | bytes 147488 | tf_op jit(solution)/shard_map/ppermute | solution.py:38
  33.5 1.3 collective-permute-start.11
  35.0 2.4 %collective-permute-done.9 = bf16[2,64,1152]{2,1,0:T(8,128)(2,1)S(1)} collective-permute-done((bf16[2,64,1152]{2,1,0:T(8,128)(2,1)S(1)}, bf16[2,64,1152]{2,1,0:T(8,128)(2,1)S(1)}, u32[]{:S(2)}, u32[]{:S(2)}) %collective-permute-start.9) | collective-permute-done | bytes 294944 | tf_op jit(solution)/shard_map/ppermute | solution.py:33
  37.5 1.5 collective-permute-done.11
  39.9 5.0 %shard_map.138.refs_7_ = bf16[32,64,256]{2,1,0:T(8,128)(2,1)} custom-call(s32[6]{0:T(128)} %stack.65.me_ref, bf16[1024,512]{1,0:T(8,128)(2,1)} %bitcast.96, bf16[128,1024]{1,0:T(8,128)(2,1)} %bitcast.98), custom_call_target="tpu_custom_call" | custom-call | flops 1000 | bytes 4194304 | tf_op jit(solution)/shard_map/pallas_call | solution.py:77
  44.8 0.9 copy.16
  45.7 5.2 %shard_map.137 = (bf16[1024,640]{1,0:T(8,128)(2,1)}, bf16[1024,512]{1,0:T(8,128)(2,1)}, f32[2,1,512]{2,1,0:T(1,128)}) custom-call(bf16[1024,512]{1,0:T(8,128)(2,1)} %bitcast.101, bf16[1024,64]{1,0:T(8,128)(2,1)} %bitcast.100, bf16[1024,512]{1,0:T(8,128)(2,1)} %bitcast.97, bf16[128,1024]{1,0:T(8,128)(2,1)} %bitcast.99, bf16[512,1024]{1,0:T(8,128)(2,1)} %w_ref.1), custom_call_target="tpu_custom_call" | custom-call | flops 1000 | bytes 4194304 | tf_op jit(solution)/shard_map/pallas_call | solution.py:77
  50.9 0.9 copy-done.12
  51.8 22.7 %shard_map.139 = (bf16[1024,512]{1,0:T(8,128)(2,1)}, bf16[1024,64]{1,0:T(8,128)(2,1)}, bf16[16,64,1408]{2,1,0:T(8,128)(2,1)}, bf16[6,64,1408]{2,1,0:T(8,128)(2,1)}, bf16[10,64,1408]{2,1,0:T(8,128)(2,1)}) custom-call(s32[6]{0:T(128)} %stack.65.me_ref, s32[64]{0:T(128)} %blocks_ref.1, bf16[10,64,1152]{2,1,0:T(8,128)(2,1)} %copy-done.11, ...), custom_call_target="tpu_custom_call" | custom-call | flops 13421772800 | bytes 4194304 | tf_op jit(solution)/shard_map/pallas_call | solution.py:77
  74.6 13.6 %collective-permute-start.15 = (bf16[6,64,1408]{2,1,0:T(8,128)(2,1)}, bf16[6,64,1408]{2,1,0:T(8,128)(2,1)S(1)}, u32[]{:S(2)}, u32[]{:S(2)}) collective-permute-start(bf16[6,64,1408]{2,1,0:T(8,128)(2,1)} %get-tuple-element.28), channel_id=1, source_target_pairs={{0,1},{1,0},{2,3},{3,2},{4,5},{5,4},{6,7},{7,6},{8,9},{9,8},{10,11... | collective-permute-start | bytes 3244040 | tf_op jit(solution)/shard_map/ppermute | solution.py:33
  88.3 2.4 %collective-permute-done.15 = bf16[6,64,1408]{2,1,0:T(8,128)(2,1)S(1)} collective-permute-done((bf16[6,64,1408]{2,1,0:T(8,128)(2,1)}, bf16[6,64,1408]{2,1,0:T(8,128)(2,1)S(1)}, u32[]{:S(2)}, u32[]{:S(2)}) %collective-permute-start.15) | collective-permute-done | bytes 1081376 | tf_op jit(solution)/shard_map/ppermute | solution.py:33
  90.7 1.0 add_convert_fusion.7
  91.7 14.0 %collective-permute-start.20 = (bf16[1,64,1408]{2,1,0:T(8,128)(2,1)S(1)}, bf16[1,64,1408]{2,1,0:T(8,128)(2,1)S(1)}, u32[]{:S(2)}, u32[]{:S(2)}) collective-permute-start(bf16[1,64,1408]{2,1,0:T(8,128)(2,1)S(1)} %add_convert_fusion.7), channel_id=1, source_target_pairs={{0,2},{2,0},{1,3},{3,1},{4,6},{6,4},{5,7},{7,5},{8,10},{10,8},{9,1... | collective-permute-start | bytes 540680 | tf_op jit(solution)/shard_map/ppermute | solution.py:33
  105.7 1.1 add_convert_fusion.2
  106.9 4.2 %collective-permute-done.20 = bf16[1,64,1408]{2,1,0:T(8,128)(2,1)S(1)} collective-permute-done((bf16[1,64,1408]{2,1,0:T(8,128)(2,1)S(1)}, bf16[1,64,1408]{2,1,0:T(8,128)(2,1)S(1)}, u32[]{:S(2)}, u32[]{:S(2)}) %collective-permute-start.20) | collective-permute-done | bytes 180256 | tf_op jit(solution)/shard_map/ppermute | solution.py:33
  111.1 1.1 add_convert_fusion.6
  112.3 6.0 %collective-permute-done.19 = bf16[2,64,1408]{2,1,0:T(8,128)(2,1)S(1)} collective-permute-done((bf16[2,64,1408]{2,1,0:T(8,128)(2,1)S(1)}, bf16[2,64,1408]{2,1,0:T(8,128)(2,1)S(1)}, u32[]{:S(2)}, u32[]{:S(2)}) %collective-permute-start.19) | collective-permute-done | bytes 360480 | tf_op jit(solution)/shard_map/ppermute | solution.py:33
  118.6 1.8 collective-permute-start.16
  120.8 2.0 collective-permute-start.22
  122.8 9.7 %collective-permute-done.18 = bf16[2,64,1408]{2,1,0:T(8,128)(2,1)S(1)} collective-permute-done((bf16[2,64,1408]{2,1,0:T(8,128)(2,1)S(1)}, bf16[2,64,1408]{2,1,0:T(8,128)(2,1)S(1)}, u32[]{:S(2)}, u32[]{:S(2)}) %collective-permute-start.18) | collective-permute-done | bytes 360480 | tf_op jit(solution)/shard_map/ppermute | solution.py:33
  132.6 1.5 collective-permute-start.17
  134.3 1.7 collective-permute-start.23
  136.0 3.1 %collective-permute-start.26 = (bf16[64,1408]{1,0:T(8,128)(2,1)S(1)}, bf16[64,1408]{1,0:T(8,128)(2,1)S(1)}, u32[]{:S(2)}, u32[]{:S(2)}) collective-permute-start(bf16[64,1408]{1,0:T(8,128)(2,1)S(1)} %get-tuple-element.53), channel_id=1, source_target_pairs={{0,28},{4,0},{8,4},{12,8},{16,12},{20,16},{24,20},{28,24},{1,29},{... | collective-permute-start | bytes 540680 | tf_op jit(solution)/shard_map/ppermute | solution.py:38
  139.1 2.6 %collective-permute-done.17 = bf16[2,64,1408]{2,1,0:T(8,128)(2,1)S(1)} collective-permute-done((bf16[2,64,1408]{2,1,0:T(8,128)(2,1)S(1)}, bf16[2,64,1408]{2,1,0:T(8,128)(2,1)S(1)}, u32[]{:S(2)}, u32[]{:S(2)}) %collective-permute-start.17) | collective-permute-done | bytes 360480 | tf_op jit(solution)/shard_map/ppermute | solution.py:33
  142.6 1.4 collective-permute-start.24
  144.0 3.0 %collective-permute-start.27 = (bf16[64,1408]{1,0:T(8,128)(2,1)S(1)}, bf16[64,1408]{1,0:T(8,128)(2,1)S(1)}, u32[]{:S(2)}, u32[]{:S(2)}) collective-permute-start(bf16[64,1408]{1,0:T(8,128)(2,1)S(1)} %get-tuple-element.51), channel_id=1, source_target_pairs={{0,28},{4,0},{8,4},{12,8},{16,12},{20,16},{24,20},{28,24},{1,29},{... | collective-permute-start | bytes 540680 | tf_op jit(solution)/shard_map/ppermute | solution.py:38
  147.0 3.4 %collective-permute-done.24 = bf16[64,1408]{1,0:T(8,128)(2,1)S(1)} collective-permute-done((bf16[64,1408]{1,0:T(8,128)(2,1)S(1)}, bf16[64,1408]{1,0:T(8,128)(2,1)S(1)}, u32[]{:S(2)}, u32[]{:S(2)}) %collective-permute-start.24) | collective-permute-done | bytes 180256 | tf_op jit(solution)/shard_map/ppermute | solution.py:38
  150.4 0.7 collective-permute-done.27
  152.0 6.4 %collective-permute-done.28 = bf16[64,1408]{1,0:T(8,128)(2,1)S(1)} collective-permute-done((bf16[64,1408]{1,0:T(8,128)(2,1)S(1)}, bf16[64,1408]{1,0:T(8,128)(2,1)S(1)}, u32[]{:S(2)}, u32[]{:S(2)}) %collective-permute-start.28) | collective-permute-done | bytes 180256 | tf_op jit(solution)/shard_map/ppermute | solution.py:33
  158.4 1.6 collective-permute-start.30
  160.0 1.7 collective-permute-start.29
  161.7 7.3 %collective-permute-done.30.refs_2_ = bf16[2,64,1408]{2,1,0:T(8,128)(2,1)S(1)} collective-permute-done((bf16[2,64,1408]{2,1,0:T(8,128)(2,1)S(1)}, bf16[2,64,1408]{2,1,0:T(8,128)(2,1)S(1)}, u32[]{:S(2)}, u32[]{:S(2)}) %collective-permute-start.30) | collective-permute-done | bytes 360480 | tf_op jit(solution)/shard_map/ppermute | solution.py:38
  169.4 3.0 %collective-permute-start.32 = (bf16[1,64,1408]{2,1,0:T(8,128)(2,1)S(1)}, bf16[1,64,1408]{2,1,0:T(8,128)(2,1)S(1)}, u32[]{:S(2)}, u32[]{:S(2)}) collective-permute-start(bf16[1,64,1408]{2,1,0:T(8,128)(2,1)S(1)} %slice.192), channel_id=1, source_target_pairs={{0,96},{32,0},{64,32},{96,64},{1,97},{33,1},{65,33},{97,65},{2,98}... | collective-permute-start | bytes 540680 | tf_op jit(solution)/shard_map/ppermute | solution.py:38
  172.5 3.4 %collective-permute-done.31.refs_3_ = bf16[1,64,1408]{2,1,0:T(8,128)(2,1)S(1)} collective-permute-done((bf16[1,64,1408]{2,1,0:T(8,128)(2,1)S(1)}, bf16[1,64,1408]{2,1,0:T(8,128)(2,1)S(1)}, u32[]{:S(2)}, u32[]{:S(2)}) %collective-permute-start.31) | collective-permute-done | bytes 180256 | tf_op jit(solution)/shard_map/ppermute | solution.py:38
  177.2 5.4 %shard_map.140 = (bf16[16,32,576]{2,1,0:T(8,128)(2,1)}, bf16[16,32,576]{2,1,0:T(8,128)(2,1)}, bf16[128,512]{1,0:T(8,128)(2,1)}, bf16[128,64]{1,0:T(8,128)(2,1)}, f32[2,8,128]{2,1,0:T(8,128)}) custom-call(s32[6]{0:T(128)} %stack.65.me_ref, bf16[2,64,1408]{2,1,0:T(8,128)(2,1)} %copy-done.2, bf16[2,64,1408]{2,1,0:T(8,128)(2,1)} %copy-done.4, ...), custom_call_target="tpu_custom_call" | custom-call | flops 1000 | bytes 4194304 | tf_op jit(solution)/shard_map/pallas_call | solution.py:77
  182.6 0.8 copy.17
  183.5 1.4 copy.18
  184.9 1.3 copy.21
  186.2 1.0 add_convert_fusion.4
  187.8 0.9 add_convert_fusion.8
  188.7 1.6 collective-permute-start.40
  190.3 4.9 %collective-permute-done.34 = bf16[5,32,576]{2,1,0:T(8,128)(2,1)S(1)} collective-permute-done((bf16[5,32,576]{2,1,0:T(8,128)(2,1)S(1)}, bf16[5,32,576]{2,1,0:T(8,128)(2,1)S(1)}, u32[]{:S(2)}, u32[]{:S(2)}) %collective-permute-start.34) | collective-permute-done | bytes 184352 | tf_op jit(solution)/shard_map/ppermute | solution.py:33
  195.4 2.0 collective-permute-done.40
  197.5 2.5 %collective-permute-start.41 = (bf16[32,576]{1,0:T(8,128)(2,1)S(1)}, bf16[32,576]{1,0:T(8,128)(2,1)S(1)}, u32[]{:S(2)}, u32[]{:S(2)}) collective-permute-start(bf16[32,576]{1,0:T(8,128)(2,1)S(1)} %get-tuple-element.59), channel_id=1, source_target_pairs={{0,28},{4,0},{8,4},{12,8},{16,12},{20,16},{24,20},{28,24},{1,29},{... | collective-permute-start | bytes 110600 | tf_op jit(solution)/shard_map/ppermute | solution.py:38
  200.0 0.9 collective-permute-start.42
  200.9 5.8 %collective-permute-start.36 = (bf16[32,576]{1,0:T(8,128)(2,1)S(1)}, bf16[32,576]{1,0:T(8,128)(2,1)S(1)}, u32[]{:S(2)}, u32[]{:S(2)}) collective-permute-start(bf16[32,576]{1,0:T(8,128)(2,1)S(1)} %get-tuple-element.57), channel_id=1, source_target_pairs={{0,12},{4,16},{8,20},{12,24},{16,28},{20,0},{24,4},{28,8},{1,13},{... | collective-permute-start | bytes 110600 | tf_op jit(solution)/shard_map/ppermute | solution.py:38
  206.7 2.6 %collective-permute-start.38 = (bf16[32,576]{1,0:T(8,128)(2,1)S(1)}, bf16[32,576]{1,0:T(8,128)(2,1)S(1)}, u32[]{:S(2)}, u32[]{:S(2)}) collective-permute-start(bf16[32,576]{1,0:T(8,128)(2,1)S(1)} %get-tuple-element.54), channel_id=1, source_target_pairs={{0,20},{4,24},{8,28},{12,0},{16,4},{20,8},{24,12},{28,16},{1,21},{... | collective-permute-start | bytes 110600 | tf_op jit(solution)/shard_map/ppermute | solution.py:38
  209.3 4.4 %collective-permute-start.39 = (bf16[32,576]{1,0:T(8,128)(2,1)S(1)}, bf16[32,576]{1,0:T(8,128)(2,1)S(1)}, u32[]{:S(2)}, u32[]{:S(2)}) collective-permute-start(bf16[32,576]{1,0:T(8,128)(2,1)S(1)} %get-tuple-element.55), channel_id=1, source_target_pairs={{0,24},{4,28},{8,0},{12,4},{16,8},{20,12},{24,16},{28,20},{1,25},{... | collective-permute-start | bytes 110600 | tf_op jit(solution)/shard_map/ppermute | solution.py:38
  213.8 1.6 collective-permute-start.37
  215.4 6.7 %collective-permute-done.37 = bf16[32,576]{1,0:T(8,128)(2,1)S(1)} collective-permute-done((bf16[32,576]{1,0:T(8,128)(2,1)S(1)}, bf16[32,576]{1,0:T(8,128)(2,1)S(1)}, u32[]{:S(2)}, u32[]{:S(2)}) %collective-permute-start.37) | collective-permute-done | bytes 36896 | tf_op jit(solution)/shard_map/ppermute | solution.py:38
  (99 shorter events, 7.6 us)
Async XLA Ops:
  1.5 0.9 copy-start
  2.4 9.7 %collective-permute-start.2 = (bf16[64,1152]{1,0:T(8,128)(2,1)S(1)}, bf16[64,1152]{1,0:T(8,128)(2,1)S(1)}, u32[]{:S(2)}, u32[]{:S(2)}) collective-permute-start(bf16[64,1152]{1,0:T(8,128)(2,1)S(1)} %shard_map.136), channel_id=1, source_target_pairs={{0,4},{4,8},{8,12},{12,16},{16,20},{20,24},{24,28},{28,0},{1,5},{5... | collective-permute-start | bytes 442376 | tf_op jit(solution)/shard_map/ppermute | solution.py:38
  4.4 7.8 %collective-permute-start.1 = (bf16[64,1152]{1,0:T(8,128)(2,1)S(1)}, bf16[64,1152]{1,0:T(8,128)(2,1)S(1)}, u32[]{:S(2)}, u32[]{:S(2)}) collective-permute-start(bf16[64,1152]{1,0:T(8,128)(2,1)S(1)} %shard_map.136), channel_id=1, source_target_pairs={{0,28},{4,0},{8,4},{12,8},{16,12},{20,16},{24,20},{28,24},{1,29},{... | collective-permute-start | bytes 442376 | tf_op jit(solution)/shard_map/ppermute | solution.py:38
  8.4 8.4 %collective-permute-start = (bf16[1,64,1152]{2,1,0:T(8,128)(2,1)S(1)}, bf16[1,64,1152]{2,1,0:T(8,128)(2,1)S(1)}, u32[]{:S(2)}, u32[]{:S(2)}) collective-permute-start(bf16[1,64,1152]{2,1,0:T(8,128)(2,1)S(1)} %bitcast.93), channel_id=1, source_target_pairs={{0,2},{2,0},{1,3},{3,1},{4,6},{6,4},{5,7},{7,5},{8,10},{10,8},{9,1... | collective-permute-start | bytes 442376 | tf_op jit(solution)/shard_map/ppermute | solution.py:33
  12.2 16.4 %collective-permute-start.3 = (bf16[2,64,1152]{2,1,0:T(8,128)(2,1)S(1)}, bf16[2,64,1152]{2,1,0:T(8,128)(2,1)S(1)}, u32[]{:S(2)}, u32[]{:S(2)}) collective-permute-start(bf16[2,64,1152]{2,1,0:T(8,128)(2,1)S(1)} %pad_maximum_fusion.1), channel_id=1, source_target_pairs={{0,2},{2,0},{1,3},{3,1},{4,6},{6,4},{5,7},{7,5},{8,10},{10,8},{9,1... | collective-permute-start | bytes 884744 | tf_op jit(solution)/shard_map/ppermute | solution.py:33
  13.6 6.4 %collective-permute-start.5 = (bf16[64,1152]{1,0:T(8,128)(2,1)S(1)}, bf16[64,1152]{1,0:T(8,128)(2,1)S(1)}, u32[]{:S(2)}, u32[]{:S(2)}) collective-permute-start(bf16[64,1152]{1,0:T(8,128)(2,1)S(1)} %collective-permute-done.2), channel_id=1, source_target_pairs={{0,4},{4,8},{8,12},{12,16},{16,20},{20,24},{24,28},{28,0},{1,5},{5... | collective-permute-start | bytes 442376 | tf_op jit(solution)/shard_map/ppermute | solution.py:38
  13.6 6.4 %collective-permute-start.4 = (bf16[64,1152]{1,0:T(8,128)(2,1)S(1)}, bf16[64,1152]{1,0:T(8,128)(2,1)S(1)}, u32[]{:S(2)}, u32[]{:S(2)}) collective-permute-start(bf16[64,1152]{1,0:T(8,128)(2,1)S(1)} %collective-permute-done.1), channel_id=1, source_target_pairs={{0,28},{4,0},{8,4},{12,8},{16,12},{20,16},{24,20},{28,24},{1,29},{... | collective-permute-start | bytes 442376 | tf_op jit(solution)/shard_map/ppermute | solution.py:38
  19.9 6.4 %collective-permute-start.8 = (bf16[64,1152]{1,0:T(8,128)(2,1)S(1)}, bf16[64,1152]{1,0:T(8,128)(2,1)S(1)}, u32[]{:S(2)}, u32[]{:S(2)}) collective-permute-start(bf16[64,1152]{1,0:T(8,128)(2,1)S(1)} %collective-permute-done.5), channel_id=1, source_target_pairs={{0,4},{4,8},{8,12},{12,16},{16,20},{20,24},{24,28},{28,0},{1,5},{5... | collective-permute-start | bytes 442376 | tf_op jit(solution)/shard_map/ppermute | solution.py:38
  19.9 6.4 %collective-permute-start.7 = (bf16[64,1152]{1,0:T(8,128)(2,1)S(1)}, bf16[64,1152]{1,0:T(8,128)(2,1)S(1)}, u32[]{:S(2)}, u32[]{:S(2)}) collective-permute-start(bf16[64,1152]{1,0:T(8,128)(2,1)S(1)} %collective-permute-done.4), channel_id=1, source_target_pairs={{0,28},{4,0},{8,4},{12,8},{16,12},{20,16},{24,20},{28,24},{1,29},{... | collective-permute-start | bytes 442376 | tf_op jit(solution)/shard_map/ppermute | solution.py:38
  23.2 11.6 %collective-permute-start.6 = (bf16[2,64,1152]{2,1,0:T(8,128)(2,1)S(1)}, bf16[2,64,1152]{2,1,0:T(8,128)(2,1)S(1)}, u32[]{:S(2)}, u32[]{:S(2)}) collective-permute-start(bf16[2,64,1152]{2,1,0:T(8,128)(2,1)S(1)} %pad_maximum_fusion.2), channel_id=1, source_target_pairs={{0,2},{2,0},{1,3},{3,1},{4,6},{6,4},{5,7},{7,5},{8,10},{10,8},{9,1... | collective-permute-start | bytes 884744 | tf_op jit(solution)/shard_map/ppermute | solution.py:33
  26.3 11.1 %collective-permute-start.9 = (bf16[2,64,1152]{2,1,0:T(8,128)(2,1)S(1)}, bf16[2,64,1152]{2,1,0:T(8,128)(2,1)S(1)}, u32[]{:S(2)}, u32[]{:S(2)}) collective-permute-start(bf16[2,64,1152]{2,1,0:T(8,128)(2,1)S(1)} %pad_maximum_fusion.3), channel_id=1, source_target_pairs={{0,2},{2,0},{1,3},{3,1},{4,6},{6,4},{5,7},{7,5},{8,10},{10,8},{9,1... | collective-permute-start | bytes 884744 | tf_op jit(solution)/shard_map/ppermute | solution.py:33
  27.2 6.4 %collective-permute-start.10 = (bf16[64,1152]{1,0:T(8,128)(2,1)S(1)}, bf16[64,1152]{1,0:T(8,128)(2,1)S(1)}, u32[]{:S(2)}, u32[]{:S(2)}) collective-permute-start(bf16[64,1152]{1,0:T(8,128)(2,1)S(1)} %collective-permute-done.8), channel_id=1, source_target_pairs={{0,4},{4,8},{8,12},{12,16},{16,20},{20,24},{24,28},{28,0},{1,5},{5... | collective-permute-start | bytes 442376 | tf_op jit(solution)/shard_map/ppermute | solution.py:38
  33.5 5.4 %collective-permute-start.11 = (bf16[1,64,1152]{2,1,0:T(8,128)(2,1)S(1)}, bf16[1,64,1152]{2,1,0:T(8,128)(2,1)S(1)}, u32[]{:S(2)}, u32[]{:S(2)}) collective-permute-start(bf16[1,64,1152]{2,1,0:T(8,128)(2,1)S(1)} %bitcast.111), channel_id=1, source_target_pairs={{0,2},{2,0},{1,3},{3,1},{4,6},{6,4},{5,7},{7,5},{8,10},{10,8},{9,1... | collective-permute-start | bytes 442376 | tf_op jit(solution)/shard_map/ppermute | solution.py:33
  34.8 10.0 %copy-start.11 = (bf16[10,64,1152]{2,1,0:T(8,128)(2,1)}, bf16[10,64,1152]{2,1,0:T(8,128)(2,1)S(1)}, u32[]{:S(2)}) copy-start(bf16[10,64,1152]{2,1,0:T(8,128)(2,1)S(1)} %constant_dynamic-update-slice_fusion.refs_0_) | copy-start | bytes 4423684
  34.8 16.1 %collective-permute-start.12 = (bf16[10,64,1152]{2,1,0:T(8,128)(2,1)S(1)}, bf16[10,64,1152]{2,1,0:T(8,128)(2,1)}, u32[]{:S(2)}, u32[]{:S(2)}) collective-permute-start(bf16[10,64,1152]{2,1,0:T(8,128)(2,1)S(1)} %constant_dynamic-update-slice_fusion.refs_0_), channel_id=1, source_target_pairs={{0,1},{1,0},{2,3},{3,2},{4,5},{5,4},{6,7},{7,6},{8,9},{9,8},{10,11... | collective-permute-start | bytes 4423688 | tf_op jit(solution)/shard_map/ppermute | solution.py:33
  37.4 7.4 %copy-start.9 = (bf16[1,128,8,64]{1,3,2,0:T(8,128)(2,1)S(1)}, bf16[1,128,8,64]{1,3,2,0:T(8,128)(2,1)}, u32[]{:S(2)}) copy-start(bf16[1,128,8,64]{1,3,2,0:T(8,128)(2,1)} %param.13) | copy-start | bytes 393220
  39.0 11.9 %copy-start.10 = (bf16[6,64,1152]{2,1,0:T(8,128)(2,1)}, bf16[6,64,1152]{2,1,0:T(8,128)(2,1)S(1)}, u32[]{:S(2)}) copy-start(bf16[6,64,1152]{2,1,0:T(8,128)(2,1)S(1)} %constant_dynamic-update-slice_fusion.8.refs_1_) | copy-start | bytes 2654212
  39.0 11.9 %collective-permute-start.13 = (bf16[6,64,1152]{2,1,0:T(8,128)(2,1)S(1)}, bf16[6,64,1152]{2,1,0:T(8,128)(2,1)S(1)}, u32[]{:S(2)}, u32[]{:S(2)}) collective-permute-start(bf16[6,64,1152]{2,1,0:T(8,128)(2,1)S(1)} %constant_dynamic-update-slice_fusion.8.refs_1_), channel_id=1, source_target_pairs={{0,1},{1,0},{2,3},{3,2},{4,5},{5,4},{6,7},{7,6},{8,9},{9,8},{10,11... | collective-permute-start | bytes 2654216 | tf_op jit(solution)/shard_map/ppermute | solution.py:33
  50.9 0.9 copy-start.12
  74.6 43.7 %copy-start.1 = (bf16[16,64,1408]{2,1,0:T(8,128)(2,1)S(1)}, bf16[16,64,1408]{2,1,0:T(8,128)(2,1)}, u32[]{:S(2)}) copy-start(bf16[16,64,1408]{2,1,0:T(8,128)(2,1)} %get-tuple-element.26) | copy-start | bytes 8650756
  74.6 16.1 %collective-permute-start.15 = (bf16[6,64,1408]{2,1,0:T(8,128)(2,1)}, bf16[6,64,1408]{2,1,0:T(8,128)(2,1)S(1)}, u32[]{:S(2)}, u32[]{:S(2)}) collective-permute-start(bf16[6,64,1408]{2,1,0:T(8,128)(2,1)} %get-tuple-element.28), channel_id=1, source_target_pairs={{0,1},{1,0},{2,3},{3,2},{4,5},{5,4},{6,7},{7,6},{8,9},{9,8},{10,11... | collective-permute-start | bytes 3244040 | tf_op jit(solution)/shard_map/ppermute | solution.py:33
  88.2 18.7 %collective-permute-start.14 = (bf16[10,64,1408]{2,1,0:T(8,128)(2,1)}, bf16[10,64,1408]{2,1,0:T(8,128)(2,1)S(1)}, u32[]{:S(2)}, u32[]{:S(2)}) collective-permute-start(bf16[10,64,1408]{2,1,0:T(8,128)(2,1)} %get-tuple-element.27), channel_id=1, source_target_pairs={{0,1},{1,0},{2,3},{3,2},{4,5},{5,4},{6,7},{7,6},{8,9},{9,8},{10,11... | collective-permute-start | bytes 5406728 | tf_op jit(solution)/shard_map/ppermute | solution.py:33
  91.7 19.4 %collective-permute-start.20 = (bf16[1,64,1408]{2,1,0:T(8,128)(2,1)S(1)}, bf16[1,64,1408]{2,1,0:T(8,128)(2,1)S(1)}, u32[]{:S(2)}, u32[]{:S(2)}) collective-permute-start(bf16[1,64,1408]{2,1,0:T(8,128)(2,1)S(1)} %add_convert_fusion.7), channel_id=1, source_target_pairs={{0,2},{2,0},{1,3},{3,1},{4,6},{6,4},{5,7},{7,5},{8,10},{10,8},{9,1... | collective-permute-start | bytes 540680 | tf_op jit(solution)/shard_map/ppermute | solution.py:33
  106.8 11.5 %collective-permute-start.19 = (bf16[2,64,1408]{2,1,0:T(8,128)(2,1)S(1)}, bf16[2,64,1408]{2,1,0:T(8,128)(2,1)S(1)}, u32[]{:S(2)}, u32[]{:S(2)}) collective-permute-start(bf16[2,64,1408]{2,1,0:T(8,128)(2,1)S(1)} %add_convert_fusion.2), channel_id=1, source_target_pairs={{0,2},{2,0},{1,3},{3,1},{4,6},{6,4},{5,7},{7,5},{8,10},{10,8},{9,1... | collective-permute-start | bytes 1081352 | tf_op jit(solution)/shard_map/ppermute | solution.py:33
  112.2 8.5 %collective-permute-start.21 = (bf16[64,1408]{1,0:T(8,128)(2,1)S(1)}, bf16[64,1408]{1,0:T(8,128)(2,1)S(1)}, u32[]{:S(2)}, u32[]{:S(2)}) collective-permute-start(bf16[64,1408]{1,0:T(8,128)(2,1)S(1)} %get-tuple-element.47), channel_id=1, source_target_pairs={{0,4},{4,8},{8,12},{12,16},{16,20},{20,24},{24,28},{28,0},{1,5},{5... | collective-permute-start | bytes 540680 | tf_op jit(solution)/shard_map/ppermute | solution.py:38
  118.5 15.7 %collective-permute-start.25 = (bf16[64,1408]{1,0:T(8,128)(2,1)S(1)}, bf16[64,1408]{1,0:T(8,128)(2,1)S(1)}, u32[]{:S(2)}, u32[]{:S(2)}) collective-permute-start(bf16[64,1408]{1,0:T(8,128)(2,1)S(1)} %fusion.13), channel_id=1, source_target_pairs={{0,28},{4,0},{8,4},{12,8},{16,12},{20,16},{24,20},{28,24},{1,29},{... | collective-permute-start | bytes 540680 | tf_op jit(solution)/shard_map/ppermute | solution.py:38
  118.6 28.4 %collective-permute-start.16 = (bf16[1,64,1408]{2,1,0:T(8,128)(2,1)S(1)}, bf16[1,64,1408]{2,1,0:T(8,128)(2,1)S(1)}, u32[]{:S(2)}, u32[]{:S(2)}) collective-permute-start(bf16[1,64,1408]{2,1,0:T(8,128)(2,1)S(1)} %get-tuple-element.46), channel_id=1, source_target_pairs={{0,2},{2,0},{1,3},{3,1},{4,6},{6,4},{5,7},{7,5},{8,10},{10,8},{9,1... | collective-permute-start | bytes 540680 | tf_op jit(solution)/shard_map/ppermute | solution.py:33
  120.4 12.0 %collective-permute-start.18 = (bf16[2,64,1408]{2,1,0:T(8,128)(2,1)S(1)}, bf16[2,64,1408]{2,1,0:T(8,128)(2,1)S(1)}, u32[]{:S(2)}, u32[]{:S(2)}) collective-permute-start(bf16[2,64,1408]{2,1,0:T(8,128)(2,1)S(1)} %get-tuple-element.49), channel_id=1, source_target_pairs={{0,2},{2,0},{1,3},{3,1},{4,6},{6,4},{5,7},{7,5},{8,10},{10,8},{9,1... | collective-permute-start | bytes 1081352 | tf_op jit(solution)/shard_map/ppermute | solution.py:33
  120.8 13.4 %collective-permute-start.22 = (bf16[64,1408]{1,0:T(8,128)(2,1)S(1)}, bf16[64,1408]{1,0:T(8,128)(2,1)S(1)}, u32[]{:S(2)}, u32[]{:S(2)}) collective-permute-start(bf16[64,1408]{1,0:T(8,128)(2,1)S(1)} %fusion.5), channel_id=1, source_target_pairs={{0,4},{4,8},{8,12},{12,16},{16,20},{20,24},{24,28},{28,0},{1,5},{5... | collective-permute-start | bytes 540680 | tf_op jit(solution)/shard_map/ppermute | solution.py:38
  132.6 9.1 %collective-permute-start.17 = (bf16[2,64,1408]{2,1,0:T(8,128)(2,1)S(1)}, bf16[2,64,1408]{2,1,0:T(8,128)(2,1)S(1)}, u32[]{:S(2)}, u32[]{:S(2)}) collective-permute-start(bf16[2,64,1408]{2,1,0:T(8,128)(2,1)S(1)} %get-tuple-element.45), channel_id=1, source_target_pairs={{0,2},{2,0},{1,3},{3,1},{4,6},{6,4},{5,7},{7,5},{8,10},{10,8},{9,1... | collective-permute-start | bytes 1081352 | tf_op jit(solution)/shard_map/ppermute | solution.py:33
  134.3 8.2 %collective-permute-start.23 = (bf16[64,1408]{1,0:T(8,128)(2,1)S(1)}, bf16[64,1408]{1,0:T(8,128)(2,1)S(1)}, u32[]{:S(2)}, u32[]{:S(2)}) collective-permute-start(bf16[64,1408]{1,0:T(8,128)(2,1)S(1)} %get-tuple-element.52), channel_id=1, source_target_pairs={{0,4},{4,8},{8,12},{12,16},{16,20},{20,24},{24,28},{28,0},{1,5},{5... | collective-permute-start | bytes 540680 | tf_op jit(solution)/shard_map/ppermute | solution.py:38
  136.0 6.5 %collective-permute-start.26 = (bf16[64,1408]{1,0:T(8,128)(2,1)S(1)}, bf16[64,1408]{1,0:T(8,128)(2,1)S(1)}, u32[]{:S(2)}, u32[]{:S(2)}) collective-permute-start(bf16[64,1408]{1,0:T(8,128)(2,1)S(1)} %get-tuple-element.53), channel_id=1, source_target_pairs={{0,28},{4,0},{8,4},{12,8},{16,12},{20,16},{24,20},{28,24},{1,29},{... | collective-permute-start | bytes 540680 | tf_op jit(solution)/shard_map/ppermute | solution.py:38
  142.6 7.8 %collective-permute-start.24 = (bf16[64,1408]{1,0:T(8,128)(2,1)S(1)}, bf16[64,1408]{1,0:T(8,128)(2,1)S(1)}, u32[]{:S(2)}, u32[]{:S(2)}) collective-permute-start(bf16[64,1408]{1,0:T(8,128)(2,1)S(1)} %get-tuple-element.50), channel_id=1, source_target_pairs={{0,4},{4,8},{8,12},{12,16},{16,20},{20,24},{24,28},{28,0},{1,5},{5... | collective-permute-start | bytes 540680 | tf_op jit(solution)/shard_map/ppermute | solution.py:38
  144.0 7.2 %collective-permute-start.27 = (bf16[64,1408]{1,0:T(8,128)(2,1)S(1)}, bf16[64,1408]{1,0:T(8,128)(2,1)S(1)}, u32[]{:S(2)}, u32[]{:S(2)}) collective-permute-start(bf16[64,1408]{1,0:T(8,128)(2,1)S(1)} %get-tuple-element.51), channel_id=1, source_target_pairs={{0,28},{4,0},{8,4},{12,8},{16,12},{20,16},{24,20},{28,24},{1,29},{... | collective-permute-start | bytes 540680 | tf_op jit(solution)/shard_map/ppermute | solution.py:38
  151.2 7.1 %collective-permute-start.28 = (bf16[64,1408]{1,0:T(8,128)(2,1)S(1)}, bf16[64,1408]{1,0:T(8,128)(2,1)S(1)}, u32[]{:S(2)}, u32[]{:S(2)}) collective-permute-start(bf16[64,1408]{1,0:T(8,128)(2,1)S(1)} %fusion.11), channel_id=1, source_target_pairs={{0,128},{128,0},{1,129},{129,1},{2,130},{130,2},{3,131},{131,3},{4... | collective-permute-start | bytes 540680 | tf_op jit(solution)/shard_map/ppermute | solution.py:33
  158.4 17.5 %copy-start.2 = (bf16[2,64,1408]{2,1,0:T(8,128)(2,1)}, bf16[2,64,1408]{2,1,0:T(8,128)(2,1)S(1)}, u32[]{:S(2)}) copy-start(bf16[2,64,1408]{2,1,0:T(8,128)(2,1)S(1)} %pad_maximum_fusion.refs_0_) | copy-start | bytes 1081348
  158.4 10.6 %collective-permute-start.30 = (bf16[2,64,1408]{2,1,0:T(8,128)(2,1)S(1)}, bf16[2,64,1408]{2,1,0:T(8,128)(2,1)S(1)}, u32[]{:S(2)}, u32[]{:S(2)}) collective-permute-start(bf16[2,64,1408]{2,1,0:T(8,128)(2,1)S(1)} %pad_maximum_fusion.refs_0_), channel_id=1, source_target_pairs={{0,32},{32,64},{64,96},{96,0},{1,33},{33,65},{65,97},{97,1},{2,34}... | collective-permute-start | bytes 1081352 | tf_op jit(solution)/shard_map/ppermute | solution.py:38
  160.0 9.5 %collective-permute-start.29 = (bf16[2,64,1408]{2,1,0:T(8,128)(2,1)S(1)}, bf16[2,64,1408]{2,1,0:T(8,128)(2,1)S(1)}, u32[]{:S(2)}, u32[]{:S(2)}) collective-permute-start(bf16[2,64,1408]{2,1,0:T(8,128)(2,1)S(1)} %pad_maximum_fusion.refs_0_), channel_id=1, source_target_pairs={{0,96},{32,0},{64,32},{96,64},{1,97},{33,1},{65,33},{97,65},{2,98}... | collective-permute-start | bytes 1081352 | tf_op jit(solution)/shard_map/ppermute | solution.py:38
  169.0 6.8 %copy-start.3 = (bf16[2,64,1408]{2,1,0:T(8,128)(2,1)}, bf16[2,64,1408]{2,1,0:T(8,128)(2,1)S(1)}, u32[]{:S(2)}) copy-start(bf16[2,64,1408]{2,1,0:T(8,128)(2,1)S(1)} %collective-permute-done.30.refs_2_) | copy-start | bytes 1081348
  169.1 6.8 %collective-permute-start.31 = (bf16[1,64,1408]{2,1,0:T(8,128)(2,1)S(1)}, bf16[1,64,1408]{2,1,0:T(8,128)(2,1)S(1)}, u32[]{:S(2)}, u32[]{:S(2)}) collective-permute-start(bf16[1,64,1408]{2,1,0:T(8,128)(2,1)S(1)} %slice.191), channel_id=1, source_target_pairs={{0,32},{32,64},{64,96},{96,0},{1,33},{33,65},{65,97},{97,1},{2,34}... | collective-permute-start | bytes 540680 | tf_op jit(solution)/shard_map/ppermute | solution.py:38
  169.4 6.4 %copy-start.4 = (bf16[2,64,1408]{2,1,0:T(8,128)(2,1)}, bf16[2,64,1408]{2,1,0:T(8,128)(2,1)S(1)}, u32[]{:S(2)}) copy-start(bf16[2,64,1408]{2,1,0:T(8,128)(2,1)S(1)} %collective-permute-done.29.refs_1_) | copy-start | bytes 1081348
  169.4 13.2 %copy-start.6 = (bf16[1024,64]{1,0:T(8,128)(2,1)S(1)}, bf16[1024,64]{1,0:T(8,128)(2,1)}, u32[]{:S(2)}) copy-start(bf16[1024,64]{1,0:T(8,128)(2,1)} %get-tuple-element.25) | copy-start | bytes 393220
  169.4 6.4 %collective-permute-start.32 = (bf16[1,64,1408]{2,1,0:T(8,128)(2,1)S(1)}, bf16[1,64,1408]{2,1,0:T(8,128)(2,1)S(1)}, u32[]{:S(2)}, u32[]{:S(2)}) collective-permute-start(bf16[1,64,1408]{2,1,0:T(8,128)(2,1)S(1)} %slice.192), channel_id=1, source_target_pairs={{0,96},{32,0},{64,32},{96,64},{1,97},{33,1},{65,33},{97,65},{2,98}... | collective-permute-start | bytes 540680 | tf_op jit(solution)/shard_map/ppermute | solution.py:38
  175.8 0.7 copy-start.7
  176.5 0.7 copy-start.8
  182.5 12.7 %copy-start.5 = (bf16[16,32,576]{2,1,0:T(8,128)(2,1)S(1)}, bf16[16,32,576]{2,1,0:T(8,128)(2,1)}, u32[]{:S(2)}) copy-start(bf16[16,32,576]{2,1,0:T(8,128)(2,1)} %get-tuple-element.32) | copy-start | bytes 1769476
  182.5 3.7 %collective-permute-start.33 = (bf16[16,32,576]{2,1,0:T(8,128)(2,1)}, bf16[16,32,576]{2,1,0:T(8,128)(2,1)S(1)}, u32[]{:S(2)}, u32[]{:S(2)}) collective-permute-start(bf16[16,32,576]{2,1,0:T(8,128)(2,1)} %get-tuple-element.33), channel_id=1, source_target_pairs={{0,1},{1,0},{2,3},{3,2},{4,5},{5,4},{6,7},{7,6},{8,9},{9,8},{10,11... | collective-permute-start | bytes 1769480 | tf_op jit(solution)/shard_map/ppermute | solution.py:33
  187.2 8.0 %collective-permute-start.34 = (bf16[5,32,576]{2,1,0:T(8,128)(2,1)S(1)}, bf16[5,32,576]{2,1,0:T(8,128)(2,1)S(1)}, u32[]{:S(2)}, u32[]{:S(2)}) collective-permute-start(bf16[5,32,576]{2,1,0:T(8,128)(2,1)S(1)} %add_convert_fusion.4), channel_id=1, source_target_pairs={{0,2},{2,0},{1,3},{3,1},{4,6},{6,4},{5,7},{7,5},{8,10},{10,8},{9,1... | collective-permute-start | bytes 552968 | tf_op jit(solution)/shard_map/ppermute | solution.py:33
  188.7 8.7 %collective-permute-start.40 = (bf16[3,32,576]{2,1,0:T(8,128)(2,1)S(1)}, bf16[3,32,576]{2,1,0:T(8,128)(2,1)S(1)}, u32[]{:S(2)}, u32[]{:S(2)}) collective-permute-start(bf16[3,32,576]{2,1,0:T(8,128)(2,1)S(1)} %add_convert_fusion.8), channel_id=1, source_target_pairs={{0,2},{2,0},{1,3},{3,1},{4,6},{6,4},{5,7},{7,5},{8,10},{10,8},{9,1... | collective-permute-start | bytes 331784 | tf_op jit(solution)/shard_map/ppermute | solution.py:33
  197.5 24.6 %collective-permute-start.41 = (bf16[32,576]{1,0:T(8,128)(2,1)S(1)}, bf16[32,576]{1,0:T(8,128)(2,1)S(1)}, u32[]{:S(2)}, u32[]{:S(2)}) collective-permute-start(bf16[32,576]{1,0:T(8,128)(2,1)S(1)} %get-tuple-element.59), channel_id=1, source_target_pairs={{0,28},{4,0},{8,4},{12,8},{16,12},{20,16},{24,20},{28,24},{1,29},{... | collective-permute-start | bytes 110600 | tf_op jit(solution)/shard_map/ppermute | solution.py:38
  200.0 22.2 %collective-permute-start.42 = (bf16[32,576]{1,0:T(8,128)(2,1)S(1)}, bf16[32,576]{1,0:T(8,128)(2,1)S(1)}, u32[]{:S(2)}, u32[]{:S(2)}) collective-permute-start(bf16[32,576]{1,0:T(8,128)(2,1)S(1)} %get-tuple-element.60), channel_id=1, source_target_pairs={{0,4},{4,8},{8,12},{12,16},{16,20},{20,24},{24,28},{28,0},{1,5},{5... | collective-permute-start | bytes 110600 | tf_op jit(solution)/shard_map/ppermute | solution.py:38
  200.9 8.4 %collective-permute-start.36 = (bf16[32,576]{1,0:T(8,128)(2,1)S(1)}, bf16[32,576]{1,0:T(8,128)(2,1)S(1)}, u32[]{:S(2)}, u32[]{:S(2)}) collective-permute-start(bf16[32,576]{1,0:T(8,128)(2,1)S(1)} %get-tuple-element.57), channel_id=1, source_target_pairs={{0,12},{4,16},{8,20},{12,24},{16,28},{20,0},{24,4},{28,8},{1,13},{... | collective-permute-start | bytes 110600 | tf_op jit(solution)/shard_map/ppermute | solution.py:38
  206.7 7.1 %collective-permute-start.35 = (bf16[32,576]{1,0:T(8,128)(2,1)S(1)}, bf16[32,576]{1,0:T(8,128)(2,1)S(1)}, u32[]{:S(2)}, u32[]{:S(2)}) collective-permute-start(bf16[32,576]{1,0:T(8,128)(2,1)S(1)} %get-tuple-element.58), channel_id=1, source_target_pairs={{0,8},{4,12},{8,16},{12,20},{16,24},{20,28},{24,0},{28,4},{1,9},{5... | collective-permute-start | bytes 110600 | tf_op jit(solution)/shard_map/ppermute | solution.py:38
  206.7 15.5 %collective-permute-start.38 = (bf16[32,576]{1,0:T(8,128)(2,1)S(1)}, bf16[32,576]{1,0:T(8,128)(2,1)S(1)}, u32[]{:S(2)}, u32[]{:S(2)}) collective-permute-start(bf16[32,576]{1,0:T(8,128)(2,1)S(1)} %get-tuple-element.54), channel_id=1, source_target_pairs={{0,20},{4,24},{8,28},{12,0},{16,4},{20,8},{24,12},{28,16},{1,21},{... | collective-permute-start | bytes 110600 | tf_op jit(solution)/shard_map/ppermute | solution.py:38
  209.3 12.8 %collective-permute-start.39 = (bf16[32,576]{1,0:T(8,128)(2,1)S(1)}, bf16[32,576]{1,0:T(8,128)(2,1)S(1)}, u32[]{:S(2)}, u32[]{:S(2)}) collective-permute-start(bf16[32,576]{1,0:T(8,128)(2,1)S(1)} %get-tuple-element.55), channel_id=1, source_target_pairs={{0,24},{4,28},{8,0},{12,4},{16,8},{20,12},{24,16},{28,20},{1,25},{... | collective-permute-start | bytes 110600 | tf_op jit(solution)/shard_map/ppermute | solution.py:38
  213.8 8.3 %collective-permute-start.37 = (bf16[32,576]{1,0:T(8,128)(2,1)S(1)}, bf16[32,576]{1,0:T(8,128)(2,1)S(1)}, u32[]{:S(2)}, u32[]{:S(2)}) collective-permute-start(bf16[32,576]{1,0:T(8,128)(2,1)S(1)} %get-tuple-element.56), channel_id=1, source_target_pairs={{0,16},{4,20},{8,24},{12,28},{16,0},{20,4},{24,8},{28,12},{1,17},{... | collective-permute-start | bytes 110600 | tf_op jit(solution)/shard_map/ppermute | solution.py:38
